TPU v7x, 32 devices: a whole 2x2x4 slice. The times are simulated.
32 devices in a mesh: shard: 2 (over x), replica: 16 (over z, y, core).
Axes of the slice: x: 2, y: 2, z: 4, core: 2. Of those that a mesh axis runs over, the one named last changes fastest.
Arguments:
- tokens: bfloat16 [8192, 1152], P(('shard', 'replica')), may hold values from -6 to 6
- out_grad: bfloat16 [8192, 1152], P(('shard', 'replica')), may hold values from -6 to 6
- picture_ids: int32 [8192], P(('shard', 'replica')), may hold values from 0 to 3, as said below
- live_slots: int32 [8192], P(('shard', 'replica')), may hold values from 0 to 1, as said below
- ln1_gain: bfloat16 [1152], P('shard'), may hold values from 0.099609375 to 1.8984375
- ln1_bias: bfloat16 [1152], P('shard'), may hold values from -3 to 3
- query_weight: bfloat16 [1152, 1152], P(None, 'shard'), may hold values from -0.1875 to 0.1875
- query_bias: bfloat16 [1152], P('shard'), may hold values from -3 to 3
- key_weight: bfloat16 [1152, 1152], P(None, 'shard'), may hold values from -0.1875 to 0.1875
- value_weight: bfloat16 [1152, 1152], P(None, 'shard'), may hold values from -0.1875 to 0.1875
- value_bias: bfloat16 [1152], P('shard'), may hold values from -3 to 3
- proj_weight: bfloat16 [1152, 1152], P('shard'), may hold values from -1.5 to 1.5
- proj_bias: bfloat16 [1152], P('shard'), may hold values from -3 to 3
- ln2_gain: bfloat16 [1152], P('shard'), may hold values from 0.099609375 to 1.8984375
- ln2_bias: bfloat16 [1152], P('shard'), may hold values from -3 to 3
- up_weight: bfloat16 [1152, 4304], P(None, 'shard'), may hold values from -0.1875 to 0.1875
- up_bias: bfloat16 [4304], P('shard'), may hold values from -3 to 3
- down_weight: bfloat16 [4304, 1152], P('shard'), may hold values from -0.09375 to 0.09375
- down_bias: bfloat16 [1152], P('shard'), may hold values from -3 to 3
Outputs:
- block_out: bfloat16 [8192, 1152], P(('shard', 'replica'))
- tokens_grad: bfloat16 [8192, 1152], P(('shard', 'replica'))
- ln1_gain_grad: float32 [1152], P('shard')
- ln1_bias_grad: float32 [1152], P('shard')
- query_weight_grad: float32 [1152, 1152], P('replica', 'shard')
- query_bias_grad: float32 [1152], P('shard')
- key_weight_grad: float32 [1152, 1152], P('replica', 'shard')
- value_weight_grad: float32 [1152, 1152], P('replica', 'shard')
- value_bias_grad: float32 [1152], P('shard')
- proj_weight_grad: float32 [1152, 1152], P('shard', 'replica')
- proj_bias_grad: float32 [1152], P('shard')
- ln2_gain_grad: float32 [1152], P('shard')
- ln2_bias_grad: float32 [1152], P('shard')
- up_weight_grad: float32 [1152, 4304], P('replica', 'shard')
- up_bias_grad: float32 [4304], P('shard')
- down_weight_grad: float32 [4304, 1152], P('shard', 'replica')
- down_bias_grad: float32 [1152], P('shard')
Inputs may be any that keep to these rules, and one draw needn't show every extreme that they name: `picture_ids`: within each aligned block of 256 slots (one device's) the ids start at 0, never fall, and every id occurs; pad slots carry the id of the block's last picture. `live_slots`: within each aligned block of 256 slots the zeros, if any, are the last slots, and every picture has live slots.
All inputs are finite; a program needn't handle non-finite values.
Results may differ from a plain program's by a relative error of at most 0.014.
Values may be sent and summed in bfloat16 or wider, within the bound.
A program may use at most 192 MiB of HBM per device.

v0:
```python
import jax
import jax.numpy as jnp
from jax import lax
from jax.sharding import PartitionSpec as P

HDIM = 72


norm_eps = 1e-06


def layer_norm(values, scale_gain, shift_bias):
    centered = values - jnp.mean(values, axis=-1, keepdims=True)
    variance = jnp.mean(centered * centered, axis=-1, keepdims=True)
    return centered * lax.rsqrt(variance + norm_eps) * scale_gain + shift_bias


def norm_back(values, scale_gain, shift_bias, grad_normed):
    outputs, pullback = jax.vjp(layer_norm, values, scale_gain, shift_bias)
    return pullback(grad_normed)


def gelu_tanh(values):
    return jax.nn.gelu(values, approximate=True)


def product(left_side, right_side):
    return jnp.dot(left_side, right_side, preferred_element_type=jnp.float32)


def product_tn(left_side, right_side):
    return lax.dot_general(
        left_side, right_side, (((0,), (0,)), ((), ())), preferred_element_type=jnp.float32
    )


def product_nt(left_side, right_side):
    return lax.dot_general(
        left_side, right_side, (((1,), (1,)), ((), ())), preferred_element_type=jnp.float32
    )


def column_sums(matrix):
    return jnp.sum(matrix, axis=0, dtype=jnp.float32)


def block_allowed(picture, alive_rows, block_rows):
    grouped = picture.reshape(-1, block_rows)
    living = alive_rows.reshape(-1, block_rows)
    return (grouped[:, :, None] == grouped[:, None, :]) & (living[:, None, :] == 1)


def split_heads(matrix, block_rows):
    return matrix.reshape(-1, block_rows, matrix.shape[1] // HDIM, HDIM)


def masked_scores(queries, keys_in, allowed, block_rows):
    scores = jnp.einsum(
        "bqhd,bkhd->bhqk",
        split_heads(queries, block_rows),
        split_heads(keys_in, block_rows),
        preferred_element_type=jnp.float32,
    ) * HDIM ** (-0.5)
    return jnp.where(allowed[:, None, :, :], scores, -1e30)


def attend(queries, keys_in, values_in, allowed, block_rows):
    scores = masked_scores(queries, keys_in, allowed, block_rows)
    highest = jnp.max(scores, axis=-1, keepdims=True)
    scaled_exp = jnp.exp(scores - highest)
    totals = jnp.sum(scaled_exp, axis=-1, keepdims=True)
    probs_low = (scaled_exp / totals).astype(jnp.bfloat16)
    mixed_out = jnp.einsum(
        "bhqk,bkhd->bqhd",
        probs_low,
        split_heads(values_in, block_rows),
        preferred_element_type=jnp.float32,
    )
    return (mixed_out.reshape(queries.shape), highest + jnp.log(totals))


def attend_back(queries, keys_in, values_in, grad_mixed, allowed, log_totals, block_rows):
    score_scale = HDIM ** (-0.5)
    scores = masked_scores(queries, keys_in, allowed, block_rows)
    attn_probs = jnp.exp(scores - log_totals)
    split_grad = split_heads(grad_mixed, block_rows)
    grad_probs = jnp.einsum(
        "bqhd,bkhd->bhqk",
        split_grad,
        split_heads(values_in, block_rows),
        preferred_element_type=jnp.float32,
    )
    grad_scores = (
        attn_probs * (grad_probs - jnp.sum(attn_probs * grad_probs, axis=-1, keepdims=True))
    ).astype(jnp.bfloat16)
    grad_queries = (
        jnp.einsum(
            "bhqk,bkhd->bqhd",
            grad_scores,
            split_heads(keys_in, block_rows),
            preferred_element_type=jnp.float32,
        )
        * score_scale
    )
    grad_keys = (
        jnp.einsum(
            "bhqk,bqhd->bkhd",
            grad_scores,
            split_heads(queries, block_rows),
            preferred_element_type=jnp.float32,
        )
        * score_scale
    )
    grad_values = jnp.einsum(
        "bhqk,bqhd->bkhd",
        attn_probs.astype(jnp.bfloat16),
        split_grad,
        preferred_element_type=jnp.float32,
    )
    return (
        grad_queries.astype(jnp.bfloat16).reshape(queries.shape),
        grad_keys.astype(jnp.bfloat16).reshape(queries.shape),
        grad_values.astype(jnp.bfloat16).reshape(queries.shape),
    )


def own_half(vector):
    half_width = vector.shape[0] // lax.axis_size("shard")
    return lax.dynamic_slice_in_dim(vector, lax.axis_index("shard") * half_width, half_width, 0)


def shards(
    tokens,
    out_grad,
    picture_ids,
    live_slots,
    ln1_gain,
    ln1_bias,
    query_weight,
    query_bias,
    key_weight,
    value_weight,
    value_bias,
    proj_weight,
    proj_bias,
    ln2_gain,
    ln2_bias,
    up_weight,
    up_bias,
    down_weight,
    down_bias,
):
    block_rows = tokens.shape[0]
    alive_cols = live_slots.astype(jnp.float32)[:, None]
    tokens_f = tokens.astype(jnp.float32)
    out_rows_f = out_grad.astype(jnp.float32) * alive_cols
    out_rows = out_rows_f.astype(jnp.bfloat16)
    gathered = (
        lax.all_gather(ln1_gain, "shard", axis=0, tiled=True),
        lax.all_gather(ln1_bias, "shard", axis=0, tiled=True),
        lax.all_gather(query_weight, "shard", axis=1, tiled=True),
        lax.all_gather(query_bias, "shard", axis=0, tiled=True),
        lax.all_gather(key_weight, "shard", axis=1, tiled=True),
        lax.all_gather(value_weight, "shard", axis=1, tiled=True),
        lax.all_gather(value_bias, "shard", axis=0, tiled=True),
        lax.all_gather(proj_weight, "shard", axis=0, tiled=True),
        lax.all_gather(proj_bias, "shard", axis=0, tiled=True),
        lax.all_gather(ln2_gain, "shard", axis=0, tiled=True),
        lax.all_gather(ln2_bias, "shard", axis=0, tiled=True),
        lax.all_gather(up_weight, "shard", axis=1, tiled=True),
        lax.all_gather(up_bias, "shard", axis=0, tiled=True),
        lax.all_gather(down_weight, "shard", axis=0, tiled=True),
        lax.all_gather(down_bias, "shard", axis=0, tiled=True),
    )
    gain_one = gathered[0].astype(jnp.float32)
    shift_one = gathered[1].astype(jnp.float32)
    full_query = gathered[2]
    bias_query = gathered[3].astype(jnp.float32)
    full_key = gathered[4]
    full_value = gathered[5]
    bias_value = gathered[6].astype(jnp.float32)
    full_proj = gathered[7]
    bias_proj = gathered[8].astype(jnp.float32)
    gain_two = gathered[9].astype(jnp.float32)
    shift_two = gathered[10].astype(jnp.float32)
    full_up = gathered[11]
    bias_up = gathered[12].astype(jnp.float32)
    full_down = gathered[13]
    bias_down = gathered[14].astype(jnp.float32)
    allowed = block_allowed(picture_ids, live_slots, block_rows)
    normed = layer_norm(tokens_f, gain_one, shift_one).astype(jnp.bfloat16)
    queries = (product(normed, full_query) + bias_query).astype(jnp.bfloat16)
    keys_all = product(normed, full_key).astype(jnp.bfloat16)
    values_all = (product(normed, full_value) + bias_value).astype(jnp.bfloat16)
    mixed_out, log_totals = attend(queries, keys_all, values_all, allowed, block_rows)
    mixed_low = mixed_out.astype(jnp.bfloat16)
    hidden = tokens_f + product(mixed_low, full_proj) + bias_proj
    normed_two = layer_norm(hidden, gain_two, shift_two).astype(jnp.bfloat16)
    up_proj = product(normed_two, full_up) + bias_up
    activated = gelu_tanh(up_proj).astype(jnp.bfloat16)
    block_out = ((hidden + product(activated, full_down) + bias_down) * alive_cols).astype(
        jnp.bfloat16
    )
    grad_act = product_nt(out_rows, full_down)
    grad_up = jax.vjp(gelu_tanh, up_proj)[1](grad_act)[0].astype(jnp.bfloat16)
    grad_normed_two = product_nt(grad_up, full_up)
    grad_hidden_part, grad_gain_two, grad_shift_two = norm_back(
        hidden, gain_two, shift_two, grad_normed_two
    )
    grad_hidden = out_rows_f + grad_hidden_part
    grad_hidden_low = grad_hidden.astype(jnp.bfloat16)
    grad_mixed = product_nt(grad_hidden_low, full_proj).astype(jnp.bfloat16)
    grad_queries, grad_keys, grad_values = attend_back(
        queries, keys_all, values_all, grad_mixed, allowed, log_totals, block_rows
    )
    grad_normed = (
        product_nt(grad_queries, full_query)
        + product_nt(grad_keys, full_key)
        + product_nt(grad_values, full_value)
    )
    grad_tokens_part, grad_gain_one, grad_shift_one = norm_back(
        tokens_f, gain_one, shift_one, grad_normed
    )
    matrix_grads = (
        lax.psum_scatter(
            product_tn(normed, grad_queries).astype(jnp.bfloat16),
            "shard",
            scatter_dimension=1,
            tiled=True,
        ).astype(jnp.float32),
        lax.psum_scatter(
            product_tn(normed, grad_keys).astype(jnp.bfloat16),
            "shard",
            scatter_dimension=1,
            tiled=True,
        ).astype(jnp.float32),
        lax.psum_scatter(
            product_tn(normed, grad_values).astype(jnp.bfloat16),
            "shard",
            scatter_dimension=1,
            tiled=True,
        ).astype(jnp.float32),
        lax.psum_scatter(
            product_tn(mixed_low, grad_hidden_low).astype(jnp.bfloat16),
            "shard",
            scatter_dimension=0,
            tiled=True,
        ).astype(jnp.float32),
        lax.psum_scatter(
            product_tn(normed_two, grad_up).astype(jnp.bfloat16),
            "shard",
            scatter_dimension=1,
            tiled=True,
        ).astype(jnp.float32),
        lax.psum_scatter(
            product_tn(activated, out_rows).astype(jnp.bfloat16),
            "shard",
            scatter_dimension=0,
            tiled=True,
        ).astype(jnp.float32),
    )
    vector_grads = (
        grad_gain_one,
        grad_shift_one,
        column_sums(grad_queries),
        column_sums(grad_values),
        column_sums(grad_hidden_low),
        grad_gain_two,
        grad_shift_two,
        column_sums(grad_up),
        column_sums(out_rows_f),
    )
    reduced = (
        lax.psum_scatter(matrix_grads[0], "replica", scatter_dimension=0, tiled=True),
        lax.psum_scatter(matrix_grads[1], "replica", scatter_dimension=0, tiled=True),
        lax.psum_scatter(matrix_grads[2], "replica", scatter_dimension=0, tiled=True),
        lax.psum_scatter(matrix_grads[3], "replica", scatter_dimension=1, tiled=True),
        lax.psum_scatter(matrix_grads[4], "replica", scatter_dimension=0, tiled=True),
        lax.psum_scatter(matrix_grads[5], "replica", scatter_dimension=1, tiled=True),
    )
    vector_totals = lax.psum(
        (
            vector_grads[0],
            vector_grads[1],
            vector_grads[2],
            vector_grads[3],
            vector_grads[4],
            vector_grads[5],
            vector_grads[6],
            vector_grads[7],
            vector_grads[8],
        ),
        ("shard", "replica"),
    )
    owned_parts = [own_half(vector) for vector in vector_totals]
    tokens_grad = (grad_hidden + grad_tokens_part).astype(jnp.bfloat16)
    return (
        block_out,
        tokens_grad,
        owned_parts[0],
        owned_parts[1],
        reduced[0],
        owned_parts[2],
        reduced[1],
        reduced[2],
        owned_parts[3],
        reduced[3],
        owned_parts[4],
        owned_parts[5],
        owned_parts[6],
        reduced[4],
        owned_parts[7],
        reduced[5],
        owned_parts[8],
    )


def solution(mesh):
    in_specs = (
        P(("shard", "replica"), None),
        P(("shard", "replica"), None),
        P(("shard", "replica")),
        P(("shard", "replica")),
        P("shard"),
        P("shard"),
        P(None, "shard"),
        P("shard"),
        P(None, "shard"),
        P(None, "shard"),
        P("shard"),
        P("shard", None),
        P("shard"),
        P("shard"),
        P("shard"),
        P(None, "shard"),
        P("shard"),
        P("shard", None),
        P("shard"),
    )
    out_specs = (
        P(("shard", "replica"), None),
        P(("shard", "replica"), None),
        P("shard"),
        P("shard"),
        P("replica", "shard"),
        P("shard"),
        P("replica", "shard"),
        P("replica", "shard"),
        P("shard"),
        P("shard", "replica"),
        P("shard"),
        P("shard"),
        P("shard"),
        P("replica", "shard"),
        P("shard"),
        P("shard", "replica"),
        P("shard"),
    )
    return jax.shard_map(shards, mesh=mesh, in_specs=in_specs, out_specs=out_specs, check_vma=False)
```

profile of v0, /device:TPU:0, one launch (start us, length us, event | category | flops | bytes accessed | tf_op | source)
XLA Modules:
  0.0 1344.4 jit_solution(14598696122529984937)
XLA Ops:
  15.5 11.9 all-reduce.22
  28.2 24.0 %all-gather.7.cloned.1.call-done = bf16[1152,1152]{0,1:T(8,128)(2,1)} async-done(((bf16[1152,576]{0,1:T(8,128)(2,1)}), bf16[1152,1152]{0,1:T(8,128)(2,1)}) %all-gather.7.cloned.1.call-update) | async-done | bytes 2654224 | tf_op jit(solution)/shard_map/all_gather | solution.py:164
  52.2 2.8 fusion.15
  55.3 38.1 %all-gather.9.cloned.1.call-done = bf16[1152,1152]{0,1:T(8,128)(2,1)} async-done(((bf16[1152,576]{0,1:T(8,128)(2,1)}), bf16[1152,1152]{0,1:T(8,128)(2,1)}) %all-gather.9.cloned.1.call-update) | async-done | bytes 2654224 | tf_op jit(solution)/shard_map/all_gather | solution.py:161
  93.4 2.8 fusion.16
  96.5 37.9 %all-gather.11.cloned.1.call-done = bf16[1152,1152]{0,1:T(8,128)(2,1)} async-done(((bf16[1152,576]{0,1:T(8,128)(2,1)}), bf16[1152,1152]{0,1:T(8,128)(2,1)}) %all-gather.11.cloned.1.call-update) | async-done | bytes 2654224 | tf_op jit(solution)/shard_map/all_gather | solution.py:163
  134.3 2.8 convolution_convert_fusion.7
  137.5 0.9 fusion.59
  138.9 1.4 copy-done
  140.3 0.9 fusion.27
  141.2 33.9 %all-gather.13.cloned.1.call-done = bf16[1152,1152]{1,0:T(8,128)(2,1)} async-done(((bf16[576,1152]{1,0:T(8,128)(2,1)}), bf16[1152,1152]{1,0:T(8,128)(2,1)}) %all-gather.13.cloned.1.call-update) | async-done | bytes 2654224 | tf_op jit(solution)/shard_map/all_gather | solution.py:166
  175.2 2.9 fusion.60
  178.4 121.5 %all-gather.15.cloned.1.call-done = bf16[1152,4304]{0,1:T(8,128)(2,1)} async-done(((bf16[1152,2152]{0,1:T(8,128)(2,1)}), bf16[1152,4304]{0,1:T(8,128)(2,1)}) %all-gather.15.cloned.1.call-update) | async-done | bytes 9916432 | tf_op jit(solution)/shard_map/all_gather | solution.py:170
  299.8 9.3 convolution_add_fusion
  309.2 115.4 %all-gather.17.cloned.1.call-done = bf16[4304,1152]{1,0:T(8,128)(2,1)} async-done(((bf16[2152,1152]{1,0:T(8,128)(2,1)}), bf16[4304,1152]{1,0:T(8,128)(2,1)}) %all-gather.17.cloned.1.call-update) | async-done | bytes 9916432 | tf_op jit(solution)/shard_map/all_gather | solution.py:172
  424.5 9.9 convert_reduce_fusion
  434.4 3.9 multiply_reduce_fusion.1
  438.7 1.0 copy-done.8
  439.7 0.9 convert_reduce_fusion.2
  440.6 1.1 convolution_convert_fusion.6
  442.0 3.4 multiply_reduce_fusion
  445.4 1.0 multiply_convert_fusion.1
  446.5 1.2 convert_reduce_fusion.4
  447.7 0.8 copy-done.19
  448.5 2.6 convolution_convert_fusion.4
  451.4 1.8 fusion.29
  454.1 2.6 convolution_convert_fusion.3
  456.8 4.3 convert_reduce_fusion.3
  461.1 2.6 convolution_convert_fusion.2
  463.6 8.5 convolution_convert_fusion
  472.2 182.3 %fusion = bf16[1152,2176]{0,1:T(8,128)(2,1)} fusion(bf16[1152,4304]{0,1:T(8,128)(2,1)} %convolution_convert_fusion), kind=kCustom, calls=%all-reduce-scatter | all-reduce-scatter fusion | flops 5013505 | bytes 14930432
  654.5 1.4 slice
  655.9 3.0 collective-permute-start
  658.9 3.5 convolution_convert_fusion.5
  662.4 9.9 convolution_convert_fusion.1
  672.4 146.1 %fusion.1 = bf16[2176,1152]{1,0:T(8,128)(2,1)} fusion(bf16[4304,1152]{1,0:T(8,128)(2,1)} %convolution_convert_fusion.1), kind=kCustom, calls=%all-reduce-scatter.1 | all-reduce-scatter fusion | flops 5013505 | bytes 14930432
  818.4 0.8 slice.1
  819.3 2.8 collective-permute-start.1
  822.7 23.0 %concatenate = bf16[1152,2200]{0,1:T(8,128)(2,1)} concatenate(bf16[1152,24]{0,1:T(8,128)(2,1)} %collective-permute-done, bf16[1152,2176]{0,1:T(8,128)(2,1)} %fusion), dimensions={1} | concatenate | bytes 10137600
  845.7 22.1 %concatenate.1 = bf16[2200,1152]{1,0:T(8,128)(2,1)} concatenate(bf16[24,1152]{1,0:T(8,128)(2,1)S(1)} %collective-permute-done.1, bf16[2176,1152]{1,0:T(8,128)(2,1)} %fusion.1), dimensions={0} | concatenate | bytes 10137600
  867.9 6.9 dynamic-slice_convert_fusion.1
  874.8 4.3 dynamic-slice_convert_fusion
  879.1 1.3 convert_element_type.193
  880.4 1.2 dynamic-slice.9
  882.3 1.4 reduce_sum.196
  883.7 1.4 reduce_sum.198
  885.1 3.1 fusion.61
  888.2 1.0 convolution_add_fusion.2
  890.0 1.3 fusion.55
  892.6 1.5 fusion.38
  894.1 43.3 %all-reduce.19 = (f32[1152]{0:T(1024)S(1)}, f32[1152]{0:T(1024)S(1)}, f32[1152]{0:T(1024)S(1)}, f32[1152]{0:T(1024)S(1)}, f32[1152]{0:T(1024)S(1)}, /*index=5*/f...) all-reduce(f32[1152]{0:T(1024)S(1)} %get-tuple-element.70, ...), channel_id=1, replica_groups=mesh['shard'=2,'replica'=16] {'shard','replica'}, use_global_device_ids=true, to_apply=%region_12.13 | all-reduce | flops 13520 | bytes 108160 | tf_op jit(solution)/shard_map/psum | solution.py:281
  943.4 9.8 fusion.14
  953.3 301.8 %all-reduce.27 = (f32[1152,576]{0,1:T(8,128)}, f32[1152,576]{0,1:T(8,128)}, f32[1152,576]{0,1:T(8,128)}, f32[576,1152]{1,0:T(8,128)S(1)}) all-reduce(bf16[1152,576]{0,1:T(8,128)(2,1)} %reduce-scatter.15.cloned.1.call-done, ...), channel_id=3, replica_groups=mesh['shard'=2,'replica'=16] {'replica'}, use_global_device_ids=true, to_apply=%region_16.17.clone | all-reduce | flops 2654208 | bytes 15925248
  1255.1 1.2 constant_dynamic-slice_fusion.5
  1256.3 0.8 copy.76
  1257.1 1.5 constant_dynamic-slice_fusion.3
  1258.6 0.8 copy.77
  1259.4 0.8 copy.78
  1260.4 0.8 copy.79
  1261.2 70.2 %all-reduce.26.cloned.1.call-done = (f32[1152,2152]{0,1:T(8,128)}, f32[2152,1152]{1,0:T(8,128)}) async-done(((f32[1152,2152]{0,1:T(8,128)}, f32[2152,1152]{1,0:T(8,128)}), (f32[1152,2152]{0,1:T(8,128)}, f32[2152,1152]{1,0:T(8,128)})) %all-reduce.26.cloned.1.call-update) | async-done | bytes 19832848
  1331.4 2.0 constant_dynamic-slice_fusion
  1333.3 1.2 copy.80
  1334.5 2.0 constant_dynamic-slice_fusion.1
  1336.5 1.2 copy.81
  (184 shorter events, 19.2 us)
Async XLA Ops:
  7.2 45.0 %all-gather.7.cloned.1.call-start = ((), (), s32[]{:S(2)}) async-start(), calls=%async_computation.4 | async-start | bytes 3981312 | tf_op jit(solution)/shard_map/all_gather | solution.py:164
  7.9 85.5 %all-gather.9.cloned.1.call-start = ((), (), s32[]{:S(2)}) async-start(), calls=%async_computation.5 | async-start | bytes 3981312 | tf_op jit(solution)/shard_map/all_gather | solution.py:161
  8.7 125.7 %all-gather.11.cloned.1.call-start = ((), (), s32[]{:S(2)}) async-start(), calls=%async_computation.6 | async-start | bytes 3981312 | tf_op jit(solution)/shard_map/all_gather | solution.py:163
  9.4 165.7 %all-gather.13.cloned.1.call-start = ((), (), s32[]{:S(2)}) async-start(), calls=%async_computation.7 | async-start | bytes 3981312 | tf_op jit(solution)/shard_map/all_gather | solution.py:166
  10.0 289.8 %all-gather.15.cloned.1.call-start = ((), (), s32[]{:S(2)}) async-start(), calls=%async_computation.8 | async-start | bytes 14874624 | tf_op jit(solution)/shard_map/all_gather | solution.py:170
  10.6 0.8 copy-start.47
  10.6 2.7 copy-start.39
  10.6 2.9 copy-start.40
  10.6 3.1 copy-start.41
  10.6 3.4 copy-start.42
  10.6 3.6 copy-start.43
  10.6 3.9 copy-start.44
  10.6 4.1 copy-start.45
  10.7 4.3 copy-start.46
  10.7 4.6 copy-start.37
  10.7 16.8 %copy-start.48 = (s32[256]{0:T(256)S(1)}, s32[256]{0:T(256)}, u32[]{:S(2)}) copy-start(s32[256]{0:T(256)} %param.22) | copy-start | bytes 3076
  10.7 16.8 %copy-start.2 = (bf16[256,1152]{1,0:T(8,128)(2,1)S(1)}, bf16[256,1152]{1,0:T(8,128)(2,1)}, u32[]{:S(2)}) copy-start(bf16[256,1152]{1,0:T(8,128)(2,1)} %param.19) | copy-start | bytes 1769476
  10.7 17.4 %copy-start.38 = (s32[256]{0:T(256)S(1)}, s32[256]{0:T(256)}, u32[]{:S(2)}) copy-start(s32[256]{0:T(256)} %param.21) | copy-start | bytes 3076
  10.7 413.8 %all-gather.17.cloned.1.call-start = ((), (), s32[]{:S(2)}) async-start(), calls=%async_computation.9 | async-start | bytes 14874624 | tf_op jit(solution)/shard_map/all_gather | solution.py:172
  11.3 942.0 %reduce-scatter.15.cloned.1.call-start = ((), (), s32[]{:S(2)}) async-start(), calls=%async_computation.10 | async-start | bytes 3981312 | tf_op jit(solution)/shard_map/reduce_scatter | solution.py:225
  27.5 411.2 %copy-start.30 = (f32[256]{0:T(256)}, f32[256]{0:T(256)S(1)}, u32[]{:S(2)}) copy-start(f32[256]{0:T(256)S(1)} %convert_element_type.194) | copy-start | bytes 3076
  28.0 27.0 %copy-start.34 = (f32[256]{0:T(256)}, f32[256]{0:T(256)S(1)}, u32[]{:S(2)}) copy-start(f32[256]{0:T(256)S(1)} %fusion.36) | copy-start | bytes 3076
  96.5 41.0 %copy-start.12 = (bf16[256,1152]{0,1:T(8,128)(2,1)}, bf16[256,1152]{0,1:T(8,128)(2,1)S(1)}, u32[]{:S(2)}) copy-start(bf16[256,1152]{0,1:T(8,128)(2,1)S(1)} %copy.69) | copy-start | bytes 1769476
  137.4 0.9 copy-start.13
  138.3 2.0 copy-start
  141.2 36.8 %copy-start.23 = (bf16[16,72,256]{2,1,0:T(8,128)(2,1)}, bf16[16,72,256]{2,1,0:T(8,128)(2,1)S(1)}, u32[]{:S(2)}) copy-start(bf16[16,72,256]{2,1,0:T(8,128)(2,1)S(1)} %fusion.27) | copy-start | bytes 1769476
  178.0 260.2 %copy-start.5 = (f32[256,1152]{1,0:T(8,128)}, f32[256,1152]{1,0:T(8,128)S(1)}, u32[]{:S(2)}) copy-start(f32[256,1152]{1,0:T(8,128)S(1)} %get-tuple-element.110) | copy-start | bytes 3538948
  178.4 246.2 %copy-start.17 = (bf16[256,1152]{1,0:T(8,128)(2,1)S(1)}, bf16[256,1152]{1,0:T(8,128)(2,1)}, u32[]{:S(2)}) copy-start(bf16[256,1152]{1,0:T(8,128)(2,1)} %param.20) | copy-start | bytes 1769476
  424.5 9.9 copy-start.3
  434.4 3.9 copy-start.7
  438.3 2.3 copy-start.49
  438.7 1.0 copy-start.8
  438.7 3.0 copy-start.32
  440.6 1.1 copy-start.21
  441.9 3.5 copy-start.1
  445.4 1.1 copy-start.14
  447.7 0.8 copy-start.19
  451.2 502.1 %reduce-scatter.17.cloned.1.call-start = ((), (), s32[]{:S(2)}) async-start(), calls=%async_computation.11 | async-start | bytes 3981312 | tf_op jit(solution)/shard_map/reduce_scatter | solution.py:231
  453.3 0.8 copy-start.10
  456.7 496.6 %reduce-scatter.19.cloned.1.call-start = ((), (), s32[]{:S(2)}) async-start(), calls=%async_computation.12 | async-start | bytes 3981312 | tf_op jit(solution)/shard_map/reduce_scatter | solution.py:237
  461.1 2.6 copy-start.6
  472.1 186.8 %copy-start.22 = (bf16[256,1152]{1,0:T(8,128)(2,1)S(1)}, bf16[256,1152]{1,0:T(8,128)(2,1)}, u32[]{:S(2)}) copy-start(bf16[256,1152]{1,0:T(8,128)(2,1)} %copy-done.21) | copy-start | bytes 1769476
  472.2 481.1 %reduce-scatter.21.cloned.1.call-start = ((), (), s32[]{:S(2)}) async-start(), calls=%async_computation.13 | async-start | bytes 3981312 | tf_op jit(solution)/shard_map/reduce_scatter | solution.py:243
  655.9 6.5 copy-start.18
  655.9 166.8 %collective-permute-start = (bf16[1152,24]{0,1:T(8,128)(2,1)}, bf16[1152,24]{0,1:T(8,128)(2,1)}, u32[]{:S(2)}, u32[]{:S(2)}) collective-permute-start(bf16[1152,24]{0,1:T(8,128)(2,1)} %slice), channel_id=1, source_target_pairs={{0,16},{1,17},{2,18},{3,19},{4,20},{5,21},{6,22},{7,23},{8,24},{9,... | collective-permute-start | bytes 165896
  672.3 659.0 %all-reduce.26.cloned.1.call-start = ((), (), s32[]{:S(2)}) async-start(), calls=%async_computation.14 | async-start | bytes 39665664
  819.3 26.5 %collective-permute-start.1 = (bf16[24,1152]{1,0:T(8,128)(2,1)S(1)}, bf16[24,1152]{1,0:T(8,128)(2,1)S(1)}, u32[]{:S(2)}, u32[]{:S(2)}) collective-permute-start(bf16[24,1152]{1,0:T(8,128)(2,1)S(1)} %slice.1), channel_id=1, source_target_pairs={{0,16},{1,17},{2,18},{3,19},{4,20},{5,21},{6,22},{7,23},{8,24},{9,... | collective-permute-start | bytes 165896
  867.9 6.9 copy-start.4
  879.1 6.0 copy-start.20
  885.1 3.1 copy-start.11
  885.1 3.1 copy-start.16
  888.2 1.8 copy-start.15
  890.0 1.3 copy-start.35
  890.0 2.0 copy-start.31
  890.0 2.0 copy-start.33
  891.3 1.3 copy-start.9
  891.9 2.2 copy-start.24
  891.9 2.1 copy-start.25
  891.9 2.1 copy-start.26
  892.0 2.1 copy-start.27
  892.0 2.1 copy-start.28
  892.0 2.1 copy-start.29
  892.6 50.8 %copy-start.36 = (f32[1152]{0:T(1024)S(1)}, f32[1152]{0:T(1024)}, u32[]{:S(2)}) copy-start(f32[1152]{0:T(1024)} %convert_element_type.193) | copy-start | bytes 13828
Sparse Core Ops, SparseCore 0:
  9.5 42.6 all-gather.6
  53.7 39.6 all-gather.8
  94.9 39.3 all-gather.10
  135.7 39.3 all-gather.12
  176.6 123.2 all-gather.14
  301.2 123.2 all-gather.16
  451.3 45.5 reduce-scatter.14
  499.1 66.5 reduce-scatter.16
  567.9 66.5 reduce-scatter.18
  672.5 66.5 reduce-scatter.20
  879.2 452.0 all-reduce.25
where the time goes:
time: 1350 us; the launch traced here: 1340 us
  blocking collectives  685 us (51%)
  waiting for transfers between devices  445 us (33%)
  matrix products  92.9 us (7%)
  local copies, waits for them, and re-layouts  79.1 us (6%)
  other arithmetic  18.5 us (1%)
  between operations  17.4 us (1%)
    unnamed x4, blocking collectives  642 us
    all_gather x1, waiting for transfers between devices, shards(): lax.all_gather(up_weight, 'shard', axis=1, tiled=True)  121 us
    all_gather x1, waiting for transfers between devices, shards(): lax.all_gather(down_weight, 'shard', axis=0, tiled=True)  115 us
    unnamed x14, waiting for transfers between devices  73.9 us
    unnamed x135, local copies, waits for them, and re-layouts  69.4 us
    psum x1, blocking collectives, shards(): lax.psum((vector_grads[0], vector_grads[1], vector_grads[2], vector_grads...  43.3 us
    all_gather x1, waiting for transfers between devices, shards(): lax.all_gather(query_weight, 'shard', axis=1, tiled=True)  38.1 us
    all_gather x1, waiting for transfers between devices, shards(): lax.all_gather(key_weight, 'shard', axis=1, tiled=True)  37.9 us
  transfers between devices with their start and end apart: 13, of which 7 were waited for; matrix products, arithmetic and copies ran while one was open for 36% of the time, Pallas kernels for 0%

commit v1 on v0

v1 whole, which is shorter than its diff:
```python
import functools

import jax
import jax.numpy as jnp
from jax import lax
from jax.experimental import pallas as pl
from jax.experimental.pallas import tpu as pltpu
from jax.sharding import PartitionSpec as P

HDIM = 72
norm_eps = 1e-06
MESH = pl.DeviceIdType.MESH
CW = 256


def norm_stats(values):
    centered = values - jnp.mean(values, axis=-1, keepdims=True)
    variance = jnp.mean(centered * centered, axis=-1, keepdims=True)
    inverse = lax.rsqrt(variance + norm_eps)
    return centered * inverse, inverse


def norm_grad(xhat, inverse, gain, grad):
    scaled = grad * gain
    return (
        scaled
        - jnp.mean(scaled, axis=-1, keepdims=True)
        - xhat * jnp.mean(scaled * xhat, axis=-1, keepdims=True)
    ) * inverse


def gelu_tanh(values):
    return jax.nn.gelu(values, approximate=True)


def product(left_side, right_side):
    return jnp.dot(left_side, right_side, preferred_element_type=jnp.float32)


def product_nt(left_side, right_side):
    return lax.dot_general(
        left_side, right_side, (((1,), (1,)), ((), ())), preferred_element_type=jnp.float32
    )


def product_tn(left_side, right_side):
    return lax.dot_general(
        left_side, right_side, (((0,), (0,)), ((), ())), preferred_element_type=jnp.float32
    )


def column_sums(matrix):
    return jnp.sum(matrix, axis=0, dtype=jnp.float32)


def swap(value):
    return lax.ppermute(value, "shard", [(0, 1), (1, 0)])


def split_heads(matrix, block_rows):
    return matrix.reshape(-1, block_rows, matrix.shape[1] // HDIM, HDIM)


def attend(queries, keys_in, values_in, allowed, block_rows):
    scores = jnp.einsum(
        "bqhd,bkhd->bhqk",
        split_heads(queries, block_rows),
        split_heads(keys_in, block_rows),
        preferred_element_type=jnp.float32,
    ) * HDIM ** (-0.5)
    scores = jnp.where(allowed[:, None, :, :], scores, -1e30)
    highest = jnp.max(scores, axis=-1, keepdims=True)
    scaled_exp = jnp.exp(scores - highest)
    totals = jnp.sum(scaled_exp, axis=-1, keepdims=True)
    probs = scaled_exp / totals
    mixed_out = jnp.einsum(
        "bhqk,bkhd->bqhd",
        probs.astype(jnp.bfloat16),
        split_heads(values_in, block_rows),
        preferred_element_type=jnp.float32,
    )
    return mixed_out.reshape(queries.shape), probs


def attend_back(queries, keys_in, values_in, grad_mixed, probs, block_rows):
    score_scale = HDIM ** (-0.5)
    split_grad = split_heads(grad_mixed, block_rows)
    grad_probs = jnp.einsum(
        "bqhd,bkhd->bhqk",
        split_grad,
        split_heads(values_in, block_rows),
        preferred_element_type=jnp.float32,
    )
    grad_scores = (
        probs * (grad_probs - jnp.sum(probs * grad_probs, axis=-1, keepdims=True))
    ).astype(jnp.bfloat16)
    grad_queries = (
        jnp.einsum(
            "bhqk,bkhd->bqhd",
            grad_scores,
            split_heads(keys_in, block_rows),
            preferred_element_type=jnp.float32,
        )
        * score_scale
    )
    grad_keys = (
        jnp.einsum(
            "bhqk,bqhd->bkhd",
            grad_scores,
            split_heads(queries, block_rows),
            preferred_element_type=jnp.float32,
        )
        * score_scale
    )
    grad_values = jnp.einsum(
        "bhqk,bqhd->bkhd",
        probs.astype(jnp.bfloat16),
        split_grad,
        preferred_element_type=jnp.float32,
    )
    return (
        grad_queries.astype(jnp.bfloat16).reshape(queries.shape),
        grad_keys.astype(jnp.bfloat16).reshape(queries.shape),
        grad_values.astype(jnp.bfloat16).reshape(queries.shape),
    )


def add_low(first, second):
    return (first.astype(jnp.float32) + second.astype(jnp.float32)).astype(jnp.bfloat16)


def reduce_kernel(
    wide_left,
    wide_right,
    thin_left,
    thin_first,
    thin_second,
    vectors,
    sums_out,
    vectors_out,
    wide_left_in,
    wide_right_in,
    thin_left_in,
    thin_other_in,
    thin_first_in,
    thin_second_in,
    grads,
    from_y,
    from_low,
    from_high,
    summed,
    vector_sum,
    vector_in,
    pair_send,
    pair_recv,
    y_send,
    y_recv,
    low_send,
    low_recv,
    high_send,
    high_recv,
    core_send,
    core_recv,
    vec_send,
    vec_recv,
):
    chunks = grads.shape[0]
    rows = grads.shape[4]
    wide_chunks = chunks - 5
    shard = lax.axis_index("shard")
    replica = lax.axis_index("replica")
    core = lax.rem(replica, 2)
    y_bit = lax.rem(replica // 2, 2)
    low_bit = lax.rem(replica // 4, 2)
    high_bit = lax.rem(replica // 8, 2)
    partner = (shard, replica + 1 - 2 * core)
    y_peer = (shard, replica + 2 - 4 * y_bit)
    low_peer = (shard, replica + 4 - 8 * low_bit)
    high_peer = (shard, replica + 8 - 16 * high_bit)
    peers = (partner, y_peer, low_peer, high_peer)
    barrier = pltpu.get_barrier_semaphore()
    for peer in peers:
        pl.semaphore_signal(barrier, inc=1, device_id=peer, device_id_type=MESH)
    pl.semaphore_wait(barrier, len(peers))

    def remote(source, target, send, recv, peer):
        return pltpu.make_async_remote_copy(
            src_ref=source,
            dst_ref=target,
            send_sem=send,
            recv_sem=recv,
            device_id=peer,
            device_id_type=MESH,
        )

    other = 1 - core
    pairs = (
        (wide_left.at[other], wide_left_in),
        (wide_right.at[other], wide_right_in),
        (thin_left.at[0], thin_left_in),
        (thin_left.at[other], thin_other_in),
        (thin_first.at[other], thin_first_in),
        (thin_second.at[other], thin_second_in),
    )
    pair_copies = [
        remote(source, target, pair_send.at[i], pair_recv.at[i], partner)
        for i, (source, target) in enumerate(pairs)
    ]
    for copy in pair_copies:
        copy.start()

    def y_copy(j):
        return remote(
            grads.at[j, :, :, 1 - y_bit], from_y.at[j], y_send.at[j], y_recv.at[j], y_peer
        )

    def low_copy(j):
        return remote(
            grads.at[j, :, 1 - low_bit, y_bit],
            from_low.at[j],
            low_send.at[j],
            low_recv.at[j],
            low_peer,
        )

    def high_copy(j):
        return remote(
            grads.at[j, 1 - high_bit, low_bit, y_bit],
            from_high.at[j],
            high_send.at[j],
            high_recv.at[j],
            high_peer,
        )

    def core_copy(j):
        return remote(
            summed.at[j, other], sums_out.at[core, j], core_send.at[j], core_recv.at[j], partner
        )

    def core_arrival(j):
        return remote(
            summed.at[j, other], sums_out.at[other, j], core_send.at[j], core_recv.at[j], partner
        )

    def vector_copy(i):
        return remote(
            vector_sum.at[i], vector_in.at[i], vec_send.at[i], vec_recv.at[i], peers[i]
        )

    vector_sum[0] = vectors[...]
    vector_copy(0).start()

    def keep(j, value):
        grads[j] = value.astype(jnp.bfloat16).reshape(grads.shape[1:])
        y_copy(j).start()

    pair_copies[0].wait_recv()
    pair_copies[1].wait_recv()

    def wide_step(j, carry):
        columns = pl.ds(pl.multiple_of(j * CW, CW), CW)
        keep(
            j,
            product_tn(wide_left[core], wide_right[core, :, columns])
            + product_tn(wide_left_in[...], wide_right_in[:, columns]),
        )
        return carry

    lax.fori_loop(0, wide_chunks, wide_step, 0)
    for copy in pair_copies[2:]:
        copy.wait_recv()

    def first_part(columns):
        return product_tn(thin_left[0], thin_first[core, :, columns]) + product_tn(
            thin_left_in[...], thin_first_in[:, columns]
        )

    def second_part(columns):
        return product_tn(thin_left[core], thin_second[core, :, columns]) + product_tn(
            thin_other_in[...], thin_second_in[:, columns]
        )

    def thin_step(j, carry):
        columns = pl.ds(pl.multiple_of(j * CW, CW), CW)
        keep(wide_chunks + j, first_part(columns))
        keep(wide_chunks + 2 + j, second_part(columns))
        return carry

    lax.fori_loop(0, 2, thin_step, 0)
    thin_rest = pl.ds(2 * CW, thin_first.shape[2] - 2 * CW)
    wide_rest = pl.ds(wide_chunks * CW, CW // 2)
    keep(
        chunks - 1,
        jnp.concatenate(
            [
                product_tn(wide_left[core], wide_right[core, :, wide_rest])
                + product_tn(wide_left_in[...], wide_right_in[:, wide_rest]),
                first_part(thin_rest),
                second_part(thin_rest),
            ],
            axis=1,
        ),
    )

    for i in range(4):
        vector_copy(i).wait_recv()
        vector_sum[i + 1] = vector_sum[i] + vector_in[i]
        if i < 3:
            vector_copy(i + 1).start()
    vectors_out[...] = vector_sum[4]

    def pump(i, carry):
        @pl.when(i < chunks)
        def _():
            y_copy(i).wait_recv()
            grads[i, :, :, y_bit] = add_low(grads[i, :, :, y_bit], from_y[i])
            low_copy(i).start()

        @pl.when(jnp.logical_and(i >= 1, i < chunks + 1))
        def _():
            j = i - 1
            low_copy(j).wait_recv()
            grads[j, :, low_bit, y_bit] = add_low(grads[j, :, low_bit, y_bit], from_low[j])
            high_copy(j).start()

        @pl.when(jnp.logical_and(i >= 2, i < chunks + 2))
        def _():
            j = i - 2
            high_copy(j).wait_recv()
            total = grads[j, high_bit, low_bit, y_bit].astype(jnp.float32) + from_high[j].astype(
                jnp.float32
            )
            summed[j] = total.reshape(2, rows // 2, CW)
            core_copy(j).start()
            sums_out[core, j] = summed[j, core]

        @pl.when(i >= 3)
        def _():
            core_arrival(i - 3).wait_recv()

        return carry

    lax.fori_loop(0, chunks + 3, pump, 0)

    def drain(j, carry):
        y_copy(j).wait_send()
        low_copy(j).wait_send()
        high_copy(j).wait_send()
        core_copy(j).wait_send()
        return carry

    lax.fori_loop(0, chunks, drain, 0)
    for copy in pair_copies:
        copy.wait_send()
    for i in range(4):
        vector_copy(i).wait_send()


def reduce_call(wide_left, wide_right, thin_left, thin_first, thin_second, vectors):
    tokens, width = wide_left.shape[1:]
    thin_width = thin_first.shape[2]
    replicas = lax.axis_size("replica")
    rows = width // replicas * 2
    chunks = wide_right.shape[2] // CW + 5
    half = rows // 2
    low = jnp.bfloat16
    vmem = pl.BlockSpec(memory_space=pltpu.VMEM)
    dma = pltpu.SemaphoreType.DMA
    return pl.pallas_call(
        reduce_kernel,
        out_shape=(
            jax.ShapeDtypeStruct((2, chunks, half, CW), jnp.float32),
            jax.ShapeDtypeStruct(vectors.shape, jnp.float32),
        ),
        in_specs=[vmem] * 6,
        out_specs=(vmem, vmem),
        scratch_shapes=[
            pltpu.VMEM(wide_left.shape[1:], low),
            pltpu.VMEM(wide_right.shape[1:], low),
            pltpu.VMEM(thin_left.shape[1:], low),
            pltpu.VMEM(thin_left.shape[1:], low),
            pltpu.VMEM(thin_first.shape[1:], low),
            pltpu.VMEM(thin_second.shape[1:], low),
            pltpu.VMEM((chunks, 2, 2, 2, rows, CW), low),
            pltpu.VMEM((chunks, 2, 2, rows, CW), low),
            pltpu.VMEM((chunks, 2, rows, CW), low),
            pltpu.VMEM((chunks, rows, CW), low),
            pltpu.VMEM((chunks, 2, half, CW), jnp.float32),
            pltpu.VMEM((5,) + vectors.shape, jnp.float32),
            pltpu.VMEM((4,) + vectors.shape, jnp.float32),
            dma((6,)),
            dma((6,)),
            dma((chunks,)),
            dma((chunks,)),
            dma((chunks,)),
            dma((chunks,)),
            dma((chunks,)),
            dma((chunks,)),
            dma((chunks,)),
            dma((chunks,)),
            dma((4,)),
            dma((4,)),
        ],
        compiler_params=pltpu.CompilerParams(
            collective_id=0, has_side_effects=True, vmem_limit_bytes=60 << 20
        ),
        name="reduce_grads",
    )(wide_left, wide_right, thin_left, thin_first, thin_second, vectors)


def by_kernel(replicas, width):
    return replicas == 2**4 and width % (replicas // 2 * 16) == 0


def plain_sums(block_out, tokens_grad, vectors, half, wide, query, key, value, proj, up, down):
    def owned(pair):
        return lax.psum_scatter(product_tn(*pair), "replica", scatter_dimension=0, tiled=True)

    vectors = lax.psum(vectors, "replica")

    def vector_at(i):
        return vectors[i * half : (i + 1) * half]

    return (
        block_out, tokens_grad, vector_at(0), vector_at(1), owned(query), vector_at(6),
        owned(key), owned(value), vector_at(7), owned(proj).T, vector_at(2), vector_at(3),
        vector_at(4), owned(up), vectors[8 * half : 8 * half + wide], owned(down).T, vector_at(5),
    )


def paired(
    tokens, out_grad, picture_ids, live_slots, ln1_gain, ln1_bias, query_weight, query_bias,
    key_weight, value_weight, value_bias, proj_weight, proj_bias, ln2_gain, ln2_bias, up_weight,
    up_bias, down_weight, down_bias,
):
    low = jnp.bfloat16
    full = jnp.float32
    rows, width = tokens.shape
    half = width // 2
    wide = up_weight.shape[1]
    shard = lax.axis_index("shard")
    replicas = lax.axis_size("replica")
    own_vectors = jnp.stack([ln1_gain, ln1_bias, proj_bias, ln2_gain, ln2_bias, down_bias])
    slots = jnp.stack([picture_ids, live_slots])
    peer_tokens, peer_out, peer_vectors, peer_slots = (
        swap(tokens), swap(out_grad), swap(own_vectors), swap(slots),
    )
    gain_one, shift_one, bias_proj, gain_two, shift_two, bias_down = jnp.where(
        shard == 0,
        jnp.concatenate([own_vectors, peer_vectors], axis=1),
        jnp.concatenate([peer_vectors, own_vectors], axis=1),
    ).astype(full)
    slots = jnp.concatenate([slots, peer_slots], axis=1)
    alive = slots[1].astype(full)[:, None]
    ids = slots[0].reshape(2, rows)
    living = slots[1].reshape(2, rows)
    allowed = (ids[:, :, None] == ids[:, None, :]) & (living[:, None, :] == 1)
    all_tokens = jnp.concatenate([tokens, peer_tokens]).astype(full)
    all_out = jnp.concatenate([out_grad, peer_out]) * alive.astype(low)
    xhat_one, inverse_one = norm_stats(all_tokens)
    normed = (xhat_one * gain_one + shift_one).astype(low)
    queries = (product(normed, query_weight) + query_bias.astype(full)).astype(low)
    keys_all = product(normed, key_weight).astype(low)
    values_all = (product(normed, value_weight) + value_bias.astype(full)).astype(low)
    mixed_out, probs = attend(queries, keys_all, values_all, allowed, rows)
    mixed = mixed_out.astype(low)
    partial = product(mixed, proj_weight)
    hidden = all_tokens[:rows] + partial[:rows] + swap(partial[rows:].astype(low)).astype(full) + bias_proj
    xhat_two, inverse_two = norm_stats(hidden)
    normed_own = (xhat_two * gain_two + shift_two).astype(low)
    normed_two = jnp.concatenate([normed_own, swap(normed_own)])
    up_proj = product(normed_two, up_weight) + up_bias.astype(full)
    activated = gelu_tanh(up_proj).astype(low)
    grad_act = product_nt(all_out, down_weight)
    grad_up = jax.vjp(gelu_tanh, up_proj)[1](grad_act)[0].astype(low)
    partial = product_nt(grad_up, up_weight)
    grad_two = partial[:rows] + swap(partial[rows:].astype(low)).astype(full)
    partial = product(activated, down_weight)
    block_out = (
        (hidden + partial[:rows] + swap(partial[rows:].astype(low)).astype(full) + bias_down)
        * alive[:rows]
    ).astype(low)
    grad_hidden = all_out[:rows].astype(full) + norm_grad(xhat_two, inverse_two, gain_two, grad_two)
    hidden_own = grad_hidden.astype(low)
    hidden_low = jnp.concatenate([hidden_own, swap(hidden_own)])
    grad_mixed = product_nt(hidden_low, proj_weight).astype(low)
    grad_queries, grad_keys, grad_values = attend_back(
        queries, keys_all, values_all, grad_mixed, probs, rows
    )
    partial = (
        product_nt(grad_queries, query_weight)
        + product_nt(grad_keys, key_weight)
        + product_nt(grad_values, value_weight)
    )
    grad_one = partial[:rows] + swap(partial[rows:].astype(low)).astype(full)
    tokens_grad = (
        grad_hidden + norm_grad(xhat_one[:rows], inverse_one[:rows], gain_one, grad_one)
    ).astype(low)
    wholes = jnp.stack(
        [
            column_sums(grad_one * xhat_one[:rows]),
            column_sums(grad_one),
            column_sums(hidden_own),
            column_sums(grad_two * xhat_two),
            column_sums(grad_two),
            column_sums(all_out[:rows]),
        ]
    )
    mine = lax.dynamic_slice_in_dim(wholes, shard * half, half, 1)
    theirs = lax.dynamic_slice_in_dim(wholes, (1 - shard) * half, half, 1)
    halves = mine + swap(theirs)
    vectors = jnp.concatenate(
        [
            halves.reshape(-1),
            column_sums(grad_queries),
            column_sums(grad_values),
            column_sums(grad_up),
        ]
    )
    if not by_kernel(replicas, width):
        return plain_sums(
            block_out, tokens_grad, vectors, half, wide,
            (normed, grad_queries), (normed, grad_keys), (normed, grad_values),
            (hidden_low, mixed), (normed_two, grad_up), (all_out, activated),
        )
    lanes = 1024
    size = vectors.shape[0]
    vectors = jnp.pad(vectors, (0, -size % lanes)).reshape(-1, 128)
    wide_pad = -wide % 128
    wide_right = jnp.pad(jnp.stack([grad_up, activated]), ((0, 0), (0, 0), (0, wide_pad)))
    sums, vectors = reduce_call(
        jnp.stack([normed_two, all_out]),
        wide_right,
        jnp.stack([normed, hidden_low]),
        jnp.stack([grad_queries, grad_values]),
        jnp.stack([grad_keys, mixed]),
        vectors,
    )
    vectors = vectors.reshape(-1)
    chunks = sums.shape[1]
    block = sums.shape[2]
    wide_chunks = chunks - 5

    def columns(slot, first, count):
        return [sums[slot, first + i] for i in range(count)]

    rest = [sums[0, chunks - 1], sums[1, chunks - 1]]
    thin_rest = half - 2 * CW
    wide_rest = wide - wide_chunks * CW

    def wide_of(slot):
        return jnp.concatenate(columns(slot, 0, wide_chunks) + [rest[slot][:, :wide_rest]], axis=1)

    def thin_of(slot, place):
        start = CW // 2 + place * thin_rest
        return jnp.concatenate(
            columns(slot, wide_chunks + 2 * place, 2) + [rest[slot][:, start : start + thin_rest]],
            axis=1,
        )

    def vector_at(i):
        return vectors[i * half : (i + 1) * half]

    return (
        block_out,
        tokens_grad,
        vector_at(0),
        vector_at(1),
        thin_of(0, 0),
        vector_at(6),
        thin_of(0, 1),
        thin_of(1, 0),
        vector_at(7),
        thin_of(1, 1).T,
        vector_at(2),
        vector_at(3),
        vector_at(4),
        wide_of(0),
        vectors[8 * half : 8 * half + wide],
        wide_of(1).T,
        vector_at(5),
    )


def solution(mesh):
    in_specs = (
        P(("shard", "replica"), None),
        P(("shard", "replica"), None),
        P(("shard", "replica")),
        P(("shard", "replica")),
        P("shard"),
        P("shard"),
        P(None, "shard"),
        P("shard"),
        P(None, "shard"),
        P(None, "shard"),
        P("shard"),
        P("shard", None),
        P("shard"),
        P("shard"),
        P("shard"),
        P(None, "shard"),
        P("shard"),
        P("shard", None),
        P("shard"),
    )
    out_specs = (
        P(("shard", "replica"), None),
        P(("shard", "replica"), None),
        P("shard"),
        P("shard"),
        P("replica", "shard"),
        P("shard"),
        P("replica", "shard"),
        P("replica", "shard"),
        P("shard"),
        P("shard", "replica"),
        P("shard"),
        P("shard"),
        P("shard"),
        P("replica", "shard"),
        P("shard"),
        P("shard", "replica"),
        P("shard"),
    )
    return jax.shard_map(paired, mesh=mesh, in_specs=in_specs, out_specs=out_specs, check_vma=False)
```

time: 1350 us -> 373 us (0.28)
  blocking collectives: 685 us -> 0 us
  waiting for transfers between devices: 445 us -> 41.3 us
  Pallas kernels: 0 us -> 172 us
  matrix products: 92.9 us -> 44.2 us
  local copies, waits for them, and re-layouts: 79.1 us -> 55.3 us
  other arithmetic: 18.5 us -> 41.4 us
  between operations: 17.4 us -> 1.65 us
    unnamed x4 -> x0, blocking collectives: 642 us -> none
    all_gather x6 -> x0, waiting for transfers between devices: 371 us -> none  [the longest x1 121 us: shards(): lax.all_gather(up_weight, 'shard', axis=1, tiled=True)]
    pallas_call x0 -> x1, Pallas kernels: none -> 172 us  [reduce_call(): pl.pallas_call(reduce_kernel, out_shape=(jax.ShapeDtypeStruct((2, chunks,...]
    unnamed x14 -> x0, waiting for transfers between devices: 73.9 us -> none
    unnamed x135 -> x104, local copies, waits for them, and re-layouts: 69.4 us -> 16 us
    psum x1 -> x0, blocking collectives: 43.3 us -> none  [shards(): lax.psum((vector_grads[0], vector_grads[1], vector_grads[2], vector_grads...]
    ppermute x0 -> x11, waiting for transfers between devices: none -> 41.3 us  [swap(): return lax.ppermute(value, 'shard', [(0, 1), (1, 0)])]
    dot_general x9 -> x3, matrix products: 35.7 us -> 3.76 us  [the longest x1 1.81 us: attend(): jnp.einsum('bqhd,bkhd->bhqk', split_heads(queries, block_rows), split_hea...]
  transfers between devices with their start and end apart: 13 -> 11, of which waited for: 7 -> 6; matrix products, arithmetic and copies ran while one was open for 36% -> 18% of each run, Pallas kernels for 0% -> 0%
where the time goes in v1:
time: 373 us; the launch traced here: 369 us
  Pallas kernels  172 us (46%)
  local copies, waits for them, and re-layouts  55.3 us (15%)
  matrix products  44.2 us (12%)
  other arithmetic  41.4 us (11%)
  waiting for transfers between devices  41.3 us (11%)
  starting transfers between devices  13.2 us (4%)
    pallas_call x1, Pallas kernels, reduce_call(): pl.pallas_call(reduce_kernel, out_shape=(jax.ShapeDtypeStruct((2, chunks,...  172 us
    ppermute x11, waiting for transfers between devices, swap(): return lax.ppermute(value, 'shard', [(0, 1), (1, 0)])  41.3 us
    dot_general x6, matrix products, product(): return jnp.dot(left_side, right_side, preferred_element_type=jnp.float32)  19.2 us
    dot_general x6, matrix products, product_nt(): lax.dot_general(left_side, right_side, (((1,), (1,)), ((), ())), preferre...  16.2 us
    unnamed x104, local copies, waits for them, and re-layouts  16 us
    ppermute x11, starting transfers between devices, swap(): return lax.ppermute(value, 'shard', [(0, 1), (1, 0)])  13.2 us
  transfers between devices with their start and end apart: 11, of which 6 were waited for; matrix products, arithmetic and copies ran while one was open for 18% of the time, Pallas kernels for 0%

profile of v1, /device:TPU:0, one launch (start us, length us, event | category | flops | bytes accessed | tf_op | source)
XLA Modules:
  0.0 368.5 jit_solution(12364677184412487565)
XLA Ops:
  1.5 3.0 collective-permute-start.2
  8.7 2.0 collective-permute-start
  14.1 11.1 %collective-permute-done = bf16[256,1152]{1,0:T(8,128)(2,1)S(1)} collective-permute-done((bf16[256,1152]{1,0:T(8,128)(2,1)}, bf16[256,1152]{1,0:T(8,128)(2,1)S(1)}, u32[]{:S(2)}, u32[]{:S(2)}) %collective-permute-start) | collective-permute-done | bytes 589856 | tf_op jit(solution)/shard_map/ppermute | solution.py:57
  25.2 1.5 convert_reduce_fusion.1
  26.7 1.5 multiply_reduce_fusion.1
  28.3 1.1 fusion.15
  29.4 1.0 reshape.346
  30.4 3.3 convolution_convert_fusion.3
  33.6 2.1 reshape.348
  35.7 3.5 fusion.16
  39.2 2.6 reshape.347
  41.8 1.8 fusion.39
  43.6 1.4 fusion.59
  45.5 1.5 copy-done.12
  47.7 1.2 fusion.60
  49.0 2.0 collective-permute-start.3
  51.0 2.5 maximum_multiply_fusion.1
  53.7 1.5 add_convert_fusion
  55.2 6.6 %collective-permute-done.3 = bf16[256,1152]{1,0:T(8,128)(2,1)S(1)} collective-permute-done((bf16[256,1152]{1,0:T(8,128)(2,1)S(1)}, bf16[256,1152]{1,0:T(8,128)(2,1)S(1)}, u32[]{:S(2)}, u32[]{:S(2)}) %collective-permute-start.3) | collective-permute-done | bytes 589856 | tf_op jit(solution)/shard_map/ppermute | solution.py:57
  62.4 1.1 add_convert_fusion.3
  63.5 1.2 collective-permute-start.4
  64.6 2.4 maximum_multiply_fusion
  67.0 2.3 copy.91
  69.4 2.9 reshape.359
  72.3 3.0 subtract_multiply_fusion
  75.7 6.2 %convolution_add_fusion = f32[512,2152]{1,0:T(8,128)S(1)} fusion(bf16[1152,2152]{0,1:T(8,128)(2,1)} %param.34, f32[2152]{0:T(1024)S(1)} %convert_element_type.182, bf16[256,1152]{1,0:T(8,128)(2,1)} %collective-permute-done.4, bf16[256,1152]{1,0:T(8,128)(2,1)} %add_convert_fusion.3), kind=kOutput, calls=%fused_computation.6 | convolution fusion | flops 2542063616 | bytes 10553760 | tf_op jit(solution)/shard_map/dot_general | solution.py:37
  81.9 3.9 %fusion.52 = f32[512,1152]{1,0:T(8,128)S(1)} fusion(bf16[2152,1152]{1,0:T(8,128)(2,1)S(1)} %bitcast.157, f32[512,2152]{1,0:T(8,128)S(1)} %convolution_add_fusion), kind=kOutput, calls=%fused_computation.167 | convolution fusion | flops 2548518912 | bytes 11724800 | tf_op jit(solution)/shard_map/dot_general | solution.py:37
  85.8 6.9 %convert_reduce_fusion = (f32[2152]{0:T(1024)}, bf16[512,2152]{1,0:T(8,128)(2,1)S(1)}, bf16[1,512,2152]{2,1,0:T(8,128)(2,1)S(1)}) fusion(f32[512,2152]{1,0:T(8,128)S(1)} %convolution_add_fusion, bf16[512,1152]{1,0:T(8,128)(2,1)S(1)} %copy-done.16, bf16[2152,1152]{1,0:T(8,128)(2,1)S(1)} %bitcast.157), kind=kOutput, calls=%fused_computation.15 | convolution fusion | flops 2565044224 | bytes 14961056 | tf_op jit(solution)/shard_map/dot_general | solution.py:41
  92.8 3.2 fusion.61
  96.7 1.6 collective-permute-start.5
  98.3 1.3 fusion.32
  99.6 1.7 pad_maximum_fusion.wide_left
  101.4 11.0 %collective-permute-done.7 = bf16[256,1152]{1,0:T(8,128)(2,1)S(1)} collective-permute-done((bf16[256,1152]{1,0:T(8,128)(2,1)S(1)}, bf16[256,1152]{1,0:T(8,128)(2,1)S(1)}, u32[]{:S(2)}, u32[]{:S(2)}) %collective-permute-start.7) | collective-permute-done | bytes 589856 | tf_op jit(solution)/shard_map/ppermute | solution.py:57
  112.9 7.3 %collective-permute-done.5 = bf16[256,1152]{1,0:T(8,128)(2,1)S(1)} collective-permute-done((bf16[256,1152]{1,0:T(8,128)(2,1)S(1)}, bf16[256,1152]{1,0:T(8,128)(2,1)S(1)}, u32[]{:S(2)}, u32[]{:S(2)}) %collective-permute-start.5) | collective-permute-done | bytes 589856 | tf_op jit(solution)/shard_map/ppermute | solution.py:57
  120.2 2.1 convert_reduce_fusion.5
  122.9 2.2 fusion.10.wide_right
  127.6 4.9 %collective-permute-done.8 = bf16[256,1152]{1,0:T(8,128)(2,1)S(1)} collective-permute-done((bf16[256,1152]{1,0:T(8,128)(2,1)S(1)}, bf16[256,1152]{1,0:T(8,128)(2,1)S(1)}, u32[]{:S(2)}, u32[]{:S(2)}) %collective-permute-start.8) | collective-permute-done | bytes 589856 | tf_op jit(solution)/shard_map/ppermute | solution.py:57
  133.3 1.0 convolution_convert_fusion.1
  134.4 3.2 multiply_reduce_fusion
  138.9 1.2 convert_reduce_fusion.4
  140.9 1.5 convert_reduce_fusion.3
  143.2 1.4 copy.73
  144.6 1.6 copy.89
  146.2 1.4 copy.67
  147.7 1.4 copy.88
  149.7 1.6 copy.90
  151.3 1.2 copy.97
  152.5 2.7 fusion.62
  155.4 1.2 convolution_add_fusion.2
  156.7 1.2 convolution_add_fusion.1
  157.9 1.4 copy-done.3
  160.3 1.3 collective-permute-start.9
  161.5 1.7 reshape.357
  163.2 1.7 reshape.356
  164.9 1.7 reshape.358
  168.2 2.6 pad_maximum_fusion.2.thin_first
  170.8 1.3 pad_maximum_fusion.3.thin_second
  172.5 1.6 pad_maximum_fusion.1.thin_left
  175.7 1.6 multiply_reduce_fusion.3
  178.3 3.0 add_convert_fusion.2
  182.2 171.5 %reduce_grads.1 = (f32[2,13,72,256]{3,2,1,0:T(8,128)}, f32[56,128]{1,0:T(8,128)}) custom-call(bf16[2,512,1152]{2,1,0:T(8,128)(2,1)} %pad_maximum_fusion.wide_left, bf16[2,512,2176]{2,1,0:T(8,128)(2,1)} %fusion.10.wide_right, bf16[2,512,1152]{2,1,0:T(8,128)(2,1)} %pad_maximum_fusion.1.thin_left, bf16[2,512,576]{2,1,0:T(8,128)(2,1)} %pad_maximum_fusion.2.thin_first, ...), custom_call_target="tpu_custom_call" | custom-call | tf_op jit(solution)/shard_map/reduce_grads/pallas_call | solution.py:369
  353.7 1.3 slice_bitcast_fusion.1
  355.9 1.5 fusion.58
  357.4 1.3 slice.263
  (181 shorter events, 36.6 us)
Async XLA Ops:
  0.7 47.0 %copy-start = (bf16[576,1152]{1,0:T(8,128)(2,1)S(1)}, bf16[576,1152]{1,0:T(8,128)(2,1)}, u32[]{:S(2)}) copy-start(bf16[576,1152]{1,0:T(8,128)(2,1)} %param.30) | copy-start | bytes 3981316
  0.7 27.6 %copy-start.1 = (bf16[256,1152]{1,0:T(8,128)(2,1)S(1)}, bf16[256,1152]{1,0:T(8,128)(2,1)}, u32[]{:S(2)}) copy-start(bf16[256,1152]{1,0:T(8,128)(2,1)} %param.19) | copy-start | bytes 1769476
  1.5 11.3 %collective-permute-start.2 = (s32[2,256]{1,0:T(2,128)S(1)}, s32[2,256]{1,0:T(2,128)S(1)}, u32[]{:S(2)}, u32[]{:S(2)}) collective-permute-start(s32[2,256]{1,0:T(2,128)S(1)} %pad_add_fusion.1), channel_id=1, source_target_pairs={{0,16},{16,0},{1,17},{17,1},{2,18},{18,2},{3,19},{19,3},{4,20},{20... | collective-permute-start | bytes 6152 | tf_op jit(solution)/shard_map/ppermute | solution.py:57
  8.6 5.3 %collective-permute-start.1 = (bf16[6,576]{1,0:T(8,128)(2,1)S(1)}, bf16[6,576]{1,0:T(8,128)(2,1)S(1)}, u32[]{:S(2)}, u32[]{:S(2)}) collective-permute-start(bf16[6,576]{1,0:T(8,128)(2,1)S(1)} %stack.87), channel_id=1, source_target_pairs={{0,16},{16,0},{1,17},{17,1},{2,18},{18,2},{3,19},{19,3},{4,20},{20... | collective-permute-start | bytes 20744 | tf_op jit(solution)/shard_map/ppermute | solution.py:57
  8.7 16.5 %collective-permute-start = (bf16[256,1152]{1,0:T(8,128)(2,1)}, bf16[256,1152]{1,0:T(8,128)(2,1)S(1)}, u32[]{:S(2)}, u32[]{:S(2)}) collective-permute-start(bf16[256,1152]{1,0:T(8,128)(2,1)} %param.19), channel_id=1, source_target_pairs={{0,16},{16,0},{1,17},{17,1},{2,18},{18,2},{3,19},{19,3},{4,20},{20... | collective-permute-start | bytes 1769480 | tf_op jit(solution)/shard_map/ppermute | solution.py:57
  10.7 40.3 %collective-permute-start.6 = (bf16[256,1152]{1,0:T(8,128)(2,1)}, bf16[256,1152]{1,0:T(8,128)(2,1)}, u32[]{:S(2)}, u32[]{:S(2)}) collective-permute-start(bf16[256,1152]{1,0:T(8,128)(2,1)} %param.20), channel_id=1, source_target_pairs={{0,16},{16,0},{1,17},{17,1},{2,18},{18,2},{3,19},{19,3},{4,20},{20... | collective-permute-start | bytes 1769480 | tf_op jit(solution)/shard_map/ppermute | solution.py:57
  13.7 14.6 %copy-start.26 = (bf16[1152,576]{0,1:T(8,128)(2,1)S(1)}, bf16[1152,576]{0,1:T(8,128)(2,1)}, u32[]{:S(2)}) copy-start(bf16[1152,576]{0,1:T(8,128)(2,1)} %param.28) | copy-start | bytes 3981316
  14.1 39.6 %copy-start.32 = (f32[1152]{0:T(1024)}, f32[1152]{0:T(1024)S(1)}, u32[]{:S(2)}) copy-start(f32[1152]{0:T(1024)S(1)} %get-tuple-element.34) | copy-start | bytes 13828
  25.2 28.5 %copy-start.2 = (bf16[256,1152]{1,0:T(8,128)(2,1)}, bf16[256,1152]{1,0:T(8,128)(2,1)S(1)}, u32[]{:S(2)}) copy-start(bf16[256,1152]{1,0:T(8,128)(2,1)S(1)} %collective-permute-done) | copy-start | bytes 1769476
  28.2 44.0 %copy-start.34 = (f32[512]{0:T(512)}, f32[512]{0:T(512)S(1)}, u32[]{:S(2)}) copy-start(f32[512]{0:T(512)S(1)} %add_rsqrt_fusion) | copy-start | bytes 6148
  35.7 6.1 %copy-start.6 = (bf16[2,256,8,72]{1,0,3,2:T(2,128)(2,1)}, bf16[2,256,8,72]{1,0,3,2:T(2,128)(2,1)S(1)}, u32[]{:S(2)}) copy-start(bf16[2,256,8,72]{1,0,3,2:T(2,128)(2,1)S(1)} %reshape.348) | copy-start | bytes 1769476
  43.6 1.4 copy-start.28
  45.0 2.0 copy-start.12
  47.0 2.0 copy-start.21
  47.7 3.3 copy-start.24
  49.0 12.8 %collective-permute-start.3 = (bf16[256,1152]{1,0:T(8,128)(2,1)S(1)}, bf16[256,1152]{1,0:T(8,128)(2,1)S(1)}, u32[]{:S(2)}, u32[]{:S(2)}) collective-permute-start(bf16[256,1152]{1,0:T(8,128)(2,1)S(1)} %slice.348), channel_id=1, source_target_pairs={{0,16},{16,0},{1,17},{17,1},{2,18},{18,2},{3,19},{19,3},{4,20},{20... | collective-permute-start | bytes 1769480 | tf_op jit(solution)/shard_map/ppermute | solution.py:57
  63.5 12.2 %collective-permute-start.4 = (bf16[256,1152]{1,0:T(8,128)(2,1)}, bf16[256,1152]{1,0:T(8,128)(2,1)}, u32[]{:S(2)}, u32[]{:S(2)}) collective-permute-start(bf16[256,1152]{1,0:T(8,128)(2,1)} %add_convert_fusion.3), channel_id=1, source_target_pairs={{0,16},{16,0},{1,17},{17,1},{2,18},{18,2},{3,19},{19,3},{4,20},{20... | collective-permute-start | bytes 1769480 | tf_op jit(solution)/shard_map/ppermute | solution.py:57
  72.3 9.6 %slice-start.1 = ((s8[4958208]{0:T(1024)(128)(4,1)}), s8[4194304]{0:T(1024)(128)(4,1)S(1)}, s32[]{:S(2)}) async-start(s8[4958208]{0:T(1024)(128)(4,1)} %bitcast.156), calls=%async_computation.1 | async-start | bytes 8388608
  75.3 6.6 %slice-start.2 = ((s8[4958208]{0:T(1024)(128)(4,1)}), s8[763904]{0:T(1024)(128)(4,1)S(1)}, s32[]{:S(2)}) async-start(s8[4958208]{0:T(1024)(128)(4,1)} %bitcast.156), calls=%async_computation.2 | async-start | bytes 1527808
  75.7 17.1 %slice-start.3 = ((s8[4958208]{0:T(1024)(128)(4,1)}), s8[4194304]{0:T(1024)(128)(4,1)S(1)}, s32[]{:S(2)}) async-start(s8[4958208]{0:T(1024)(128)(4,1)} %bitcast.158), calls=%async_computation.3 | async-start | bytes 8388608
  81.9 4.0 %copy-start.16 = (bf16[512,1152]{1,0:T(8,128)(2,1)S(1)}, bf16[512,1152]{1,0:T(8,128)(2,1)}, u32[]{:S(2)}) copy-start(bf16[512,1152]{1,0:T(8,128)(2,1)} %maximum_multiply_fusion) | copy-start | bytes 3538948
  81.9 10.9 %slice-start.4 = ((s8[4958208]{0:T(1024)(128)(4,1)}), s8[763904]{0:T(1024)(128)(4,1)S(1)}, s32[]{:S(2)}) async-start(s8[4958208]{0:T(1024)(128)(4,1)} %bitcast.158), calls=%async_computation.4 | async-start | bytes 1527808
  96.0 3.6 copy-start.11
  96.1 16.3 %collective-permute-start.7 = (bf16[256,1152]{1,0:T(8,128)(2,1)S(1)}, bf16[256,1152]{1,0:T(8,128)(2,1)S(1)}, u32[]{:S(2)}, u32[]{:S(2)}) collective-permute-start(bf16[256,1152]{1,0:T(8,128)(2,1)S(1)} %slice.346), channel_id=1, source_target_pairs={{0,16},{16,0},{1,17},{17,1},{2,18},{18,2},{3,19},{19,3},{4,20},{20... | collective-permute-start | bytes 1769480 | tf_op jit(solution)/shard_map/ppermute | solution.py:57
  96.7 23.5 %collective-permute-start.5 = (bf16[256,1152]{1,0:T(8,128)(2,1)S(1)}, bf16[256,1152]{1,0:T(8,128)(2,1)S(1)}, u32[]{:S(2)}, u32[]{:S(2)}) collective-permute-start(bf16[256,1152]{1,0:T(8,128)(2,1)S(1)} %slice.347), channel_id=1, source_target_pairs={{0,16},{16,0},{1,17},{17,1},{2,18},{18,2},{3,19},{19,3},{4,20},{20... | collective-permute-start | bytes 1769480 | tf_op jit(solution)/shard_map/ppermute | solution.py:57
  122.3 10.2 %copy-start.19 = (bf16[256,1152]{1,0:T(8,128)(2,1)}, bf16[256,1152]{1,0:T(8,128)(2,1)S(1)}, u32[]{:S(2)}) copy-start(bf16[256,1152]{1,0:T(8,128)(2,1)S(1)} %get-tuple-element.38) | copy-start | bytes 1769476
  122.3 10.2 %collective-permute-start.8 = (bf16[256,1152]{1,0:T(8,128)(2,1)S(1)}, bf16[256,1152]{1,0:T(8,128)(2,1)S(1)}, u32[]{:S(2)}, u32[]{:S(2)}) collective-permute-start(bf16[256,1152]{1,0:T(8,128)(2,1)S(1)} %get-tuple-element.38), channel_id=1, source_target_pairs={{0,16},{16,0},{1,17},{17,1},{2,18},{18,2},{3,19},{19,3},{4,20},{20... | collective-permute-start | bytes 1769480 | tf_op jit(solution)/shard_map/ppermute | solution.py:57
  127.5 6.8 %copy-start.29 = (bf16[2,256,8,72]{1,0,3,2:T(2,128)(2,1)S(1)}, bf16[2,256,8,72]{1,0,3,2:T(2,128)(2,1)}, u32[]{:S(2)}) copy-start(bf16[2,256,8,72]{1,0,3,2:T(2,128)(2,1)} %reshape.346) | copy-start | bytes 1769476
  132.5 0.8 copy-start.30
  134.4 3.5 copy-start.13
  137.8 1.1 copy-start.7
  138.9 1.2 copy-start.8
  142.4 0.8 copy-start.22
  152.5 2.8 copy-start.23
  152.5 2.9 copy-start.25
  155.4 1.3 copy-start.27
  157.9 1.5 copy-start.3
  159.4 3.8 %copy-start.14 = (bf16[2,256,8,72]{3,2,1,0:T(8,128)(2,1)S(1)}, bf16[2,256,8,72]{3,2,1,0:T(8,128)(2,1)}, u32[]{:S(2)}) copy-start(bf16[2,256,8,72]{3,2,1,0:T(8,128)(2,1)} %copy.88) | copy-start | bytes 1769476
  160.3 13.8 %collective-permute-start.9 = (bf16[256,1152]{1,0:T(8,128)(2,1)}, bf16[256,1152]{1,0:T(8,128)(2,1)}, u32[]{:S(2)}, u32[]{:S(2)}) collective-permute-start(bf16[256,1152]{1,0:T(8,128)(2,1)} %slice.345), channel_id=1, source_target_pairs={{0,16},{16,0},{1,17},{17,1},{2,18},{18,2},{3,19},{19,3},{4,20},{20... | collective-permute-start | bytes 1769480 | tf_op jit(solution)/shard_map/ppermute | solution.py:57
  163.2 1.7 copy-start.15
  164.9 5.9 %copy-start.17 = (bf16[1,512,576]{2,1,0:T(8,128)(2,1)S(1)}, bf16[1,512,576]{2,1,0:T(8,128)(2,1)}, u32[]{:S(2)}) copy-start(bf16[1,512,576]{2,1,0:T(8,128)(2,1)} %reshape.359) | copy-start | bytes 1769476
  166.6 4.2 %copy-start.18 = (bf16[1,512,576]{2,1,0:T(8,128)(2,1)S(1)}, bf16[1,512,576]{2,1,0:T(8,128)(2,1)}, u32[]{:S(2)}) copy-start(bf16[1,512,576]{2,1,0:T(8,128)(2,1)} %reshape.358) | copy-start | bytes 1769476
  168.2 3.9 %copy-start.20 = (bf16[256,1152]{1,0:T(8,128)(2,1)S(1)}, bf16[256,1152]{1,0:T(8,128)(2,1)}, u32[]{:S(2)}) copy-start(bf16[256,1152]{1,0:T(8,128)(2,1)} %copy-done.19) | copy-start | bytes 1769476
  168.2 3.9 %copy-start.31 = (bf16[256,1152]{1,0:T(8,128)(2,1)S(1)}, bf16[256,1152]{1,0:T(8,128)(2,1)}, u32[]{:S(2)}) copy-start(bf16[256,1152]{1,0:T(8,128)(2,1)} %copy-done.30) | copy-start | bytes 1769476
  170.8 1.6 copy-start.10
  172.1 2.0 copy-start.33
  172.5 2.5 copy-start.4
  172.5 3.2 copy-start.5
  174.1 3.2 copy-start.35
  174.1 3.2 copy-start.36
  174.1 3.3 copy-start.37
  174.1 3.3 copy-start.38
  174.1 4.2 %copy-start.9 = (f32[256,1152]{1,0:T(8,128)S(1)}, f32[256,1152]{1,0:T(8,128)}, u32[]{:S(2)}) copy-start(f32[256,1152]{1,0:T(8,128)} %get-tuple-element.39) | copy-start | bytes 3538948
  174.1 4.2 %slice-start = ((f32[512]{0:T(512)}), f32[256]{0:T(256)S(1)}, s32[]{:S(2)}) async-start(f32[512]{0:T(512)} %copy-done.34), calls=%async_computation | async-start | bytes 2048 | tf_op jit(solution)/shard_map/slice | solution.py:497
  177.5 3.8 %collective-permute-start.10 = (f32[6,576]{1,0:T(8,128)S(1)}, f32[6,576]{1,0:T(8,128)S(1)}, u32[]{:S(2)}, u32[]{:S(2)}) collective-permute-start(f32[6,576]{1,0:T(8,128)S(1)} %constant_dynamic-slice_fusion), channel_id=1, source_target_pairs={{0,16},{16,0},{1,17},{17,1},{2,18},{18,2},{3,19},{19,3},{4,20},{20... | collective-permute-start | bytes 41480 | tf_op jit(solution)/shard_map/ppermute | solution.py:57
  178.3 3.2 copy-start.39
  365.4 2.9 copy-start.41
  365.4 2.8 copy-start.40

commit v2 on v1

v2 whole, which is shorter than its diff:
```python
import functools

import jax
import jax.numpy as jnp
from jax import lax
from jax.experimental import pallas as pl
from jax.experimental.pallas import tpu as pltpu
from jax.sharding import PartitionSpec as P

HDIM = 72
norm_eps = 1e-06
MESH = pl.DeviceIdType.MESH
CW = 256
GELU_SCALE = 0.7978845608028654


def norm_stats(values):
    centered = values - jnp.mean(values, axis=-1, keepdims=True)
    variance = jnp.mean(centered * centered, axis=-1, keepdims=True)
    inverse = lax.rsqrt(variance + norm_eps)
    return centered * inverse, inverse


def norm_grad(xhat, inverse, gain, grad):
    scaled = grad * gain
    return (
        scaled
        - jnp.mean(scaled, axis=-1, keepdims=True)
        - xhat * jnp.mean(scaled * xhat, axis=-1, keepdims=True)
    ) * inverse


def gelu_tanh(values):
    return jax.nn.gelu(values, approximate=True)


def product(left_side, right_side):
    return jnp.dot(left_side, right_side, preferred_element_type=jnp.float32)


def product_nt(left_side, right_side):
    return lax.dot_general(
        left_side, right_side, (((1,), (1,)), ((), ())), preferred_element_type=jnp.float32
    )


def product_tn(left_side, right_side):
    return lax.dot_general(
        left_side, right_side, (((0,), (0,)), ((), ())), preferred_element_type=jnp.float32
    )


def column_sums(matrix):
    return jnp.sum(matrix, axis=0, dtype=jnp.float32)


def swap(value):
    return lax.ppermute(value, "shard", [(0, 1), (1, 0)])


def split_heads(matrix, block_rows):
    return matrix.reshape(-1, block_rows, matrix.shape[1] // HDIM, HDIM)


def attend(queries, keys_in, values_in, allowed, block_rows):
    scores = jnp.einsum(
        "bqhd,bkhd->bhqk",
        split_heads(queries, block_rows),
        split_heads(keys_in, block_rows),
        preferred_element_type=jnp.float32,
    ) * HDIM ** (-0.5)
    scores = jnp.where(allowed[:, None, :, :], scores, -1e30)
    highest = jnp.max(scores, axis=-1, keepdims=True)
    scaled_exp = jnp.exp(scores - highest)
    totals = jnp.sum(scaled_exp, axis=-1, keepdims=True)
    probs = scaled_exp / totals
    mixed_out = jnp.einsum(
        "bhqk,bkhd->bqhd",
        probs.astype(jnp.bfloat16),
        split_heads(values_in, block_rows),
        preferred_element_type=jnp.float32,
    )
    return mixed_out.reshape(queries.shape), probs


def attend_back(queries, keys_in, values_in, grad_mixed, probs, block_rows):
    score_scale = HDIM ** (-0.5)
    split_grad = split_heads(grad_mixed, block_rows)
    grad_probs = jnp.einsum(
        "bqhd,bkhd->bhqk",
        split_grad,
        split_heads(values_in, block_rows),
        preferred_element_type=jnp.float32,
    )
    grad_scores = (
        probs * (grad_probs - jnp.sum(probs * grad_probs, axis=-1, keepdims=True))
    ).astype(jnp.bfloat16)
    grad_queries = (
        jnp.einsum(
            "bhqk,bkhd->bqhd",
            grad_scores,
            split_heads(keys_in, block_rows),
            preferred_element_type=jnp.float32,
        )
        * score_scale
    )
    grad_keys = (
        jnp.einsum(
            "bhqk,bqhd->bkhd",
            grad_scores,
            split_heads(queries, block_rows),
            preferred_element_type=jnp.float32,
        )
        * score_scale
    )
    grad_values = jnp.einsum(
        "bhqk,bqhd->bkhd",
        probs.astype(jnp.bfloat16),
        split_grad,
        preferred_element_type=jnp.float32,
    )
    return (
        grad_queries.astype(jnp.bfloat16).reshape(queries.shape),
        grad_keys.astype(jnp.bfloat16).reshape(queries.shape),
        grad_values.astype(jnp.bfloat16).reshape(queries.shape),
    )


def add_low(first, second):
    return (first.astype(jnp.float32) + second.astype(jnp.float32)).astype(jnp.bfloat16)


def by_kernel(replicas, width):
    return replicas == 2**4 and width % (replicas // 2 * 16) == 0


def plain_sums(block_out, tokens_grad, vectors, half, wide, query, key, value, proj, up, down):
    def owned(pair):
        return lax.psum_scatter(product_tn(*pair), "replica", scatter_dimension=0, tiled=True)

    vectors = lax.psum(vectors, "replica")

    def vector_at(i):
        return vectors[i * half : (i + 1) * half]

    return (
        block_out, tokens_grad, vector_at(0), vector_at(1), owned(query), vector_at(6),
        owned(key), owned(value), vector_at(7), owned(proj).T, vector_at(2), vector_at(3),
        vector_at(4), owned(up), vectors[8 * half : 8 * half + wide], owned(down).T, vector_at(5),
    )


def paired(
    tokens, out_grad, picture_ids, live_slots, ln1_gain, ln1_bias, query_weight, query_bias,
    key_weight, value_weight, value_bias, proj_weight, proj_bias, ln2_gain, ln2_bias, up_weight,
    up_bias, down_weight, down_bias,
):
    low = jnp.bfloat16
    full = jnp.float32
    rows, width = tokens.shape
    half = width // 2
    wide = up_weight.shape[1]
    shard = lax.axis_index("shard")
    own_vectors = jnp.stack([ln1_gain, ln1_bias, proj_bias, ln2_gain, ln2_bias, down_bias])
    slots = jnp.stack([picture_ids, live_slots])
    peer_tokens, peer_out, peer_vectors, peer_slots = (
        swap(tokens), swap(out_grad), swap(own_vectors), swap(slots),
    )
    gain_one, shift_one, bias_proj, gain_two, shift_two, bias_down = jnp.where(
        shard == 0,
        jnp.concatenate([own_vectors, peer_vectors], axis=1),
        jnp.concatenate([peer_vectors, own_vectors], axis=1),
    ).astype(full)
    slots = jnp.concatenate([slots, peer_slots], axis=1)
    alive = slots[1].astype(full)[:, None]
    ids = slots[0].reshape(2, rows)
    living = slots[1].reshape(2, rows)
    allowed = (ids[:, :, None] == ids[:, None, :]) & (living[:, None, :] == 1)
    all_tokens = jnp.concatenate([tokens, peer_tokens]).astype(full)
    all_out = jnp.concatenate([out_grad, peer_out]) * alive.astype(low)
    xhat_one, inverse_one = norm_stats(all_tokens)
    normed = (xhat_one * gain_one + shift_one).astype(low)
    queries = (product(normed, query_weight) + query_bias.astype(full)).astype(low)
    keys_all = product(normed, key_weight).astype(low)
    values_all = (product(normed, value_weight) + value_bias.astype(full)).astype(low)
    mixed_out, probs = attend(queries, keys_all, values_all, allowed, rows)
    mixed = mixed_out.astype(low)
    partial = product(mixed, proj_weight)
    hidden = all_tokens[:rows] + partial[:rows] + swap(partial[rows:].astype(low)).astype(full) + bias_proj
    xhat_two, inverse_two = norm_stats(hidden)
    normed_own = (xhat_two * gain_two + shift_two).astype(low)
    normed_two = jnp.concatenate([normed_own, swap(normed_own)])
    up_proj = product(normed_two, up_weight) + up_bias.astype(full)
    activated = gelu_tanh(up_proj).astype(low)
    grad_act = product_nt(all_out, down_weight)
    grad_up = jax.vjp(gelu_tanh, up_proj)[1](grad_act)[0].astype(low)
    partial = product_nt(grad_up, up_weight)
    grad_two = partial[:rows] + swap(partial[rows:].astype(low)).astype(full)
    partial = product(activated, down_weight)
    block_out = (
        (hidden + partial[:rows] + swap(partial[rows:].astype(low)).astype(full) + bias_down)
        * alive[:rows]
    ).astype(low)
    grad_hidden = all_out[:rows].astype(full) + norm_grad(xhat_two, inverse_two, gain_two, grad_two)
    hidden_own = grad_hidden.astype(low)
    hidden_low = jnp.concatenate([hidden_own, swap(hidden_own)])
    grad_mixed = product_nt(hidden_low, proj_weight).astype(low)
    grad_queries, grad_keys, grad_values = attend_back(
        queries, keys_all, values_all, grad_mixed, probs, rows
    )
    partial = (
        product_nt(grad_queries, query_weight)
        + product_nt(grad_keys, key_weight)
        + product_nt(grad_values, value_weight)
    )
    grad_one = partial[:rows] + swap(partial[rows:].astype(low)).astype(full)
    tokens_grad = (
        grad_hidden + norm_grad(xhat_one[:rows], inverse_one[:rows], gain_one, grad_one)
    ).astype(low)
    wholes = jnp.stack(
        [
            column_sums(grad_one * xhat_one[:rows]),
            column_sums(grad_one),
            column_sums(hidden_own),
            column_sums(grad_two * xhat_two),
            column_sums(grad_two),
            column_sums(all_out[:rows]),
        ]
    )
    mine = lax.dynamic_slice_in_dim(wholes, shard * half, half, 1)
    theirs = lax.dynamic_slice_in_dim(wholes, (1 - shard) * half, half, 1)
    halves = mine + swap(theirs)
    vectors = jnp.concatenate(
        [
            halves.reshape(-1),
            column_sums(grad_queries),
            column_sums(grad_values),
            column_sums(grad_up),
        ]
    )
    return plain_sums(
        block_out, tokens_grad, vectors, half, wide,
        (normed, grad_queries), (normed, grad_keys), (normed, grad_values),
        (hidden_low, mixed), (normed_two, grad_up), (all_out, activated),
    )


def take(ref, start, count):
    return ref.at[pl.ds(start, count)]


def layer_kernel(
    tokens,
    out_grad,
    slots,
    vectors,
    up_bias,
    query_hbm,
    key_hbm,
    value_hbm,
    proj_hbm,
    up_hbm,
    down_hbm,
    block_out,
    tokens_grad,
    sums_out,
    vectors_out,
    up_bias_out,
    query_weight,
    key_weight,
    value_weight,
    proj_weight,
    all_tokens,
    out_in,
    all_slots,
    vectors_in,
    queries,
    keys_all,
    values_all,
    probs,
    hidden,
    grad_hidden,
    own_part,
    own_down,
    part_send,
    part_in,
    wide_left,
    wide_right,
    thin_left,
    thin_first,
    thin_second,
    wide_left_in,
    wide_right_in,
    thin_left_in,
    thin_other_in,
    thin_first_in,
    thin_second_in,
    from_y,
    from_low,
    from_high,
    totals,
    halves,
    halves_in,
    vector_sum,
    vector_in,
    up_sum,
    up_in,
    load_sem,
    swap_send,
    swap_recv,
    pair_send,
    pair_recv,
    y_send,
    y_recv,
    low_send,
    low_recv,
    high_send,
    high_recv,
    core_send,
    core_recv,
    keep_sem,
    vec_send,
    vec_recv,
):
    full = jnp.float32
    low = jnp.bfloat16
    chunks = from_y.shape[0]
    rows = from_y.shape[3]
    block, width = tokens.shape
    thin = queries.shape[1]
    wide = up_bias.shape[1]
    heads = thin // HDIM
    score_scale = HDIM ** (-0.5)
    wide_chunks = chunks - 5
    half_block = block // 2
    strip = 32
    shard = lax.axis_index("shard")
    replica = lax.axis_index("replica")
    core = lax.rem(replica, 2)
    other = 1 - core
    y_bit = lax.rem(replica // 2, 2)
    low_bit = lax.rem(replica // 4, 2)
    high_bit = lax.rem(replica // 8, 2)
    twin = (1 - shard, replica)
    partner = (shard, replica + 1 - 2 * core)
    y_peer = (shard, replica + 2 - 4 * y_bit)
    low_peer = (shard, replica + 4 - 8 * low_bit)
    high_peer = (shard, replica + 8 - 16 * high_bit)
    peers = (partner, y_peer, low_peer, high_peer)

    def remote(source, target, send, recv, peer):
        return pltpu.make_async_remote_copy(
            src_ref=source,
            dst_ref=target,
            send_sem=send,
            recv_sem=recv,
            device_id=peer,
            device_id_type=MESH,
        )

    def swapped(index, source, target):
        return remote(source, target, swap_send.at[index], swap_recv.at[index], twin)

    def paired_copy(index, source, target):
        return remote(source, target, pair_send.at[index], pair_recv.at[index], partner)

    loads = [
        pltpu.make_async_copy(source, target, load_sem.at[i])
        for i, (source, target) in enumerate(
            (
                (query_hbm, query_weight),
                (key_hbm, key_weight),
                (value_hbm, value_weight),
                (proj_hbm, proj_weight),
            )
        )
    ]
    for load in loads:
        load.start()

    barrier = pltpu.get_barrier_semaphore()
    for peer in (twin,) + peers:
        pl.semaphore_signal(barrier, inc=1, device_id=peer, device_id_type=MESH)
    pl.semaphore_wait(barrier, 5)

    vectors_swap = swapped(0, vectors, vectors_in)
    slots_swap = swapped(1, slots, all_slots.at[1])
    tokens_swap = swapped(2, tokens, take(all_tokens, block, block))
    out_swap = swapped(3, out_grad, out_in)
    part_swaps = [
        [
            swapped(
                4 + 2 * i + j,
                part_send.at[i, pl.ds(j * half_block, half_block)],
                part_in.at[i, pl.ds(j * half_block, half_block)],
            )
            for j in range(2)
        ]
        for i in range(4)
    ]
    normed_swaps = [
        swapped(
            12 + j,
            wide_left.at[0, pl.ds(j * half_block, half_block)],
            wide_left.at[0, pl.ds(block + j * half_block, half_block)],
        )
        for j in range(2)
    ]
    hidden_swaps = [
        swapped(
            14 + j,
            thin_left.at[1, pl.ds(j * half_block, half_block)],
            thin_left.at[1, pl.ds(block + j * half_block, half_block)],
        )
        for j in range(2)
    ]
    halves_swap = swapped(16, halves.at[1], halves_in)

    def pair_rows(index, source, target, b):
        here = pl.ds(b * block, block)
        return paired_copy(index + b, source.at[here], target.at[here])

    def left_pair(b):
        return pair_rows(0, wide_left.at[other], wide_left_in, b)

    def right_pair(b):
        return pair_rows(2, wide_right.at[other], wide_right_in, b)

    def normed_pair(b):
        return pair_rows(4, thin_left.at[0], thin_left_in, b)

    def other_pair(b):
        return pair_rows(6, thin_left.at[other], thin_other_in, b)

    def first_pair(b):
        return pair_rows(8, thin_first.at[other], thin_first_in, b)

    def second_pair(b):
        return pair_rows(10, thin_second.at[other], thin_second_in, b)

    vectors_swap.start()
    slots_swap.start()
    tokens_swap.start()
    out_swap.start()

    all_slots[0] = slots[...]
    take(all_tokens, 0, block)[...] = tokens[...]
    totals[...] = jnp.zeros_like(totals)
    up_sum[0] = jnp.zeros(up_sum.shape[1:], full)

    vectors_swap.wait_recv()
    slots_swap.wait_recv()
    here_half = vectors[...]
    there_half = vectors_in[...]
    joined = jnp.where(
        shard == 0,
        jnp.concatenate([here_half, there_half], axis=1),
        jnp.concatenate([there_half, here_half], axis=1),
    )
    gain_one, shift_one, bias_proj = joined[0:1], joined[1:2], joined[2:3]
    gain_two, shift_two, bias_down = joined[3:4], joined[4:5], joined[5:6]
    bias_query, bias_value = here_half[6:7], here_half[7:8]

    def strips(count, first, body):
        def step(i, carry):
            body(pl.ds(pl.multiple_of(first + i * strip, strip), strip))
            return carry

        lax.fori_loop(0, count // strip, step, 0, unroll=2)

    def mlp_scope(up_weight, down_weight, grad_act, wide_sem):
        wide_loads = [
            pltpu.make_async_copy(up_hbm, up_weight, wide_sem.at[0]),
            pltpu.make_async_copy(down_hbm, down_weight, wide_sem.at[1]),
        ]
        for load in wide_loads:
            load.start()

        def attend_step(b, carry):
            here = pl.ds(pl.multiple_of(b * block, block), block)

            @pl.when(b == 1)
            def _():
                tokens_swap.wait_recv()

            def norm_strip(at):
                xhat, _ = norm_stats(all_tokens[at, :].astype(full))
                thin_left[0, at, :] = (xhat * gain_one + shift_one).astype(low)

            strips(block, b * block, norm_strip)

            @pl.when(b == 0)
            def _():
                for load in loads:
                    load.wait()

            normed = thin_left[0, here, :]
            queries[here, :] = (product(normed, query_weight[...]) + bias_query).astype(low)
            keys_all[here, :] = product(normed, key_weight[...]).astype(low)
            values_all[here, :] = (product(normed, value_weight[...]) + bias_value).astype(low)
            marks = all_slots[b]
            across = jnp.where(marks[1:2] == 1.0, marks[0:1], -1.0)
            down_ids = jnp.transpose(marks)[:, 0:1]
            allowed = down_ids == across
            q_all = queries[here, :]
            k_all = keys_all[here, :]
            v_all = values_all[here, :]
            for h in range(heads):
                cut = slice(h * HDIM, (h + 1) * HDIM)
                scores = product_nt(q_all[:, cut], k_all[:, cut]) * score_scale
                scores = jnp.where(allowed, scores, -1e30)
                scaled = jnp.exp(scores - jnp.max(scores, axis=-1, keepdims=True))
                share = 1.0 / jnp.sum(scaled, axis=-1, keepdims=True)
                probs_low = (scaled * share).astype(low)
                probs[b * heads + h] = probs_low
                thin_second[1, here, cut] = product(probs_low, v_all[:, cut]).astype(low)
            mixed = thin_second[1, here, :]

            def proj_tile(n, inner):
                at = pl.ds(pl.multiple_of(n * 384, 384), 384)
                value = product(mixed, proj_weight[:, at])

                @pl.when(b == 0)
                def _():
                    own_part[:, at] = value

                @pl.when(b == 1)
                def _():
                    part_send[0, :, at] = value.astype(low)

                return inner

            lax.fori_loop(0, width // 384, proj_tile, 0)
            return carry

        lax.fori_loop(0, 2, attend_step, 0)
        for copy in part_swaps[0]:
            copy.start()
        for b in range(2):
            normed_pair(b).start()

        out_swap.wait_recv()
        for b, source in enumerate((out_grad, out_in)):
            alive = jnp.transpose(all_slots[b])[:, 1:2].astype(low)
            wide_left[1, pl.ds(b * block, block), :] = source[...] * alive
        wide_loads[1].wait()
        out_rows = wide_left[1]

        def act_tile(t, carry):
            at = pl.ds(pl.multiple_of(t * 512, 512), 512)
            grad_act[:, at] = product_nt(out_rows, down_weight[at, :]).astype(low)
            return carry

        lax.fori_loop(0, wide_chunks // 2, act_tile, 0)
        rest_from = wide_chunks * CW
        rest = wide - rest_from
        rest_at = pl.ds(rest_from, rest)
        grad_act[:, rest_at] = product_nt(out_rows, down_weight[rest_at, :]).astype(low)
        wide_loads[0].wait()
        pad_at = pl.ds(rest_from, CW // 2)
        wide_right[0, :, pad_at] = jnp.zeros((2 * block, CW // 2), low)
        wide_right[1, :, pad_at] = jnp.zeros((2 * block, CW // 2), low)

        for j in range(2):
            part_swaps[0][j].wait_recv()

            def hidden_strip(at):
                value = (
                    tokens[at, :].astype(full)
                    + own_part[at, :]
                    + part_in[0, at, :].astype(full)
                    + bias_proj
                )
                hidden[at, :] = value
                xhat, _ = norm_stats(value)
                wide_left[0, at, :] = (xhat * gain_two + shift_two).astype(low)

            strips(half_block, j * half_block, hidden_strip)
            normed_swaps[j].start()

        def mlp_step(b, carry):
            here = pl.ds(pl.multiple_of(b * block, block), block)

            @pl.when(b == 1)
            def _():
                for copy in normed_swaps:
                    copy.wait_recv()

            normed = wide_left[0, here, :]

            def gelu_tile(at):
                value = product(normed, up_weight[:, at]) + up_bias[:, at]
                square = value * value
                bent = jnp.tanh(GELU_SCALE * value * (1.0 + 0.044715 * square))
                bulge = 0.5 * (1.0 + bent)
                wide_right[1, here, at] = (value * bulge).astype(low)
                slope = bulge + 0.5 * value * (1.0 - bent * bent) * (
                    GELU_SCALE * (1.0 + 0.134145 * square)
                )
                grad = (slope * grad_act[here, at].astype(full)).astype(low)
                wide_right[0, here, at] = grad
                up_sum[0, :, at] += jnp.sum(grad.astype(full), axis=0, keepdims=True)

            def up_tile(t, inner):
                gelu_tile(pl.ds(pl.multiple_of(t * CW, CW), CW))
                return inner

            lax.fori_loop(0, wide_chunks, up_tile, 0)
            gelu_tile(rest_at)

            @pl.when(b == 0)
            def _():
                right_pair(0).start()

            @pl.when(b == 1)
            def _():
                left_pair(0).start()
                left_pair(1).start()
                right_pair(1).start()

            grad_rows = wide_right[0, here, pl.ds(0, wide)]

            def back_tile(n, inner):
                at = pl.ds(pl.multiple_of(n * 384, 384), 384)
                value = product_nt(grad_rows, up_weight[at, :])

                @pl.when(b == 0)
                def _():
                    own_part[:, at] = value

                @pl.when(b == 1)
                def _():
                    part_send[1, :, at] = value.astype(low)

                return inner

            lax.fori_loop(0, width // 384, back_tile, 0)

            @pl.when(b == 1)
            def _():
                for copy in part_swaps[1]:
                    copy.start()

            act_rows = wide_right[1, here, pl.ds(0, wide)]

            def down_tile(n, inner):
                at = pl.ds(pl.multiple_of(n * 384, 384), 384)
                value = product(act_rows, down_weight[:, at])

                @pl.when(b == 0)
                def _():
                    own_down[:, at] = value

                @pl.when(b == 1)
                def _():
                    part_send[2, :, at] = value.astype(low)

                return inner

            lax.fori_loop(0, width // 384, down_tile, 0)
            return carry

        lax.fori_loop(0, 2, mlp_step, 0)
        for copy in part_swaps[2]:
            copy.start()

    pl.run_scoped(
        mlp_scope,
        pltpu.VMEM(up_hbm.shape, low),
        pltpu.VMEM(down_hbm.shape, low),
        pltpu.VMEM((2 * block, wide_right.shape[2]), low),
        pltpu.SemaphoreType.DMA((2,)),
    )

    def grad_scope(grads, summed):
        def y_copy(j):
            return remote(
                grads.at[j, :, :, 1 - y_bit], from_y.at[j], y_send.at[j], y_recv.at[j], y_peer
            )

        def low_copy(j):
            return remote(
                grads.at[j, :, 1 - low_bit, y_bit],
                from_low.at[j],
                low_send.at[j],
                low_recv.at[j],
                low_peer,
            )

        def high_copy(j):
            return remote(
                grads.at[j, 1 - high_bit, low_bit, y_bit],
                from_high.at[j],
                high_send.at[j],
                high_recv.at[j],
                high_peer,
            )

        def core_copy(j):
            return remote(
                summed.at[j, other],
                sums_out.at[core, j],
                core_send.at[j],
                core_recv.at[j],
                partner,
            )

        def core_arrival(j):
            return remote(
                summed.at[j, other],
                sums_out.at[other, j],
                core_send.at[j],
                core_recv.at[j],
                partner,
            )

        def keep_copy(j):
            return pltpu.make_async_copy(summed.at[j, core], sums_out.at[core, j], keep_sem.at[j])

        def emit(j, value):
            grads[j] = value.astype(low).reshape(grads.shape[1:])
            y_copy(j).start()

        def pump(i):
            @pl.when(i < chunks)
            def _():
                y_copy(i).wait_recv()
                grads[i, :, :, y_bit] = add_low(grads[i, :, :, y_bit], from_y[i])
                low_copy(i).start()

            @pl.when(jnp.logical_and(i >= 1, i < chunks + 1))
            def _():
                j = i - 1
                low_copy(j).wait_recv()
                grads[j, :, low_bit, y_bit] = add_low(grads[j, :, low_bit, y_bit], from_low[j])
                high_copy(j).start()

            @pl.when(jnp.logical_and(i >= 2, i < chunks + 2))
            def _():
                j = i - 2
                high_copy(j).wait_recv()
                total = grads[j, high_bit, low_bit, y_bit].astype(full) + from_high[j].astype(full)
                summed[j] = total.reshape(2, rows // 2, CW)
                core_copy(j).start()
                keep_copy(j).start()

            @pl.when(i >= 3)
            def _():
                core_arrival(i - 3).wait_recv()
                keep_copy(i - 3).wait()

        def pump_step(i, carry):
            pump(i)
            return carry

        for b in range(2):
            left_pair(b).wait_recv()
            right_pair(b).wait_recv()

        def wide_step(j, carry):
            columns = pl.ds(pl.multiple_of(j * CW, CW), CW)
            emit(
                j,
                product_tn(wide_left[core], wide_right[core, :, columns])
                + product_tn(wide_left_in[...], wide_right_in[:, columns]),
            )
            return carry

        lax.fori_loop(0, wide_chunks, wide_step, 0)

        for j in range(2):
            part_swaps[1][j].wait_recv()

            def norm_back_strip(at):
                grad = own_part[at, :] + part_in[1, at, :].astype(full)
                xhat, inverse = norm_stats(hidden[at, :])
                out_rows = wide_left[1, at, :].astype(full)
                value = out_rows + norm_grad(xhat, inverse, gain_two, grad)
                grad_hidden[at, :] = value
                rounded = value.astype(low)
                thin_left[1, at, :] = rounded
                totals[2:3] += column_sums(rounded.astype(full))[None]
                totals[3:4] += column_sums(grad * xhat)[None]
                totals[4:5] += column_sums(grad)[None]
                totals[5:6] += column_sums(out_rows)[None]

            strips(half_block, j * half_block, norm_back_strip)
            hidden_swaps[j].start()

        def back_step(b, carry):
            here = pl.ds(pl.multiple_of(b * block, block), block)

            @pl.when(b == 1)
            def _():
                for copy in hidden_swaps:
                    copy.wait_recv()
                for i in range(2):
                    other_pair(i).start()

            grad_mixed = product_nt(thin_left[1, here, :], proj_weight[...]).astype(low)
            q_all = queries[here, :]
            k_all = keys_all[here, :]
            v_all = values_all[here, :]
            for h in range(heads):
                cut = slice(h * HDIM, (h + 1) * HDIM)
                probs_low = probs[b * heads + h]
                probs_full = probs_low.astype(full)
                mixed_grad = grad_mixed[:, cut]
                grad_probs = product_nt(mixed_grad, v_all[:, cut])
                weighted = probs_full * grad_probs
                grad_scores = (
                    weighted - probs_full * jnp.sum(weighted, axis=-1, keepdims=True)
                ).astype(low)
                thin_first[0, here, cut] = (product(grad_scores, k_all[:, cut]) * score_scale).astype(low)
                thin_second[0, here, cut] = (
                    product_tn(grad_scores, q_all[:, cut]) * score_scale
                ).astype(low)
                thin_first[1, here, cut] = product_tn(probs_low, mixed_grad).astype(low)

            @pl.when(b == 0)
            def _():
                first_pair(0).start()
                second_pair(0).start()

            @pl.when(b == 1)
            def _():
                first_pair(1).start()
                second_pair(1).start()

            grad_q = thin_first[0, here, :]
            grad_k = thin_second[0, here, :]
            grad_v = thin_first[1, here, :]

            def normed_tile(n, inner):
                at = pl.ds(pl.multiple_of(n * 384, 384), 384)
                value = (
                    product_nt(grad_q, query_weight[at, :])
                    + product_nt(grad_k, key_weight[at, :])
                    + product_nt(grad_v, value_weight[at, :])
                )

                @pl.when(b == 0)
                def _():
                    own_part[:, at] = value

                @pl.when(b == 1)
                def _():
                    part_send[3, :, at] = value.astype(low)

                return inner

            lax.fori_loop(0, width // 384, normed_tile, 0)
            lax.fori_loop(2 * b, 2 * b + 2, pump_step, 0)
            return carry

        lax.fori_loop(0, 2, back_step, 0)
        for copy in part_swaps[3]:
            copy.start()

        for b in range(2):
            for pair in (normed_pair, other_pair, first_pair, second_pair):
                pair(b).wait_recv()

        def first_part(columns):
            return product_tn(thin_left[0], thin_first[core, :, columns]) + product_tn(
                thin_left_in[...], thin_first_in[:, columns]
            )

        def second_part(columns):
            return product_tn(thin_left[core], thin_second[core, :, columns]) + product_tn(
                thin_other_in[...], thin_second_in[:, columns]
            )

        def thin_step(j, carry):
            columns = pl.ds(pl.multiple_of(j * CW, CW), CW)
            emit(wide_chunks + j, first_part(columns))
            emit(wide_chunks + 2 + j, second_part(columns))
            return carry

        lax.fori_loop(0, 2, thin_step, 0)
        thin_rest = pl.ds(2 * CW, thin - 2 * CW)
        wide_rest = pl.ds(wide_chunks * CW, CW // 2)
        emit(
            chunks - 1,
            jnp.concatenate(
                [
                    product_tn(wide_left[core], wide_right[core, :, wide_rest])
                    + product_tn(wide_left_in[...], wide_right_in[:, wide_rest]),
                    first_part(thin_rest),
                    second_part(thin_rest),
                ],
                axis=1,
            ),
        )

        for copy in part_swaps[2]:
            copy.wait_recv()

        def out_strip(at):
            alive = jnp.transpose(all_slots[0])
            value = hidden[at, :] + own_down[at, :] + part_in[2, at, :].astype(full) + bias_down
            block_out[at, :] = value.astype(low)

        strips(block, 0, out_strip)
        alive = jnp.transpose(all_slots[0])[:, 1:2].astype(low)
        block_out[...] = block_out[...] * alive

        for copy in part_swaps[3]:
            copy.wait_recv()

        def final_strip(at):
            grad = own_part[at, :] + part_in[3, at, :].astype(full)
            xhat, inverse = norm_stats(tokens[at, :].astype(full))
            tokens_grad[at, :] = (
                grad_hidden[at, :] + norm_grad(xhat, inverse, gain_one, grad)
            ).astype(low)
            totals[0:1] += column_sums(grad * xhat)[None]
            totals[1:2] += column_sums(grad)[None]

        strips(block, 0, final_strip)
        sums = totals[...]
        lower = sums[:, :thin]
        upper = sums[:, thin:]
        halves[0] = jnp.where(shard == 0, lower, upper)
        halves[1] = jnp.where(shard == 0, upper, lower)
        halves_swap.start()
        grad_query_bias = column_sums(thin_first[0].astype(full))[None]
        grad_value_bias = column_sums(thin_first[1].astype(full))[None]
        halves_swap.wait_recv()
        vector_sum[0] = halves[0] + halves_in[...]
        vector_sum[0, 6:7] = grad_query_bias
        vector_sum[0, 7:8] = grad_value_bias

        def vector_copies(i):
            return (
                remote(
                    vector_sum.at[i], vector_in.at[i], vec_send.at[2 * i], vec_recv.at[2 * i], peers[i]
                ),
                remote(
                    up_sum.at[i], up_in.at[i], vec_send.at[2 * i + 1], vec_recv.at[2 * i + 1], peers[i]
                ),
            )

        def vector_start(i):
            for copy in vector_copies(i):
                copy.start()

        def vector_finish(i):
            for copy in vector_copies(i):
                copy.wait_recv()
            vector_sum[i + 1] = vector_sum[i] + vector_in[i]
            up_sum[i + 1] = up_sum[i] + up_in[i]

        vector_start(0)
        vector_finish(0)
        vector_start(1)

        lax.fori_loop(4, chunks, pump_step, 0)
        vector_finish(1)
        vector_start(2)
        pump(chunks)
        vector_finish(2)
        vector_start(3)
        pump(chunks + 1)
        pump(chunks + 2)
        vector_finish(3)
        vectors_out[...] = vector_sum[4]
        up_bias_out[...] = up_sum[4]

        def drain(j, carry):
            y_copy(j).wait_send()
            low_copy(j).wait_send()
            high_copy(j).wait_send()
            core_copy(j).wait_send()
            return carry

        lax.fori_loop(0, chunks, drain, 0)
        for i in range(4):
            for copy in vector_copies(i):
                copy.wait_send()

    pl.run_scoped(
        grad_scope,
        pltpu.VMEM((chunks, 2, 2, 2, rows, CW), low),
        pltpu.VMEM((chunks, 2, rows // 2, CW), full),
    )
    for copy in [vectors_swap, slots_swap, tokens_swap, out_swap, halves_swap]:
        copy.wait_send()
    for copies in part_swaps + [normed_swaps, hidden_swaps]:
        for copy in copies:
            copy.wait_send()
    for b in range(2):
        for pair in (left_pair, right_pair, normed_pair, other_pair, first_pair, second_pair):
            pair(b).wait_send()


def layer_call(
    tokens, out_grad, slots, vectors, up_bias, query_weight, key_weight, value_weight, proj_weight,
    up_weight, down_weight,
):
    low = jnp.bfloat16
    full = jnp.float32
    block, width = tokens.shape
    thin = query_weight.shape[1]
    wide = up_weight.shape[1]
    wide_pad = wide + -wide % 128
    heads = thin // HDIM
    replicas = lax.axis_size("replica")
    rows = width // replicas * 2
    chunks = wide // CW + 5
    half = rows // 2
    both = 2 * block
    vmem = pl.BlockSpec(memory_space=pltpu.VMEM)
    anywhere = pl.BlockSpec(memory_space=pl.ANY)
    dma = pltpu.SemaphoreType.DMA
    return pl.pallas_call(
        layer_kernel,
        out_shape=(
            jax.ShapeDtypeStruct(tokens.shape, low),
            jax.ShapeDtypeStruct(tokens.shape, low),
            jax.ShapeDtypeStruct((2, chunks, half, CW), full),
            jax.ShapeDtypeStruct(vectors.shape, full),
            jax.ShapeDtypeStruct((1, wide_pad), full),
        ),
        in_specs=[vmem] * 5 + [anywhere] * 6,
        out_specs=(vmem, vmem, anywhere, vmem, vmem),
        scratch_shapes=[
            pltpu.VMEM((width, thin), low),
            pltpu.VMEM((width, thin), low),
            pltpu.VMEM((width, thin), low),
            pltpu.VMEM((thin, width), low),
            pltpu.VMEM((both, width), low),
            pltpu.VMEM((block, width), low),
            pltpu.VMEM((2,) + slots.shape, full),
            pltpu.VMEM(vectors.shape, full),
            pltpu.VMEM((both, thin), low),
            pltpu.VMEM((both, thin), low),
            pltpu.VMEM((both, thin), low),
            pltpu.VMEM((2 * heads, block, block), low),
            pltpu.VMEM((block, width), full),
            pltpu.VMEM((block, width), full),
            pltpu.VMEM((block, width), full),
            pltpu.VMEM((block, width), full),
            pltpu.VMEM((4, block, width), low),
            pltpu.VMEM((4, block, width), low),
            pltpu.VMEM((2, both, width), low),
            pltpu.VMEM((2, both, wide_pad), low),
            pltpu.VMEM((2, both, width), low),
            pltpu.VMEM((2, both, thin), low),
            pltpu.VMEM((2, both, thin), low),
            pltpu.VMEM((both, width), low),
            pltpu.VMEM((both, wide_pad), low),
            pltpu.VMEM((both, width), low),
            pltpu.VMEM((both, width), low),
            pltpu.VMEM((both, thin), low),
            pltpu.VMEM((both, thin), low),
            pltpu.VMEM((chunks, 2, 2, rows, CW), low),
            pltpu.VMEM((chunks, 2, rows, CW), low),
            pltpu.VMEM((chunks, rows, CW), low),
            pltpu.VMEM((8, width), full),
            pltpu.VMEM((2, 8, thin), full),
            pltpu.VMEM((8, thin), full),
            pltpu.VMEM((5, 8, thin), full),
            pltpu.VMEM((4, 8, thin), full),
            pltpu.VMEM((5, 1, wide_pad), full),
            pltpu.VMEM((4, 1, wide_pad), full),
            dma((4,)),
            dma((17,)),
            dma((17,)),
            dma((12,)),
            dma((12,)),
            dma((chunks,)),
            dma((chunks,)),
            dma((chunks,)),
            dma((chunks,)),
            dma((chunks,)),
            dma((chunks,)),
            dma((chunks,)),
            dma((chunks,)),
            dma((chunks,)),
            dma((8,)),
            dma((8,)),
        ],
        compiler_params=pltpu.CompilerParams(
            collective_id=0, has_side_effects=True, vmem_limit_bytes=67043328
        ),
        name="layer",
    )(
        tokens, out_grad, slots, vectors, up_bias, query_weight, key_weight, value_weight,
        proj_weight, up_weight, down_weight,
    )


def whole_layer(
    tokens, out_grad, picture_ids, live_slots, ln1_gain, ln1_bias, query_weight, query_bias,
    key_weight, value_weight, value_bias, proj_weight, proj_bias, ln2_gain, ln2_bias, up_weight,
    up_bias, down_weight, down_bias,
):
    full = jnp.float32
    width = tokens.shape[1]
    if not by_kernel(lax.axis_size("replica"), width):
        return paired(
            tokens, out_grad, picture_ids, live_slots, ln1_gain, ln1_bias, query_weight,
            query_bias, key_weight, value_weight, value_bias, proj_weight, proj_bias, ln2_gain,
            ln2_bias, up_weight, up_bias, down_weight, down_bias,
        )
    half = width // 2
    wide = up_weight.shape[1]
    vectors = jnp.stack(
        [ln1_gain, ln1_bias, proj_bias, ln2_gain, ln2_bias, down_bias, query_bias, value_bias]
    ).astype(full)
    slots = jnp.stack([picture_ids, live_slots] + [live_slots] * 6).astype(full)
    block_out, tokens_grad, sums, vectors, up_bias_grad = layer_call(
        tokens, out_grad, slots, vectors, up_bias.astype(full)[None], query_weight, key_weight,
        value_weight, proj_weight, up_weight, down_weight,
    )
    chunks = sums.shape[1]
    wide_chunks = chunks - 5

    def columns(slot, first, count):
        return [sums[slot, first + i] for i in range(count)]

    rest = [sums[0, chunks - 1], sums[1, chunks - 1]]
    thin_rest = half - 2 * CW
    wide_rest = wide - wide_chunks * CW

    def wide_of(slot):
        return jnp.concatenate(columns(slot, 0, wide_chunks) + [rest[slot][:, :wide_rest]], axis=1)

    def thin_of(slot, place):
        start = CW // 2 + place * thin_rest
        return jnp.concatenate(
            columns(slot, wide_chunks + 2 * place, 2) + [rest[slot][:, start : start + thin_rest]],
            axis=1,
        )

    return (
        block_out,
        tokens_grad,
        vectors[0],
        vectors[1],
        thin_of(0, 0),
        vectors[6],
        thin_of(0, 1),
        thin_of(1, 0),
        vectors[7],
        thin_of(1, 1).T,
        vectors[2],
        vectors[3],
        vectors[4],
        wide_of(0),
        up_bias_grad[0, :wide],
        wide_of(1).T,
        vectors[5],
    )


def solution(mesh):
    in_specs = (
        P(("shard", "replica"), None),
        P(("shard", "replica"), None),
        P(("shard", "replica")),
        P(("shard", "replica")),
        P("shard"),
        P("shard"),
        P(None, "shard"),
        P("shard"),
        P(None, "shard"),
        P(None, "shard"),
        P("shard"),
        P("shard", None),
        P("shard"),
        P("shard"),
        P("shard"),
        P(None, "shard"),
        P("shard"),
        P("shard", None),
        P("shard"),
    )
    out_specs = (
        P(("shard", "replica"), None),
        P(("shard", "replica"), None),
        P("shard"),
        P("shard"),
        P("replica", "shard"),
        P("shard"),
        P("replica", "shard"),
        P("replica", "shard"),
        P("shard"),
        P("shard", "replica"),
        P("shard"),
        P("shard"),
        P("shard"),
        P("replica", "shard"),
        P("shard"),
        P("shard", "replica"),
        P("shard"),
    )
    return jax.shard_map(whole_layer, mesh=mesh, in_specs=in_specs, out_specs=out_specs, check_vma=False)
```

time: 373 us -> 220 us (0.59)
  matrix products: 44.2 us -> 0 us
  waiting for transfers between devices: 41.3 us -> 0 us
  other arithmetic: 41.4 us -> 2.76 us
  local copies, waits for them, and re-layouts: 55.3 us -> 28.8 us
  Pallas kernels: 172 us -> 186 us
  starting transfers between devices: 13.2 us -> 0 us
    dot_general x18 -> x0, matrix products: 44.2 us -> none  [the longest x6 19.2 us: product(): return jnp.dot(left_side, right_side, preferred_element_type=jnp.float32)]
    ppermute x11 -> x0, waiting for transfers between devices: 41.3 us -> none  [swap(): return lax.ppermute(value, 'shard', [(0, 1), (1, 0)])]
    pallas_call x1, Pallas kernels: 172 us -> 186 us  [layer_call(): pl.pallas_call(layer_kernel, out_shape=(jax.ShapeDtypeStruct(tokens.shape...]
    ppermute x11 -> x0, starting transfers between devices: 13.2 us -> none  [swap(): return lax.ppermute(value, 'shard', [(0, 1), (1, 0)])]
    another operation x8 -> x0, other arithmetic: 11.7 us -> none  [the longest x2 3.04 us: paired(): jnp.stack([normed_two, all_out])]
    another operation x21 -> x10, local copies, waits for them, and re-layouts: 16.4 us -> 6.59 us  [the longest x9 5.63 us: whole_layer(): jnp.stack([ln1_gain, ln1_bias, proj_bias, ln2_gain, ln2_bias, down_bias,...]
    convert_element_type x6 -> x0, local copies, waits for them, and re-layouts: 9.29 us -> none  [the longest x3 5.84 us: paired(): mixed = mixed_out.astype(low)]
    mul x3 -> x0, other arithmetic: 7.85 us -> none  [the longest x2 4.84 us: paired(): all_out = jnp.concatenate([out_grad, peer_out]) * alive.astype(low)]
  transfers between devices with their start and end apart: 11 -> 0, of which waited for: 6 -> 0; matrix products, arithmetic and copies ran while one was open for 18% -> 0% of each run, Pallas kernels for 0% -> 0%
where the time goes in v2:
time: 220 us; the launch traced here: 219 us
  Pallas kernels  186 us (85%)
  local copies, waits for them, and re-layouts  28.8 us (13%)
  other arithmetic  2.76 us (1%)
    pallas_call x1, Pallas kernels, layer_call(): pl.pallas_call(layer_kernel, out_shape=(jax.ShapeDtypeStruct(tokens.shape...  186 us
    unnamed x28, local copies, waits for them, and re-layouts  16.1 us
    another operation x9, local copies, waits for them, and re-layouts, whole_layer(): jnp.stack([ln1_gain, ln1_bias, proj_bias, ln2_gain, ln2_bias, down_bias,...  5.63 us

profile of v2, /device:TPU:0, one launch (start us, length us, event | category | flops | bytes accessed | tf_op | source)
XLA Modules:
  0.0 218.7 jit_solution(11961441072070897204)
XLA Ops:
  0.7 0.0 copy-start.1
  0.7 0.8 stack.45
  1.5 0.7 stack.46
  2.1 0.7 stack.51
  2.8 0.7 stack.52
  3.5 0.7 stack.47
  4.2 0.7 stack.48
  4.9 0.7 stack.49
  5.6 0.7 stack.50
  6.3 1.0 stack.44
  7.3 0.6 convert_element_type.7.slots
  7.9 1.3 reshape.34.up_bias
  9.2 0.6 convert_element_type.8.vectors
  9.8 2.6 %copy.36.query_hbm = bf16[1152,576]{1,0:T(8,128)(2,1)} copy(bf16[1152,576]{0,1:T(8,128)(2,1)} %param.25) | data formatting | bytes 2654208 | tf_op args[6]
  12.4 0.0 copy-done.1
  12.4 0.0 copy-start.2
  12.4 1.7 copy.37.key_hbm
  14.1 0.0 copy-done.2
  14.1 1.6 copy.38.value_hbm
  15.7 8.4 %copy.39.up_hbm = bf16[1152,2152]{1,0:T(8,128)(2,1)} copy(bf16[1152,2152]{0,1:T(8,128)(2,1)} %param.34) | data formatting | bytes 9916416 | tf_op args[15]
  24.1 186.4 %layer.1 = (bf16[256,1152]{1,0:T(8,128)(2,1)}, bf16[256,1152]{1,0:T(8,128)(2,1)}, f32[2,13,72,256]{3,2,1,0:T(8,128)}, f32[8,576]{1,0:T(8,128)}, f32[1,2176]{1,0:T(1,128)}) custom-call(bf16[256,1152]{1,0:T(8,128)(2,1)} %tokens.1, bf16[256,1152]{1,0:T(8,128)(2,1)} %out_grad.1, f32[8,256]{1,0:T(8,128)} %convert_element_type.7.slots, ...), custom_call_target="tpu_custom_call" | custom-call | tf_op jit(solution)/shard_map/layer/pallas_call | solution.py:1016
  210.5 0.0 copy-start
  210.5 1.5 slice_reduce_fusion
  212.0 1.9 slice_reduce_fusion.1
  213.9 1.2 slice_bitcast_fusion.1
  215.1 0.1 fusion
  215.2 0.0 copy-start.4
  215.2 0.8 pad_maximum_fusion.2
  216.0 0.1 fusion.1
  216.1 0.8 pad_maximum_fusion
  216.8 0.0 copy-start.3
  216.8 0.0 copy-done
  217.0 0.0 copy-start.5
  217.0 0.0 copy-start.6
  217.0 0.0 copy-done.4
  217.0 0.9 copy.58
  217.9 0.0 copy-done.3
  217.9 0.8 copy.59
  218.7 0.0 copy-done.5
  218.7 0.0 copy-done.6
  (10 shorter events, 0.2 us)
Async XLA Ops:
  0.7 11.7 %copy-start.1 = (bf16[1152,576]{0,1:T(8,128)(2,1)S(1)}, bf16[1152,576]{0,1:T(8,128)(2,1)}, u32[]{:S(2)}) copy-start(bf16[1152,576]{0,1:T(8,128)(2,1)} %param.27) | copy-start | bytes 3981316
  12.4 1.7 copy-start.2
  210.5 6.3 %copy-start = (f32[2,13,72,256]{3,2,1,0:T(8,128)S(1)}, f32[2,13,72,256]{3,2,1,0:T(8,128)}, u32[]{:S(2)}) copy-start(f32[2,13,72,256]{3,2,1,0:T(8,128)} %get-tuple-element.25) | copy-start | bytes 5750788
  215.2 1.8 copy-start.4
  216.8 1.1 copy-start.3
  217.0 1.7 copy-start.5
  217.0 1.7 copy-start.6

commit v3 on v2

--- a/solution.py
+++ b/solution.py
@@ -11,6 +11,8 @@
 norm_eps = 1e-06
 MESH = pl.DeviceIdType.MESH
 CW = 256
+EARLY = 2
+AHEAD = 3
 GELU_SCALE = 0.7978845608028654
 
 
@@ -250,28 +252,38 @@
 
 
 def layer_kernel(
-    tokens,
-    out_grad,
-    slots,
-    vectors,
-    up_bias,
+    tokens_hbm,
+    out_hbm,
+    picture_ids,
+    live_slots,
+    ln1_gain,
+    ln1_bias,
+    proj_bias,
+    ln2_gain,
+    ln2_bias,
+    down_bias,
+    query_bias,
+    value_bias,
+    up_bias_in,
     query_hbm,
     key_hbm,
     value_hbm,
     proj_hbm,
     up_hbm,
     down_hbm,
-    block_out,
-    tokens_grad,
-    sums_out,
+    rows_out,
+    wide_out,
+    thin_out,
     vectors_out,
     up_bias_out,
+    slots,
+    vectors,
+    up_bias,
     query_weight,
     key_weight,
     value_weight,
     proj_weight,
     all_tokens,
-    out_in,
     all_slots,
     vectors_in,
     queries,
@@ -295,9 +307,11 @@
     thin_other_in,
     thin_first_in,
     thin_second_in,
-    from_y,
-    from_low,
+    early,
+    from_first,
+    from_second,
     from_high,
+    rest_in,
     totals,
     halves,
     halves_in,
@@ -305,28 +319,40 @@
     vector_in,
     up_sum,
     up_in,
+    flat_0,
+    flat_1,
+    flat_2,
+    flat_3,
+    flat_4,
+    flat_5,
+    flat_6,
+    flat_7,
+    flat_slots_0,
+    flat_slots_1,
+    flat_up,
+    small_sem,
     load_sem,
     swap_send,
     swap_recv,
     pair_send,
     pair_recv,
-    y_send,
-    y_recv,
-    low_send,
-    low_recv,
+    first_send,
+    first_recv,
+    second_send,
+    second_recv,
     high_send,
     high_recv,
     core_send,
     core_recv,
-    keep_sem,
     vec_send,
     vec_recv,
 ):
     full = jnp.float32
     low = jnp.bfloat16
-    chunks = from_y.shape[0]
-    rows = from_y.shape[3]
-    block, width = tokens.shape
+    chunks = from_first.shape[0]
+    rows = from_first.shape[3]
+    early_chunks = early.shape[0]
+    block, width = tokens_hbm.shape
     thin = queries.shape[1]
     wide = up_bias.shape[1]
     heads = thin // HDIM
@@ -372,21 +398,49 @@
                 (key_hbm, key_weight),
                 (value_hbm, value_weight),
                 (proj_hbm, proj_weight),
+                (tokens_hbm, take(all_tokens, 0, block)),
+                (out_hbm, wide_left.at[1, pl.ds(0, block)]),
             )
         )
     ]
-    for load in loads:
-        load.start()
-
     barrier = pltpu.get_barrier_semaphore()
     for peer in (twin,) + peers:
         pl.semaphore_signal(barrier, inc=1, device_id=peer, device_id_type=MESH)
+    small = [
+        pltpu.make_async_copy(source, target, small_sem.at[i])
+        for i, (source, target) in enumerate(
+            (
+                (ln1_gain, flat_0),
+                (ln1_bias, flat_1),
+                (proj_bias, flat_2),
+                (ln2_gain, flat_3),
+                (ln2_bias, flat_4),
+                (down_bias, flat_5),
+                (query_bias, flat_6),
+                (value_bias, flat_7),
+                (picture_ids, flat_slots_0),
+                (live_slots, flat_slots_1),
+                (up_bias_in, flat_up),
+            )
+        )
+    ]
+    for load in small + loads[4:] + loads[:4]:
+        load.start()
+    slots[...] = jnp.zeros_like(slots)
+    for load in small:
+        load.wait()
+    named = (flat_0, flat_1, flat_2, flat_3, flat_4, flat_5, flat_6, flat_7)
+    for i, value in enumerate(named):
+        vectors[i : i + 1, :] = value[...].astype(full).reshape(1, thin)
+    slots[0:1, :] = flat_slots_0[...].astype(full).reshape(1, block)
+    slots[1:2, :] = flat_slots_1[...].astype(full).reshape(1, block)
+    up_bias[0:1, :] = flat_up[...].astype(full).reshape(1, wide)
     pl.semaphore_wait(barrier, 5)
 
     vectors_swap = swapped(0, vectors, vectors_in)
     slots_swap = swapped(1, slots, all_slots.at[1])
-    tokens_swap = swapped(2, tokens, take(all_tokens, block, block))
-    out_swap = swapped(3, out_grad, out_in)
+    tokens_swap = swapped(2, tokens_hbm, take(all_tokens, block, block))
+    out_swap = swapped(3, out_hbm, wide_left.at[1, pl.ds(block, block)])
     part_swaps = [
         [
             swapped(
@@ -444,7 +498,8 @@
     out_swap.start()
 
     all_slots[0] = slots[...]
-    take(all_tokens, 0, block)[...] = tokens[...]
+    for load in loads[4:]:
+        load.wait()
     totals[...] = jnp.zeros_like(totals)
     up_sum[0] = jnp.zeros(up_sum.shape[1:], full)
 
@@ -468,6 +523,115 @@
 
         lax.fori_loop(0, count // strip, step, 0, unroll=2)
 
+    def is_low_first(j):
+        return lax.rem(j, 4) == 1
+
+    def first_pick(grads, k, low_first):
+        if low_first:
+            return grads.at[k, :, 1 - low_bit], low_peer
+        return grads.at[k, :, :, 1 - y_bit], y_peer
+
+    def second_pick(grads, k, low_first):
+        if low_first:
+            return grads.at[k, :, low_bit, 1 - y_bit], y_peer
+        return grads.at[k, :, 1 - low_bit, y_bit], low_peer
+
+    def first_copy(grads, k, j, low_first):
+        source, peer = first_pick(grads, k, low_first)
+        return remote(source, from_first.at[j], first_send.at[j], first_recv.at[j], peer)
+
+    def second_copy(grads, k, j, low_first):
+        source, peer = second_pick(grads, k, low_first)
+        return remote(source, from_second.at[j], second_send.at[j], second_recv.at[j], peer)
+
+    def high_copy(grads, k, j):
+        return remote(
+            grads.at[k, 1 - high_bit, low_bit, y_bit],
+            from_high.at[j],
+            high_send.at[j],
+            high_recv.at[j],
+            high_peer,
+        )
+
+    def by_order(j, action):
+        low_first = is_low_first(j)
+
+        @pl.when(low_first)
+        def _():
+            action(True)
+
+        @pl.when(jnp.logical_not(low_first))
+        def _():
+            action(False)
+
+    def issue(grads, k, j):
+        by_order(j, lambda low_first: first_copy(grads, k, j, low_first).start())
+
+    def emit(grads, k, j, value, ahead):
+        grads[k] = value.astype(low).reshape(grads.shape[1:])
+
+        @pl.when(j < ahead)
+        def _():
+            issue(grads, k, j)
+
+    def take_first(grads, k, j):
+        def action(low_first):
+            first_copy(grads, k, j, low_first).wait_recv()
+            if low_first:
+                grads[k, :, low_bit] = add_low(grads[k, :, low_bit], from_first[j])
+            else:
+                grads[k, :, :, y_bit] = add_low(grads[k, :, :, y_bit], from_first[j])
+            second_copy(grads, k, j, low_first).start()
+
+        by_order(j, action)
+
+    def take_second(grads, k, j):
+        by_order(j, lambda low_first: second_copy(grads, k, j, low_first).wait_recv())
+        grads[k, :, low_bit, y_bit] = add_low(grads[k, :, low_bit, y_bit], from_second[j])
+        high_copy(grads, k, j).start()
+
+    def rest_copy(summed, j):
+        return remote(summed.at[j, other], rest_in, core_send.at[j], core_recv.at[j], partner)
+
+    def wide_place(slot, j):
+        return wide_out.at[slot, :, pl.ds(pl.multiple_of(j * CW, CW), CW)]
+
+    def thin_place(slot, j):
+        at = (j - wide_chunks) // 2
+        return thin_out.at[
+            slot, lax.rem(j - wide_chunks, 2), :, pl.ds(pl.multiple_of(at * CW, CW), CW)
+        ]
+
+    def core_copy(summed, j, place):
+        return remote(
+            summed.at[j, other], place(core, j), core_send.at[j], core_recv.at[j], partner
+        )
+
+    def take_high(grads, k, j, summed):
+        high_copy(grads, k, j).wait_recv()
+        total = grads[k, high_bit, low_bit, y_bit].astype(full) + from_high[j].astype(full)
+        summed[j] = total.reshape(2, rows // 2, CW)
+
+        @pl.when(j < wide_chunks)
+        def _():
+            core_copy(summed, j, wide_place).start()
+            wide_place(core, j)[...] = summed[j, core]
+
+        @pl.when(jnp.logical_and(j >= wide_chunks, j < chunks - 1))
+        def _():
+            core_copy(summed, j, thin_place).start()
+            thin_place(core, j)[...] = summed[j, core]
+
+        @pl.when(j == chunks - 1)
+        def _():
+            rest_copy(summed, j).start()
+
+    def wide_value(j):
+        columns = pl.ds(pl.multiple_of(j * CW, CW), CW)
+        return product_tn(wide_left[core], wide_right[core, :, columns]) + product_tn(
+            wide_left_in[...], wide_right_in[:, columns]
+        )
+
     def mlp_scope(up_weight, down_weight, grad_act, wide_sem):
         wide_loads = [
             pltpu.make_async_copy(up_hbm, up_weight, wide_sem.at[0]),
@@ -491,13 +655,13 @@
 
             @pl.when(b == 0)
             def _():
-                for load in loads:
+                for load in loads[:4]:
                     load.wait()
 
             normed = thin_left[0, here, :]
-            queries[here, :] = (product(normed, query_weight[...]) + bias_query).astype(low)
-            keys_all[here, :] = product(normed, key_weight[...]).astype(low)
-            values_all[here, :] = (product(normed, value_weight[...]) + bias_value).astype(low)
+            queries[here, :] = (product_nt(normed, query_weight[...]) + bias_query).astype(low)
+            keys_all[here, :] = product_nt(normed, key_weight[...]).astype(low)
+            values_all[here, :] = (product_nt(normed, value_weight[...]) + bias_value).astype(low)
             marks = all_slots[b]
             across = jnp.where(marks[1:2] == 1.0, marks[0:1], -1.0)
             down_ids = jnp.transpose(marks)[:, 0:1]
@@ -540,9 +704,10 @@
             normed_pair(b).start()
 
         out_swap.wait_recv()
-        for b, source in enumerate((out_grad, out_in)):
+        for b in range(2):
             alive = jnp.transpose(all_slots[b])[:, 1:2].astype(low)
-            wide_left[1, pl.ds(b * block, block), :] = source[...] * alive
+            whole = pl.ds(b * block, block)
+            wide_left[1, whole, :] = wide_left[1, whole, :] * alive
         wide_loads[1].wait()
         out_rows = wide_left[1]
 
@@ -566,7 +731,7 @@
 
             def hidden_strip(at):
                 value = (
-                    tokens[at, :].astype(full)
+                    all_tokens[at, :].astype(full)
                     + own_part[at, :]
                     + part_in[0, at, :].astype(full)
                     + bias_proj
@@ -589,7 +754,7 @@
             normed = wide_left[0, here, :]
 
             def gelu_tile(at):
-                value = product(normed, up_weight[:, at]) + up_bias[:, at]
+                value = product_nt(normed, up_weight[at, :]) + up_bias[0:1, at]
                 square = value * value
                 bent = jnp.tanh(GELU_SCALE * value * (1.0 + 0.044715 * square))
                 bulge = 0.5 * (1.0 + bent)
@@ -618,11 +783,23 @@
                 left_pair(1).start()
                 right_pair(1).start()
 
+            @pl.when(b == 1)
+            def _():
+                for i in range(2):
+                    left_pair(i).wait_recv()
+                    right_pair(i).wait_recv()
+
+                def early_step(j, inner):
+                    emit(early, j, j, wide_value(j), AHEAD)
+                    return inner
+
+                lax.fori_loop(0, early_chunks, early_step, 0)
+
             grad_rows = wide_right[0, here, pl.ds(0, wide)]
 
             def back_tile(n, inner):
                 at = pl.ds(pl.multiple_of(n * 384, 384), 384)
-                value = product_nt(grad_rows, up_weight[at, :])
+                value = product(grad_rows, up_weight[:, at])
 
                 @pl.when(b == 0)
                 def _():
@@ -661,8 +838,6 @@
             return carry
 
         lax.fori_loop(0, 2, mlp_step, 0)
-        for copy in part_swaps[2]:
-            copy.start()
 
     pl.run_scoped(
         mlp_scope,
@@ -673,100 +848,55 @@
     )
 
     def grad_scope(grads, summed):
-        def y_copy(j):
-            return remote(
-                grads.at[j, :, :, 1 - y_bit], from_y.at[j], y_send.at[j], y_recv.at[j], y_peer
-            )
-
-        def low_copy(j):
-            return remote(
-                grads.at[j, :, 1 - low_bit, y_bit],
-                from_low.at[j],
-                low_send.at[j],
-                low_recv.at[j],
-                low_peer,
-            )
-
-        def high_copy(j):
-            return remote(
-                grads.at[j, 1 - high_bit, low_bit, y_bit],
-                from_high.at[j],
-                high_send.at[j],
-                high_recv.at[j],
-                high_peer,
-            )
-
-        def core_copy(j):
-            return remote(
-                summed.at[j, other],
-                sums_out.at[core, j],
-                core_send.at[j],
-                core_recv.at[j],
-                partner,
-            )
-
-        def core_arrival(j):
-            return remote(
-                summed.at[j, other],
-                sums_out.at[other, j],
-                core_send.at[j],
-                core_recv.at[j],
-                partner,
-            )
-
-        def keep_copy(j):
-            return pltpu.make_async_copy(summed.at[j, core], sums_out.at[core, j], keep_sem.at[j])
-
-        def emit(j, value):
-            grads[j] = value.astype(low).reshape(grads.shape[1:])
-            y_copy(j).start()
-
-        def pump(i):
+        def held(j, action):
+            @pl.when(j < early_chunks)
+            def _():
+                action(early, j, j)
+
+            @pl.when(j >= early_chunks)
+            def _():
+                action(grads, j - early_chunks, j)
+
+        def pump_step(i, carry):
+            @pl.when(i >= 6)
+            def _():
+                rest_copy(summed, i - 6).wait_recv()
+
+            @pl.when(jnp.logical_and(i >= 4, i < chunks + 4))
+            def _():
+                held(i - 4, lambda ref, k, j: take_high(ref, k, j, summed))
+
+            @pl.when(jnp.logical_and(i >= 2, i < chunks + 2))
+            def _():
+                held(i - 2, take_second)
+
             @pl.when(i < chunks)
             def _():
-                y_copy(i).wait_recv()
-                grads[i, :, :, y_bit] = add_low(grads[i, :, :, y_bit], from_y[i])
-                low_copy(i).start()
-
-            @pl.when(jnp.logical_and(i >= 1, i < chunks + 1))
-            def _():
-                j = i - 1
-                low_copy(j).wait_recv()
-                grads[j, :, low_bit, y_bit] = add_low(grads[j, :, low_bit, y_bit], from_low[j])
-                high_copy(j).start()
-
-            @pl.when(jnp.logical_and(i >= 2, i < chunks + 2))
-            def _():
-                j = i - 2
-                high_copy(j).wait_recv()
-                total = grads[j, high_bit, low_bit, y_bit].astype(full) + from_high[j].astype(full)
-                summed[j] = total.reshape(2, rows // 2, CW)
-                core_copy(j).start()
-                keep_copy(j).start()
-
-            @pl.when(i >= 3)
-            def _():
-                core_arrival(i - 3).wait_recv()
-                keep_copy(i - 3).wait()
-
-        def pump_step(i, carry):
-            pump(i)
+                held(i, take_first)
+
             return carry
 
-        for b in range(2):
-            left_pair(b).wait_recv()
-            right_pair(b).wait_recv()
+        def pump(first, last, made=wide_chunks):
+            def step(i, carry):
+                pump_step(i, carry)
+
+                @pl.when(i + AHEAD < made)
+                def _():
+                    issue(grads, i + AHEAD - early_chunks, i + AHEAD)
+
+                return carry
+
+            lax.fori_loop(first, last, step, 0)
+
+        def emit_late(j, value, ahead):
+            emit(grads, j - early_chunks, j, value, ahead)
 
         def wide_step(j, carry):
-            columns = pl.ds(pl.multiple_of(j * CW, CW), CW)
-            emit(
-                j,
-                product_tn(wide_left[core], wide_right[core, :, columns])
-                + product_tn(wide_left_in[...], wide_right_in[:, columns]),
-            )
+            emit_late(j, wide_value(j), AHEAD)
             return carry
 
-        lax.fori_loop(0, wide_chunks, wide_step, 0)
+        lax.fori_loop(early_chunks, wide_chunks, wide_step, 0)
+        pump(0, 2)
 
         for j in range(2):
             part_swaps[1][j].wait_recv()
@@ -786,6 +916,10 @@
 
             strips(half_block, j * half_block, norm_back_strip)
             hidden_swaps[j].start()
+        for copy in part_swaps[2]:
+            copy.start()
+
+        pump(2, 3)
 
         def back_step(b, carry):
             here = pl.ds(pl.multiple_of(b * block, block), block)
@@ -834,9 +968,9 @@
             def normed_tile(n, inner):
                 at = pl.ds(pl.multiple_of(n * 384, 384), 384)
                 value = (
-                    product_nt(grad_q, query_weight[at, :])
-                    + product_nt(grad_k, key_weight[at, :])
-                    + product_nt(grad_v, value_weight[at, :])
+                    product(grad_q, query_weight[:, at])
+                    + product(grad_k, key_weight[:, at])
+                    + product(grad_v, value_weight[:, at])
                 )
 
                 @pl.when(b == 0)
@@ -850,7 +984,7 @@
                 return inner
 
             lax.fori_loop(0, width // 384, normed_tile, 0)
-            lax.fori_loop(2 * b, 2 * b + 2, pump_step, 0)
+            pump(3 + 2 * b, 5 + 2 * b)
             return carry
 
         lax.fori_loop(0, 2, back_step, 0)
@@ -873,14 +1007,16 @@
 
         def thin_step(j, carry):
             columns = pl.ds(pl.multiple_of(j * CW, CW), CW)
-            emit(wide_chunks + j, first_part(columns))
-            emit(wide_chunks + 2 + j, second_part(columns))
+            emit_late(wide_chunks + 2 * j, first_part(columns), 7 + AHEAD)
+            emit_late(wide_chunks + 2 * j + 1, second_part(columns), 7 + AHEAD)
             return carry
 
         lax.fori_loop(0, 2, thin_step, 0)
         thin_rest = pl.ds(2 * CW, thin - 2 * CW)
         wide_rest = pl.ds(wide_chunks * CW, CW // 2)
-        emit(
+        rest = wide - wide_chunks * CW
+        rest_columns = pl.ds(wide_chunks * CW, rest)
+        emit_late(
             chunks - 1,
             jnp.concatenate(
                 [
@@ -891,27 +1027,17 @@
                 ],
                 axis=1,
             ),
+            7 + AHEAD,
         )
-
-        for copy in part_swaps[2]:
-            copy.wait_recv()
-
-        def out_strip(at):
-            alive = jnp.transpose(all_slots[0])
-            value = hidden[at, :] + own_down[at, :] + part_in[2, at, :].astype(full) + bias_down
-            block_out[at, :] = value.astype(low)
-
-        strips(block, 0, out_strip)
-        alive = jnp.transpose(all_slots[0])[:, 1:2].astype(low)
-        block_out[...] = block_out[...] * alive
+        pump(7, 10, chunks)
 
         for copy in part_swaps[3]:
             copy.wait_recv()
 
         def final_strip(at):
             grad = own_part[at, :] + part_in[3, at, :].astype(full)
-            xhat, inverse = norm_stats(tokens[at, :].astype(full))
-            tokens_grad[at, :] = (
+            xhat, inverse = norm_stats(all_tokens[at, :].astype(full))
+            rows_out[1, at, :] = (
                 grad_hidden[at, :] + norm_grad(xhat, inverse, gain_one, grad)
             ).astype(low)
             totals[0:1] += column_sums(grad * xhat)[None]
@@ -924,6 +1050,7 @@
         halves[0] = jnp.where(shard == 0, lower, upper)
         halves[1] = jnp.where(shard == 0, upper, lower)
         halves_swap.start()
+        pump(10, 12, chunks)
         grad_query_bias = column_sums(thin_first[0].astype(full))[None]
         grad_value_bias = column_sums(thin_first[1].astype(full))[None]
         halves_swap.wait_recv()
@@ -952,26 +1079,41 @@
             up_sum[i + 1] = up_sum[i] + up_in[i]
 
         vector_start(0)
+        for copy in part_swaps[2]:
+            copy.wait_recv()
+
+        def out_strip(at):
+            value = hidden[at, :] + own_down[at, :] + part_in[2, at, :].astype(full) + bias_down
+            rows_out[0, at, :] = value.astype(low)
+
+        strips(block, 0, out_strip)
+        alive = jnp.transpose(all_slots[0])[:, 1:2].astype(low)
+        rows_out[0] = rows_out[0] * alive
+
         vector_finish(0)
         vector_start(1)
-
-        lax.fori_loop(4, chunks, pump_step, 0)
+        pump(12, chunks + 1, chunks)
         vector_finish(1)
         vector_start(2)
-        pump(chunks)
+        pump(chunks + 1, chunks + 4, chunks)
         vector_finish(2)
         vector_start(3)
-        pump(chunks + 1)
-        pump(chunks + 2)
+        pump(chunks + 4, chunks + 6, chunks)
+        for slot in range(2):
+            source = jnp.where(core == slot, summed[chunks - 1, core], rest_in[...])
+            wide_out[slot, :, rest_columns] = source[:, :rest]
+            for place in range(2):
+                start = CW // 2 + place * (thin - 2 * CW)
+                thin_out[slot, place, :, thin_rest] = source[:, start : start + thin - 2 * CW]
         vector_finish(3)
         vectors_out[...] = vector_sum[4]
         up_bias_out[...] = up_sum[4]
 
         def drain(j, carry):
-            y_copy(j).wait_send()
-            low_copy(j).wait_send()
-            high_copy(j).wait_send()
-            core_copy(j).wait_send()
+            held(j, lambda ref, k, i: first_copy(ref, k, i, False).wait_send())
+            held(j, lambda ref, k, i: second_copy(ref, k, i, False).wait_send())
+            held(j, lambda ref, k, i: high_copy(ref, k, i).wait_send())
+            rest_copy(summed, j).wait_send()
             return carry
 
         lax.fori_loop(0, chunks, drain, 0)
@@ -981,7 +1123,7 @@
 
     pl.run_scoped(
         grad_scope,
-        pltpu.VMEM((chunks, 2, 2, 2, rows, CW), low),
+        pltpu.VMEM((chunks - early_chunks, 2, 2, 2, rows, CW), low),
         pltpu.VMEM((chunks, 2, rows // 2, CW), full),
     )
     for copy in [vectors_swap, slots_swap, tokens_swap, out_swap, halves_swap]:
@@ -994,15 +1136,13 @@
             pair(b).wait_send()
 
 
-def layer_call(
-    tokens, out_grad, slots, vectors, up_bias, query_weight, key_weight, value_weight, proj_weight,
-    up_weight, down_weight,
-):
+def layer_call(tokens, out_grad, slots, vectors, up_bias, matrices):
+    query_weight, up_weight, down_weight = matrices[0], matrices[4], matrices[5]
     low = jnp.bfloat16
     full = jnp.float32
     block, width = tokens.shape
-    thin = query_weight.shape[1]
-    wide = up_weight.shape[1]
+    thin = query_weight.shape[0]
+    wide = up_weight.shape[0]
     wide_pad = wide + -wide % 128
     heads = thin // HDIM
     replicas = lax.axis_size("replica")
@@ -1016,23 +1156,25 @@
     return pl.pallas_call(
         layer_kernel,
         out_shape=(
-            jax.ShapeDtypeStruct(tokens.shape, low),
-            jax.ShapeDtypeStruct(tokens.shape, low),
-            jax.ShapeDtypeStruct((2, chunks, half, CW), full),
-            jax.ShapeDtypeStruct(vectors.shape, full),
+            jax.ShapeDtypeStruct((2,) + tokens.shape, low),
+            jax.ShapeDtypeStruct((2, half, wide), full),
+            jax.ShapeDtypeStruct((2, 2, half, thin), full),
+            jax.ShapeDtypeStruct((8, thin), full),
             jax.ShapeDtypeStruct((1, wide_pad), full),
         ),
-        in_specs=[vmem] * 5 + [anywhere] * 6,
-        out_specs=(vmem, vmem, anywhere, vmem, vmem),
+        in_specs=[anywhere] * 19,
+        out_specs=(vmem,) * 5,
         scratch_shapes=[
-            pltpu.VMEM((width, thin), low),
-            pltpu.VMEM((width, thin), low),
-            pltpu.VMEM((width, thin), low),
+            pltpu.VMEM((8, block), full),
+            pltpu.VMEM((8, thin), full),
+            pltpu.VMEM((8, wide), full),
+            pltpu.VMEM((thin, width), low),
+            pltpu.VMEM((thin, width), low),
+            pltpu.VMEM((thin, width), low),
             pltpu.VMEM((thin, width), low),
             pltpu.VMEM((both, width), low),
-            pltpu.VMEM((block, width), low),
-            pltpu.VMEM((2,) + slots.shape, full),
-            pltpu.VMEM(vectors.shape, full),
+            pltpu.VMEM((2, 8, block), full),
+            pltpu.VMEM((8, thin), full),
             pltpu.VMEM((both, thin), low),
             pltpu.VMEM((both, thin), low),
             pltpu.VMEM((both, thin), low),
@@ -1054,9 +1196,11 @@
             pltpu.VMEM((both, width), low),
             pltpu.VMEM((both, thin), low),
             pltpu.VMEM((both, thin), low),
+            pltpu.VMEM((EARLY, 2, 2, 2, rows, CW), low),
             pltpu.VMEM((chunks, 2, 2, rows, CW), low),
             pltpu.VMEM((chunks, 2, rows, CW), low),
             pltpu.VMEM((chunks, rows, CW), low),
+            pltpu.VMEM((half, CW), full),
             pltpu.VMEM((8, width), full),
             pltpu.VMEM((2, 8, thin), full),
             pltpu.VMEM((8, thin), full),
@@ -1064,12 +1208,15 @@
             pltpu.VMEM((4, 8, thin), full),
             pltpu.VMEM((5, 1, wide_pad), full),
             pltpu.VMEM((4, 1, wide_pad), full),
-            dma((4,)),
+            *[pltpu.VMEM((thin,), low)] * 8,
+            *[pltpu.VMEM((block,), jnp.int32)] * 2,
+            pltpu.VMEM((wide,), low),
+            dma((11,)),
+            dma((6,)),
             dma((17,)),
             dma((17,)),
             dma((12,)),
             dma((12,)),
-            dma((chunks,)),
             dma((chunks,)),
             dma((chunks,)),
             dma((chunks,)),
@@ -1085,10 +1232,7 @@
             collective_id=0, has_side_effects=True, vmem_limit_bytes=67043328
         ),
         name="layer",
-    )(
-        tokens, out_grad, slots, vectors, up_bias, query_weight, key_weight, value_weight,
-        proj_weight, up_weight, down_weight,
-    )
+    )(tokens, out_grad, *slots, *vectors, up_bias, *matrices)
 
 
 def whole_layer(
@@ -1096,7 +1240,6 @@
     key_weight, value_weight, value_bias, proj_weight, proj_bias, ln2_gain, ln2_bias, up_weight,
     up_bias, down_weight, down_bias,
 ):
-    full = jnp.float32
     width = tokens.shape[1]
     if not by_kernel(lax.axis_size("replica"), width):
         return paired(
@@ -1104,53 +1247,32 @@
             query_bias, key_weight, value_weight, value_bias, proj_weight, proj_bias, ln2_gain,
             ln2_bias, up_weight, up_bias, down_weight, down_bias,
         )
-    half = width // 2
     wide = up_weight.shape[1]
-    vectors = jnp.stack(
-        [ln1_gain, ln1_bias, proj_bias, ln2_gain, ln2_bias, down_bias, query_bias, value_bias]
-    ).astype(full)
-    slots = jnp.stack([picture_ids, live_slots] + [live_slots] * 6).astype(full)
-    block_out, tokens_grad, sums, vectors, up_bias_grad = layer_call(
-        tokens, out_grad, slots, vectors, up_bias.astype(full)[None], query_weight, key_weight,
-        value_weight, proj_weight, up_weight, down_weight,
-    )
-    chunks = sums.shape[1]
-    wide_chunks = chunks - 5
-
-    def columns(slot, first, count):
-        return [sums[slot, first + i] for i in range(count)]
-
-    rest = [sums[0, chunks - 1], sums[1, chunks - 1]]
-    thin_rest = half - 2 * CW
-    wide_rest = wide - wide_chunks * CW
-
-    def wide_of(slot):
-        return jnp.concatenate(columns(slot, 0, wide_chunks) + [rest[slot][:, :wide_rest]], axis=1)
-
-    def thin_of(slot, place):
-        start = CW // 2 + place * thin_rest
-        return jnp.concatenate(
-            columns(slot, wide_chunks + 2 * place, 2) + [rest[slot][:, start : start + thin_rest]],
-            axis=1,
-        )
-
+    rows_out, wide_out, thin_out, vectors, up_bias_grad = layer_call(
+        tokens,
+        out_grad,
+        (picture_ids, live_slots),
+        (ln1_gain, ln1_bias, proj_bias, ln2_gain, ln2_bias, down_bias, query_bias, value_bias),
+        up_bias,
+        (query_weight.T, key_weight.T, value_weight.T, proj_weight, up_weight.T, down_weight),
+    )
     return (
-        block_out,
-        tokens_grad,
+        rows_out[0],
+        rows_out[1],
         vectors[0],
         vectors[1],
-        thin_of(0, 0),
+        thin_out[0, 0],
         vectors[6],
-        thin_of(0, 1),
-        thin_of(1, 0),
+        thin_out[0, 1],
+        thin_out[1, 0],
         vectors[7],
-        thin_of(1, 1).T,
+        thin_out[1, 1].T,
         vectors[2],
         vectors[3],
         vectors[4],
-        wide_of(0),
+        wide_out[0],
         up_bias_grad[0, :wide],
-        wide_of(1).T,
+        wide_out[1].T,
         vectors[5],
     )
 

time: 220 us -> 171 us (0.78)
  Pallas kernels: 186 us -> 163 us
  local copies, waits for them, and re-layouts: 28.8 us -> 7.21 us
  other arithmetic: 2.76 us -> 0 us
    pallas_call x1, Pallas kernels: 186 us -> 163 us  [layer_call(): pl.pallas_call(layer_kernel, out_shape=(jax.ShapeDtypeStruct((2,) + token...]
    unnamed x28 -> x6, local copies, waits for them, and re-layouts: 16.1 us -> 0.61 us
    another operation x10 -> x0, local copies, waits for them, and re-layouts: 6.59 us -> none  [the longest x9 5.63 us: whole_layer(): jnp.stack([ln1_gain, ln1_bias, proj_bias, ln2_gain, ln2_bias, down_bias,...]
    transpose x0 -> x2, local copies, waits for them, and re-layouts: none -> 3.18 us  [the longest x1 2.06 us: whole_layer(): thin_out[1, 1]]
where the time goes in v3:
time: 171 us
  Pallas kernels  163 us (95%)
  local copies, waits for them, and re-layouts  7.21 us (4%)
    pallas_call x1, Pallas kernels, layer_call(): pl.pallas_call(layer_kernel, out_shape=(jax.ShapeDtypeStruct((2,) + token...  163 us

profile of v3, /device:TPU:0, one launch (start us, length us, event | category | flops | bytes accessed | tf_op | source)
XLA Modules:
  0.0 170.7 jit_solution(14676458185070898590)
XLA Ops:
  0.7 162.8 %layer.1 = (bf16[2,256,1152]{2,1,0:T(8,128)(2,1)}, f32[2,72,2152]{2,1,0:T(8,128)}, f32[2,2,72,576]{3,2,1,0:T(8,128)}, f32[8,576]{1,0:T(8,128)}, f32[1,2176]{1,0:T(1,128)}) custom-call(bf16[256,1152]{1,0:T(8,128)(2,1)} %tokens_hbm.1, bf16[256,1152]{1,0:T(8,128)(2,1)} %out_hbm.1, s32[256]{0:T(256)} %picture_ids.1, s32[256]{0:T(256)} %live_slots.1, ...), custom_call_target="tpu_custom_call" | custom-call | tf_op jit(solution)/shard_map/layer/pallas_call | solution.py:1156
  163.4 0.0 copy-start
  163.5 1.7 slice_reduce_fusion.1
  165.2 2.1 %slice_bitcast_fusion.4 = (f32[576,72]{0,1:T(8,128)}, f32[72,576]{1,0:T(8,128)}, f32[72,576]{1,0:T(8,128)}, f32[72,576]{1,0:T(8,128)}) fusion(f32[2,2,72,576]{3,2,1,0:T(8,128)} %get-tuple-element.24), kind=kLoop, calls=%fused_computation.4 | loop fusion | bytes 1327104 | tf_op jit(solution)/shard_map/transpose | solution.py:1269
  167.2 0.0 copy-start.1
  167.2 0.0 copy-done
  167.2 1.1 slice_bitcast_fusion
  168.3 0.0 copy-start.2
  168.3 0.6 copy-done.1
  168.9 1.1 slice_bitcast_fusion.2
  170.0 0.0 copy-done.2
  170.0 0.6 slice_reduce_fusion
Async XLA Ops:
  163.4 3.8 %copy-start = (f32[2,72,2152]{2,1,0:T(8,128)S(1)}, f32[2,72,2152]{2,1,0:T(8,128)}, u32[]{:S(2)}) copy-start(f32[2,72,2152]{2,1,0:T(8,128)} %get-tuple-element.25) | copy-start | bytes 3718660
  167.2 1.7 %copy-start.1 = (bf16[2,256,1152]{2,1,0:T(8,128)(2,1)S(1)}, bf16[2,256,1152]{2,1,0:T(8,128)(2,1)}, u32[]{:S(2)}) copy-start(bf16[2,256,1152]{2,1,0:T(8,128)(2,1)} %get-tuple-element.22) | copy-start | bytes 3538948
  168.3 1.7 copy-start.2

commit v4 on v3

--- a/solution.py
+++ b/solution.py
@@ -13,6 +13,7 @@
 CW = 256
 EARLY = 2
 AHEAD = 3
+UNROLL = 2
 GELU_SCALE = 0.7978845608028654
 
 
@@ -427,6 +428,16 @@
     for load in small + loads[4:] + loads[:4]:
         load.start()
     slots[...] = jnp.zeros_like(slots)
+    tokens_swaps = [
+        swapped(
+            index,
+            tokens_hbm.at[pl.ds(j * half_block, half_block)],
+            all_tokens.at[pl.ds(block + j * half_block, half_block)],
+        )
+        for j, index in ((0, 2), (1, 17))
+    ]
+    pl.semaphore_wait(barrier, 5)
+    tokens_swaps[0].start()
     for load in small:
         load.wait()
     named = (flat_0, flat_1, flat_2, flat_3, flat_4, flat_5, flat_6, flat_7)
@@ -435,11 +446,9 @@
     slots[0:1, :] = flat_slots_0[...].astype(full).reshape(1, block)
     slots[1:2, :] = flat_slots_1[...].astype(full).reshape(1, block)
     up_bias[0:1, :] = flat_up[...].astype(full).reshape(1, wide)
-    pl.semaphore_wait(barrier, 5)
 
     vectors_swap = swapped(0, vectors, vectors_in)
     slots_swap = swapped(1, slots, all_slots.at[1])
-    tokens_swap = swapped(2, tokens_hbm, take(all_tokens, block, block))
     out_swap = swapped(3, out_hbm, wide_left.at[1, pl.ds(block, block)])
     part_swaps = [
         [
@@ -477,24 +486,25 @@
     def left_pair(b):
         return pair_rows(0, wide_left.at[other], wide_left_in, b)
 
-    def right_pair(b):
-        return pair_rows(2, wide_right.at[other], wide_right_in, b)
+    def right_pair(q):
+        here = pl.ds(q * half_block, half_block)
+        return paired_copy(2 + q, wide_right.at[other, here], wide_right_in.at[here])
 
     def normed_pair(b):
-        return pair_rows(4, thin_left.at[0], thin_left_in, b)
+        return pair_rows(6, thin_left.at[0], thin_left_in, b)
 
     def other_pair(b):
-        return pair_rows(6, thin_left.at[other], thin_other_in, b)
+        return pair_rows(8, thin_left.at[other], thin_other_in, b)
 
     def first_pair(b):
-        return pair_rows(8, thin_first.at[other], thin_first_in, b)
+        return pair_rows(10, thin_first.at[other], thin_first_in, b)
 
     def second_pair(b):
-        return pair_rows(10, thin_second.at[other], thin_second_in, b)
+        return pair_rows(12, thin_second.at[other], thin_second_in, b)
 
     vectors_swap.start()
     slots_swap.start()
-    tokens_swap.start()
+    tokens_swaps[1].start()
     out_swap.start()
 
     all_slots[0] = slots[...]
@@ -645,7 +655,8 @@
 
             @pl.when(b == 1)
             def _():
-                tokens_swap.wait_recv()
+                for copy in tokens_swaps:
+                    copy.wait_recv()
 
             def norm_strip(at):
                 xhat, _ = norm_stats(all_tokens[at, :].astype(full))
@@ -743,101 +754,83 @@
             strips(half_block, j * half_block, hidden_strip)
             normed_swaps[j].start()
 
-        def mlp_step(b, carry):
-            here = pl.ds(pl.multiple_of(b * block, block), block)
-
-            @pl.when(b == 1)
-            def _():
-                for copy in normed_swaps:
-                    copy.wait_recv()
-
-            normed = wide_left[0, here, :]
-
-            def gelu_tile(at):
-                value = product_nt(normed, up_weight[at, :]) + up_bias[0:1, at]
-                square = value * value
-                bent = jnp.tanh(GELU_SCALE * value * (1.0 + 0.044715 * square))
-                bulge = 0.5 * (1.0 + bent)
-                wide_right[1, here, at] = (value * bulge).astype(low)
-                slope = bulge + 0.5 * value * (1.0 - bent * bent) * (
-                    GELU_SCALE * (1.0 + 0.134145 * square)
-                )
-                grad = (slope * grad_act[here, at].astype(full)).astype(low)
-                wide_right[0, here, at] = grad
-                up_sum[0, :, at] += jnp.sum(grad.astype(full), axis=0, keepdims=True)
-
-            def up_tile(t, inner):
-                gelu_tile(pl.ds(pl.multiple_of(t * CW, CW), CW))
-                return inner
-
-            lax.fori_loop(0, wide_chunks, up_tile, 0)
-            gelu_tile(rest_at)
-
-            @pl.when(b == 0)
-            def _():
-                right_pair(0).start()
-
-            @pl.when(b == 1)
-            def _():
-                left_pair(0).start()
-                left_pair(1).start()
-                right_pair(1).start()
-
-            @pl.when(b == 1)
-            def _():
-                for i in range(2):
-                    left_pair(i).wait_recv()
-                    right_pair(i).wait_recv()
-
-                def early_step(j, inner):
-                    emit(early, j, j, wide_value(j), AHEAD)
-                    return inner
-
-                lax.fori_loop(0, early_chunks, early_step, 0)
-
-            grad_rows = wide_right[0, here, pl.ds(0, wide)]
+        left_pair(0).start()
+
+        def gelu_tile(here, at):
+            value = product_nt(wide_left[0, here, :], up_weight[at, :]) + up_bias[0:1, at]
+            square = value * value
+            bent = jnp.tanh(GELU_SCALE * value * (1.0 + 0.044715 * square))
+            bulge = 0.5 * (1.0 + bent)
+            wide_right[1, here, at] = (value * bulge).astype(low)
+            slope = bulge + 0.5 * value * (1.0 - bent * bent) * (
+                GELU_SCALE * (1.0 + 0.134145 * square)
+            )
+            grad = (slope * grad_act[here, at].astype(full)).astype(low)
+            wide_right[0, here, at] = grad
+            up_sum[0, :, at] += jnp.sum(grad.astype(full), axis=0, keepdims=True)
+
+        def back_tiles(b):
+            grad_rows = wide_right[0, pl.ds(b * block, block), pl.ds(0, wide)]
 
             def back_tile(n, inner):
                 at = pl.ds(pl.multiple_of(n * 384, 384), 384)
                 value = product(grad_rows, up_weight[:, at])
-
-                @pl.when(b == 0)
+                if b == 0:
+                    own_part[:, at] = value
+                else:
+                    part_send[1, :, at] = value.astype(low)
+                return inner
+
+            lax.fori_loop(0, width // 384, back_tile, 0)
+
+        def mlp_step(q, carry):
+            here = pl.ds(pl.multiple_of(q * half_block, half_block), half_block)
+            for j in range(2):
+
+                @pl.when(q == 2 + j)
                 def _():
-                    own_part[:, at] = value
-
-                @pl.when(b == 1)
-                def _():
-                    part_send[1, :, at] = value.astype(low)
-
+                    normed_swaps[j].wait_recv()
+                    if j == 1:
+                        left_pair(1).start()
+
+            def up_tile(t, inner):
+                gelu_tile(here, pl.ds(pl.multiple_of(t * CW, CW), CW))
                 return inner
 
-            lax.fori_loop(0, width // 384, back_tile, 0)
-
-            @pl.when(b == 1)
+            lax.fori_loop(0, wide_chunks, up_tile, 0, unroll=UNROLL)
+            gelu_tile(here, rest_at)
+            right_pair(q).start()
+
+            @pl.when(q == 1)
             def _():
-                for copy in part_swaps[1]:
-                    copy.start()
-
-            act_rows = wide_right[1, here, pl.ds(0, wide)]
-
-            def down_tile(n, inner):
-                at = pl.ds(pl.multiple_of(n * 384, 384), 384)
-                value = product(act_rows, down_weight[:, at])
-
-                @pl.when(b == 0)
-                def _():
-                    own_down[:, at] = value
-
-                @pl.when(b == 1)
-                def _():
-                    part_send[2, :, at] = value.astype(low)
-
-                return inner
-
-            lax.fori_loop(0, width // 384, down_tile, 0)
+                back_tiles(0)
+
             return carry
 
-        lax.fori_loop(0, 2, mlp_step, 0)
+        lax.fori_loop(0, 4, mlp_step, 0)
+        for i in range(2):
+            left_pair(i).wait_recv()
+        for q in range(4):
+            right_pair(q).wait_recv()
+
+        def early_step(j, inner):
+            emit(early, j, j, wide_value(j), AHEAD)
+            return inner
+
+        lax.fori_loop(0, early_chunks, early_step, 0)
+        back_tiles(1)
+        for copy in part_swaps[1]:
+            copy.start()
+        act_rows = wide_right[1, :, pl.ds(0, wide)]
+
+        def down_tile(n, inner):
+            at = pl.ds(pl.multiple_of(n * 384, 384), 384)
+            value = product(act_rows, down_weight[:, at])
+            own_down[:, at] = value[:block]
+            part_send[2, :, at] = value[block:].astype(low)
+            return inner
+
+        lax.fori_loop(0, width // 384, down_tile, 0)
 
     pl.run_scoped(
         mlp_scope,
@@ -1126,14 +1119,90 @@
         pltpu.VMEM((chunks - early_chunks, 2, 2, 2, rows, CW), low),
         pltpu.VMEM((chunks, 2, rows // 2, CW), full),
     )
-    for copy in [vectors_swap, slots_swap, tokens_swap, out_swap, halves_swap]:
+    for copy in [vectors_swap, slots_swap, *tokens_swaps, out_swap, halves_swap]:
         copy.wait_send()
     for copies in part_swaps + [normed_swaps, hidden_swaps]:
         for copy in copies:
             copy.wait_send()
+    for q in range(4):
+        right_pair(q).wait_send()
     for b in range(2):
-        for pair in (left_pair, right_pair, normed_pair, other_pair, first_pair, second_pair):
+        for pair in (left_pair, normed_pair, other_pair, first_pair, second_pair):
             pair(b).wait_send()
+
+
+def publish_kernel(rows_in, wide_in, thin_in, vectors_in, up_in, *refs):
+    outs, (rows_at, wide_at, thin_at, vectors_at, up_at) = refs[:17], refs[17:22]
+    flats, in_sem, out_sem = refs[22:31], refs[31], refs[32]
+    loads = [
+        pltpu.make_async_copy(source, target, in_sem.at[i])
+        for i, (source, target) in enumerate(
+            (
+                (vectors_in, vectors_at),
+                (up_in, up_at),
+                (thin_in, thin_at),
+                (wide_in, wide_at),
+                (rows_in, rows_at),
+            )
+        )
+    ]
+    for load in loads:
+        load.start()
+    stores = []
+
+    def store(source, place):
+        copy = pltpu.make_async_copy(source, outs[place], out_sem.at[place])
+        copy.start()
+        stores.append(copy)
+
+    loads[0].wait()
+    loads[1].wait()
+    for i in range(8):
+        flats[i][...] = vectors_at[i : i + 1, :].reshape(flats[i].shape)
+    wide = flats[8].shape[0]
+    flats[8][...] = up_at[:, :wide].reshape(flats[8].shape)
+    loads[2].wait()
+    for source, place in ((thin_at.at[0, 0], 4), (thin_at.at[0, 1], 6), (thin_at.at[1, 0], 7), (thin_at.at[1, 1], 9)):
+        store(source, place)
+    loads[3].wait()
+    store(wide_at.at[0], 13)
+    store(wide_at.at[1], 15)
+    loads[4].wait()
+    store(rows_at.at[0], 0)
+    store(rows_at.at[1], 1)
+    for flat, place in zip(flats, (2, 3, 10, 11, 12, 16, 5, 8, 14)):
+        store(flat, place)
+    for copy in stores:
+        copy.wait()
+
+
+def publish_call(rows_out, wide_out, thin_out, vectors, up_bias_grad):
+    full = jnp.float32
+    thin = vectors.shape[1]
+    _, half, wide = wide_out.shape
+    anywhere = pl.BlockSpec(memory_space=pl.ANY)
+    vector = jax.ShapeDtypeStruct((thin,), full)
+    matrix = jax.ShapeDtypeStruct((half, thin), full)
+    tall = jax.ShapeDtypeStruct((half, wide), full)
+    rows = jax.ShapeDtypeStruct(rows_out.shape[1:], rows_out.dtype)
+    inputs = (rows_out, wide_out, thin_out, vectors, up_bias_grad)
+    return pl.pallas_call(
+        publish_kernel,
+        out_shape=(
+            rows, rows, vector, vector, matrix, vector, matrix, matrix, vector, matrix, vector,
+            vector, vector, tall, jax.ShapeDtypeStruct((wide,), full), tall, vector,
+        ),
+        in_specs=[anywhere] * 5,
+        out_specs=(anywhere,) * 17,
+        scratch_shapes=[
+            *[pltpu.VMEM(value.shape, value.dtype) for value in inputs],
+            *[pltpu.VMEM((thin,), full)] * 8,
+            pltpu.VMEM((wide,), full),
+            pltpu.SemaphoreType.DMA((5,)),
+            pltpu.SemaphoreType.DMA((17,)),
+        ],
+        name="publish",
+    )(*inputs)
 
 
 def layer_call(tokens, out_grad, slots, vectors, up_bias, matrices):
@@ -1213,10 +1282,10 @@
             pltpu.VMEM((wide,), low),
             dma((11,)),
             dma((6,)),
-            dma((17,)),
-            dma((17,)),
-            dma((12,)),
-            dma((12,)),
+            dma((18,)),
+            dma((18,)),
+            dma((14,)),
+            dma((14,)),
             dma((chunks,)),
             dma((chunks,)),
             dma((chunks,)),
@@ -1247,8 +1316,7 @@
             query_bias, key_weight, value_weight, value_bias, proj_weight, proj_bias, ln2_gain,
             ln2_bias, up_weight, up_bias, down_weight, down_bias,
         )
-    wide = up_weight.shape[1]
-    rows_out, wide_out, thin_out, vectors, up_bias_grad = layer_call(
+    packed = layer_call(
         tokens,
         out_grad,
         (picture_ids, live_slots),
@@ -1256,25 +1324,10 @@
         up_bias,
         (query_weight.T, key_weight.T, value_weight.T, proj_weight, up_weight.T, down_weight),
     )
-    return (
-        rows_out[0],
-        rows_out[1],
-        vectors[0],
-        vectors[1],
-        thin_out[0, 0],
-        vectors[6],
-        thin_out[0, 1],
-        thin_out[1, 0],
-        vectors[7],
-        thin_out[1, 1].T,
-        vectors[2],
-        vectors[3],
-        vectors[4],
-        wide_out[0],
-        up_bias_grad[0, :wide],
-        wide_out[1].T,
-        vectors[5],
-    )
+    outs = list(publish_call(*packed))
+    outs[9] = outs[9].T
+    outs[15] = outs[15].T
+    return tuple(outs)
 
 
 def solution(mesh):

time: 171 us -> 161 us (0.942)
  local copies, waits for them, and re-layouts: 7.21 us -> 0 us
  Pallas kernels: 163 us -> 160 us
    pallas_call x1, Pallas kernels: 163 us -> 157 us  [layer_call(): pl.pallas_call(layer_kernel, out_shape=(jax.ShapeDtypeStruct((2,) + token...]
    pallas_call x0 -> x1, Pallas kernels: none -> 3.19 us  [publish_call(): pl.pallas_call(publish_kernel, out_shape=(rows, rows, vector, vector, mat...]
    transpose x2 -> x0, local copies, waits for them, and re-layouts: 3.18 us -> none  [the longest x1 2.06 us: whole_layer(): thin_out[1, 1]]
    slice x2 -> x0, local copies, waits for them, and re-layouts: 2.32 us -> none  [the longest x1 1.7 us: whole_layer(): vectors[5]]
where the time goes in v4:
time: 161 us
  Pallas kernels  160 us (99%)
    pallas_call x1, Pallas kernels, layer_call(): pl.pallas_call(layer_kernel, out_shape=(jax.ShapeDtypeStruct((2,) + token...  157 us

profile of v4, /device:TPU:0, one launch (start us, length us, event | category | flops | bytes accessed | tf_op | source)
XLA Modules:
  0.0 160.7 jit_solution(5088189719116792112)
XLA Ops:
  0.7 156.7 %layer.1 = (bf16[2,256,1152]{2,1,0:T(8,128)(2,1)}, f32[2,72,2152]{2,1,0:T(8,128)}, f32[2,2,72,576]{3,2,1,0:T(8,128)}, f32[8,576]{1,0:T(8,128)}, f32[1,2176]{1,0:T(1,128)}) custom-call(bf16[256,1152]{1,0:T(8,128)(2,1)} %tokens_hbm.1, bf16[256,1152]{1,0:T(8,128)(2,1)} %out_hbm.1, s32[256]{0:T(256)} %picture_ids.1, s32[256]{0:T(256)} %live_slots.1, ...), custom_call_target="tpu_custom_call" | custom-call | tf_op jit(solution)/shard_map/layer/pallas_call | solution.py:1225
  157.4 3.2 %publish.1 = (bf16[256,1152]{1,0:T(8,128)(2,1)}, bf16[256,1152]{1,0:T(8,128)(2,1)}, f32[576]{0:T(1024)}, f32[576]{0:T(1024)}, f32[72,576]{1,0:T(8,128)}, /*index...) custom-call(bf16[2,256,1152]{2,1,0:T(8,128)(2,1)} %get-tuple-element, ...), custom_call_target="tpu_custom_call" | custom-call | tf_op jit(solution)/shard_map/publish/pallas_call | solution.py:1189

commit v5 on v4

--- a/solution.py
+++ b/solution.py
@@ -11,8 +11,10 @@
 norm_eps = 1e-06
 MESH = pl.DeviceIdType.MESH
 CW = 256
-EARLY = 2
-AHEAD = 3
+SUB = 128
+EARLY = 4
+AHEAD = 6
+LAGS = (3, 6, 8)
 UNROLL = 2
 GELU_SCALE = 0.7978845608028654
 
@@ -272,11 +274,16 @@
     proj_hbm,
     up_hbm,
     down_hbm,
+    rows_hbm,
+    wide_hbm,
+    thin_hbm,
+    rest_hbm,
+    vectors_hbm,
+    up_sum_hbm,
     rows_out,
     wide_out,
     thin_out,
-    vectors_out,
-    up_bias_out,
+    rest_out,
     slots,
     vectors,
     up_bias,
@@ -284,6 +291,8 @@
     key_weight,
     value_weight,
     proj_weight,
+    proj_other,
+    mixed_other,
     all_tokens,
     all_slots,
     vectors_in,
@@ -292,7 +301,6 @@
     values_all,
     probs,
     hidden,
-    grad_hidden,
     own_part,
     own_down,
     part_send,
@@ -312,7 +320,6 @@
     from_first,
     from_second,
     from_high,
-    rest_in,
     totals,
     halves,
     halves_in,
@@ -335,6 +342,8 @@
     load_sem,
     swap_send,
     swap_recv,
+    proj_send,
+    proj_recv,
     pair_send,
     pair_recv,
     first_send,
@@ -347,18 +356,21 @@
     core_recv,
     vec_send,
     vec_recv,
+    out_sem,
 ):
     full = jnp.float32
     low = jnp.bfloat16
     chunks = from_first.shape[0]
     rows = from_first.shape[3]
     early_chunks = early.shape[0]
+    second_lag, high_lag, core_lag = LAGS
     block, width = tokens_hbm.shape
     thin = queries.shape[1]
     wide = up_bias.shape[1]
     heads = thin // HDIM
     score_scale = HDIM ** (-0.5)
-    wide_chunks = chunks - 5
+    wide_chunks = chunks // 2 - 5
+    wide_subs = 2 * wide_chunks
     half_block = block // 2
     strip = 32
     shard = lax.axis_index("shard")
@@ -374,6 +386,7 @@
     low_peer = (shard, replica + 4 - 8 * low_bit)
     high_peer = (shard, replica + 8 - 16 * high_bit)
     peers = (partner, y_peer, low_peer, high_peer)
+    vector_peers = (partner, high_peer, low_peer, y_peer)
 
     def remote(source, target, send, recv, peer):
         return pltpu.make_async_remote_copy(
@@ -436,8 +449,6 @@
         )
         for j, index in ((0, 2), (1, 17))
     ]
-    pl.semaphore_wait(barrier, 5)
-    tokens_swaps[0].start()
     for load in small:
         load.wait()
     named = (flat_0, flat_1, flat_2, flat_3, flat_4, flat_5, flat_6, flat_7)
@@ -446,10 +457,18 @@
     slots[0:1, :] = flat_slots_0[...].astype(full).reshape(1, block)
     slots[1:2, :] = flat_slots_1[...].astype(full).reshape(1, block)
     up_bias[0:1, :] = flat_up[...].astype(full).reshape(1, wide)
+    pl.semaphore_wait(barrier, 5)
 
     vectors_swap = swapped(0, vectors, vectors_in)
     slots_swap = swapped(1, slots, all_slots.at[1])
-    out_swap = swapped(3, out_hbm, wide_left.at[1, pl.ds(block, block)])
+    out_swaps = [
+        swapped(
+            index,
+            out_hbm.at[pl.ds(j * half_block, half_block)],
+            wide_left.at[1, pl.ds(block + j * half_block, half_block)],
+        )
+        for j, index in ((0, 3), (1, 13))
+    ]
     part_swaps = [
         [
             swapped(
@@ -459,16 +478,28 @@
             )
             for j in range(2)
         ]
-        for i in range(4)
+        for i in range(3)
     ]
-    normed_swaps = [
+    mixed_swaps = [
         swapped(
-            12 + j,
-            wide_left.at[0, pl.ds(j * half_block, half_block)],
-            wide_left.at[0, pl.ds(block + j * half_block, half_block)],
-        )
-        for j in range(2)
+            10 + b,
+            thin_second.at[1, pl.ds(b * block, block)],
+            mixed_other.at[pl.ds((1 - b) * block, block)],
+        )
+        for b in range(2)
     ]
+    quarter = thin // 4
+    most = width // 9 * 5
+    rest_width = width - most
+    own_rows = pl.ds((2 * low_bit + y_bit) * quarter, quarter)
+    own_columns = pl.ds(pl.multiple_of(core * rest_width, 128), most)
+    proj_piece = proj_other.at[own_rows, own_columns]
+    proj_swap = swapped(12, proj_hbm.at[own_rows, own_columns], proj_piece)
+    proj_y = remote(proj_piece, proj_piece, proj_send.at[0], proj_recv.at[0], y_peer)
+    proj_low_piece = proj_other.at[pl.ds(low_bit * 2 * quarter, 2 * quarter), own_columns]
+    proj_low = remote(proj_low_piece, proj_low_piece, proj_send.at[1], proj_recv.at[1], low_peer)
+    proj_core_piece = proj_other.at[:, pl.ds(pl.multiple_of(core * most, 128), rest_width)]
+    proj_core = remote(proj_core_piece, proj_core_piece, proj_send.at[2], proj_recv.at[2], partner)
     hidden_swaps = [
         swapped(
             14 + j,
@@ -504,12 +535,20 @@
 
     vectors_swap.start()
     slots_swap.start()
-    tokens_swaps[1].start()
-    out_swap.start()
+    proj_swap.start()
+    for copy in tokens_swaps:
+        copy.start()
 
     all_slots[0] = slots[...]
     for load in loads[4:]:
         load.wait()
+
+    def mask_rows(b, first, count):
+        alive = jnp.transpose(all_slots[b])[first : first + count, 1:2].astype(low)
+        at = pl.ds(b * block + first, count)
+        wide_left[1, at, :] = wide_left[1, at, :] * alive
+
+    mask_rows(0, 0, block)
     totals[...] = jnp.zeros_like(totals)
     up_sum[0] = jnp.zeros(up_sum.shape[1:], full)
 
@@ -534,7 +573,7 @@
         lax.fori_loop(0, count // strip, step, 0, unroll=2)
 
     def is_low_first(j):
-        return lax.rem(j, 4) == 1
+        return jnp.logical_and(lax.rem(j, 4) == 1, j < chunks - 1)
 
     def first_pick(grads, k, low_first):
         if low_first:
@@ -578,11 +617,13 @@
         by_order(j, lambda low_first: first_copy(grads, k, j, low_first).start())
 
     def emit(grads, k, j, value, ahead):
-        grads[k] = value.astype(low).reshape(grads.shape[1:])
-
-        @pl.when(j < ahead)
-        def _():
-            issue(grads, k, j)
+        for i in range(2):
+            piece = value[:, i * SUB : (i + 1) * SUB].astype(low)
+            grads[k + i] = piece.reshape(grads.shape[1:])
+
+            @pl.when(j + i < ahead)
+            def _():
+                issue(grads, k + i, j + i)
 
     def take_first(grads, k, j):
         def action(low_first):
@@ -600,17 +641,21 @@
         grads[k, :, low_bit, y_bit] = add_low(grads[k, :, low_bit, y_bit], from_second[j])
         high_copy(grads, k, j).start()
 
+    def wide_place(slot, j):
+        return wide_out.at[slot, :, pl.ds(pl.multiple_of(j * SUB, SUB), SUB)]
+
+    def thin_place(slot, j):
+        tile = j // 2 - wide_chunks
+        start = tile // 2 * CW + lax.rem(j, 2) * SUB
+        return thin_out.at[slot, lax.rem(tile, 2), :, pl.ds(pl.multiple_of(start, SUB), SUB)]
+
+    def rest_place(slot, j):
+        return rest_out.at[slot, j - (chunks - 2)]
+
     def rest_copy(summed, j):
-        return remote(summed.at[j, other], rest_in, core_send.at[j], core_recv.at[j], partner)
-
-    def wide_place(slot, j):
-        return wide_out.at[slot, :, pl.ds(pl.multiple_of(j * CW, CW), CW)]
-
-    def thin_place(slot, j):
-        at = (j - wide_chunks) // 2
-        return thin_out.at[
-            slot, lax.rem(j - wide_chunks, 2), :, pl.ds(pl.multiple_of(at * CW, CW), CW)
-        ]
+        return remote(
+            summed.at[j, other], rest_out.at[core, 0], core_send.at[j], core_recv.at[j], partner
+        )
 
     def core_copy(summed, j, place):
         return remote(
@@ -620,21 +665,17 @@
     def take_high(grads, k, j, summed):
         high_copy(grads, k, j).wait_recv()
         total = grads[k, high_bit, low_bit, y_bit].astype(full) + from_high[j].astype(full)
-        summed[j] = total.reshape(2, rows // 2, CW)
-
-        @pl.when(j < wide_chunks)
-        def _():
-            core_copy(summed, j, wide_place).start()
-            wide_place(core, j)[...] = summed[j, core]
-
-        @pl.when(jnp.logical_and(j >= wide_chunks, j < chunks - 1))
-        def _():
-            core_copy(summed, j, thin_place).start()
-            thin_place(core, j)[...] = summed[j, core]
-
-        @pl.when(j == chunks - 1)
-        def _():
-            rest_copy(summed, j).start()
+        summed[j] = total.reshape(2, rows // 2, SUB)
+        for where, place in (
+            (j < wide_subs, wide_place),
+            (jnp.logical_and(j >= wide_subs, j < chunks - 2), thin_place),
+            (j >= chunks - 2, rest_place),
+        ):
+
+            @pl.when(where)
+            def _():
+                core_copy(summed, j, place).start()
+                place(core, j)[...] = summed[j, core]
 
     def wide_value(j):
         columns = pl.ds(pl.multiple_of(j * CW, CW), CW)
@@ -653,8 +694,15 @@
         def attend_step(b, carry):
             here = pl.ds(pl.multiple_of(b * block, block), block)
 
+            @pl.when(b == 0)
+            def _():
+                proj_swap.wait_recv()
+                proj_y.start()
+
             @pl.when(b == 1)
             def _():
+                proj_y.wait_recv()
+                proj_low.start()
                 for copy in tokens_swaps:
                     copy.wait_recv()
 
@@ -689,38 +737,24 @@
                 probs_low = (scaled * share).astype(low)
                 probs[b * heads + h] = probs_low
                 thin_second[1, here, cut] = product(probs_low, v_all[:, cut]).astype(low)
-            mixed = thin_second[1, here, :]
-
-            def proj_tile(n, inner):
-                at = pl.ds(pl.multiple_of(n * 384, 384), 384)
-                value = product(mixed, proj_weight[:, at])
-
-                @pl.when(b == 0)
+            for i in range(2):
+
+                @pl.when(b == i)
                 def _():
-                    own_part[:, at] = value
-
-                @pl.when(b == 1)
-                def _():
-                    part_send[0, :, at] = value.astype(low)
-
-                return inner
-
-            lax.fori_loop(0, width // 384, proj_tile, 0)
+                    mixed_swaps[i].start()
+
             return carry
 
         lax.fori_loop(0, 2, attend_step, 0)
-        for copy in part_swaps[0]:
+        for copy in out_swaps:
             copy.start()
         for b in range(2):
             normed_pair(b).start()
-
-        out_swap.wait_recv()
-        for b in range(2):
-            alive = jnp.transpose(all_slots[b])[:, 1:2].astype(low)
-            whole = pl.ds(b * block, block)
-            wide_left[1, whole, :] = wide_left[1, whole, :] * alive
-        wide_loads[1].wait()
-        out_rows = wide_left[1]
+        proj_low.wait_recv()
+        proj_core.start()
+        for load in wide_loads:
+            load.wait()
+        out_rows = wide_left[1, pl.ds(0, block), :]
 
         def act_tile(t, carry):
             at = pl.ds(pl.multiple_of(t * 512, 512), 512)
@@ -732,42 +766,66 @@
         rest = wide - rest_from
         rest_at = pl.ds(rest_from, rest)
         grad_act[:, rest_at] = product_nt(out_rows, down_weight[rest_at, :]).astype(low)
-        wide_loads[0].wait()
         pad_at = pl.ds(rest_from, CW // 2)
         wide_right[0, :, pad_at] = jnp.zeros((2 * block, CW // 2), low)
         wide_right[1, :, pad_at] = jnp.zeros((2 * block, CW // 2), low)
 
-        for j in range(2):
-            part_swaps[0][j].wait_recv()
+        def make_hidden(b):
+            here = pl.ds(b * block, block)
+            mixed_swaps[1 - b].wait_recv()
+            mixed = thin_second[1, here, :]
+            mixed_far = mixed_other[here, :]
+
+            def proj_tile(n, inner):
+                at = pl.ds(pl.multiple_of(n * 384, 384), 384)
+                own_part[:, at] = product(mixed, proj_weight[:, at]) + product(
+                    mixed_far, proj_other[:, at]
+                )
+                return inner
+
+            lax.fori_loop(0, width // 384, proj_tile, 0)
 
             def hidden_strip(at):
-                value = (
-                    all_tokens[at, :].astype(full)
-                    + own_part[at, :]
-                    + part_in[0, at, :].astype(full)
-                    + bias_proj
-                )
-                hidden[at, :] = value
+                there = pl.ds(at.start + b * block, strip)
+                value = all_tokens[there, :].astype(full) + own_part[at, :] + bias_proj
+                if b == 0:
+                    hidden[at, :] = value
                 xhat, _ = norm_stats(value)
-                wide_left[0, at, :] = (xhat * gain_two + shift_two).astype(low)
-
-            strips(half_block, j * half_block, hidden_strip)
-            normed_swaps[j].start()
-
-        left_pair(0).start()
-
-        def gelu_tile(here, at):
+                wide_left[0, there, :] = (xhat * gain_two + shift_two).astype(low)
+
+            strips(block, 0, hidden_strip)
+
+        def gelu_parts(here, at):
             value = product_nt(wide_left[0, here, :], up_weight[at, :]) + up_bias[0:1, at]
             square = value * value
             bent = jnp.tanh(GELU_SCALE * value * (1.0 + 0.044715 * square))
             bulge = 0.5 * (1.0 + bent)
             wide_right[1, here, at] = (value * bulge).astype(low)
-            slope = bulge + 0.5 * value * (1.0 - bent * bent) * (
+            return bulge + 0.5 * value * (1.0 - bent * bent) * (
                 GELU_SCALE * (1.0 + 0.134145 * square)
             )
-            grad = (slope * grad_act[here, at].astype(full)).astype(low)
+
+        def keep_grad(here, at, value):
+            grad = value.astype(low)
             wide_right[0, here, at] = grad
             up_sum[0, :, at] += jnp.sum(grad.astype(full), axis=0, keepdims=True)
+
+        def over_tiles(tile):
+            def step(t, inner):
+                tile(pl.ds(pl.multiple_of(t * CW, CW), CW))
+                return inner
+
+            lax.fori_loop(0, wide_chunks, step, 0, unroll=UNROLL)
+            tile(rest_at)
+
+        near = pl.ds(0, block)
+        far = pl.ds(block, block)
+
+        def far_tile(at):
+            wide_right[0, far, at] = gelu_parts(far, at).astype(low)
+
+        def near_tile(at):
+            keep_grad(near, at, gelu_parts(near, at) * grad_act[:, at].astype(full))
 
         def back_tiles(b):
             grad_rows = wide_right[0, pl.ds(b * block, block), pl.ds(0, wide)]
@@ -778,48 +836,45 @@
                 if b == 0:
                     own_part[:, at] = value
                 else:
-                    part_send[1, :, at] = value.astype(low)
+                    part_send[0, :, at] = value.astype(low)
                 return inner
 
             lax.fori_loop(0, width // 384, back_tile, 0)
 
-        def mlp_step(q, carry):
-            here = pl.ds(pl.multiple_of(q * half_block, half_block), half_block)
-            for j in range(2):
-
-                @pl.when(q == 2 + j)
-                def _():
-                    normed_swaps[j].wait_recv()
-                    if j == 1:
-                        left_pair(1).start()
-
-            def up_tile(t, inner):
-                gelu_tile(here, pl.ds(pl.multiple_of(t * CW, CW), CW))
-                return inner
-
-            lax.fori_loop(0, wide_chunks, up_tile, 0, unroll=UNROLL)
-            gelu_tile(here, rest_at)
+        proj_core.wait_recv()
+        make_hidden(1)
+        over_tiles(far_tile)
+        make_hidden(0)
+        left_pair(0).start()
+        over_tiles(near_tile)
+        for q in range(2):
             right_pair(q).start()
-
-            @pl.when(q == 1)
-            def _():
-                back_tiles(0)
-
-            return carry
-
-        lax.fori_loop(0, 4, mlp_step, 0)
+        back_tiles(0)
+        for j in range(2):
+            out_swaps[j].wait_recv()
+            mask_rows(1, j * half_block, half_block)
+            here = pl.ds(block + j * half_block, half_block)
+
+            def slope_tile(at):
+                grad = product_nt(wide_left[1, here, :], down_weight[at, :])
+                keep_grad(here, at, wide_right[0, here, at].astype(full) * grad)
+
+            if j == 1:
+                left_pair(1).start()
+            over_tiles(slope_tile)
+            right_pair(2 + j).start()
         for i in range(2):
             left_pair(i).wait_recv()
         for q in range(4):
             right_pair(q).wait_recv()
 
         def early_step(j, inner):
-            emit(early, j, j, wide_value(j), AHEAD)
+            emit(early, 2 * j, 2 * j, wide_value(j), AHEAD)
             return inner
 
-        lax.fori_loop(0, early_chunks, early_step, 0)
+        lax.fori_loop(0, early_chunks // 2, early_step, 0)
         back_tiles(1)
-        for copy in part_swaps[1]:
+        for copy in part_swaps[0]:
             copy.start()
         act_rows = wide_right[1, :, pl.ds(0, wide)]
 
@@ -827,7 +882,7 @@
             at = pl.ds(pl.multiple_of(n * 384, 384), 384)
             value = product(act_rows, down_weight[:, at])
             own_down[:, at] = value[:block]
-            part_send[2, :, at] = value[block:].astype(low)
+            part_send[1, :, at] = value[block:].astype(low)
             return inner
 
         lax.fori_loop(0, width // 384, down_tile, 0)
@@ -836,7 +891,7 @@
         mlp_scope,
         pltpu.VMEM(up_hbm.shape, low),
         pltpu.VMEM(down_hbm.shape, low),
-        pltpu.VMEM((2 * block, wide_right.shape[2]), low),
+        pltpu.VMEM((block, wide_right.shape[2]), low),
         pltpu.SemaphoreType.DMA((2,)),
     )
 
@@ -851,17 +906,17 @@
                 action(grads, j - early_chunks, j)
 
         def pump_step(i, carry):
-            @pl.when(i >= 6)
+            @pl.when(i >= core_lag)
             def _():
-                rest_copy(summed, i - 6).wait_recv()
-
-            @pl.when(jnp.logical_and(i >= 4, i < chunks + 4))
+                rest_copy(summed, i - core_lag).wait_recv()
+
+            @pl.when(jnp.logical_and(i >= high_lag, i < chunks + high_lag))
             def _():
-                held(i - 4, lambda ref, k, j: take_high(ref, k, j, summed))
-
-            @pl.when(jnp.logical_and(i >= 2, i < chunks + 2))
+                held(i - high_lag, lambda ref, k, j: take_high(ref, k, j, summed))
+
+            @pl.when(jnp.logical_and(i >= second_lag, i < chunks + second_lag))
             def _():
-                held(i - 2, take_second)
+                held(i - second_lag, take_second)
 
             @pl.when(i < chunks)
             def _():
@@ -869,7 +924,7 @@
 
             return carry
 
-        def pump(first, last, made=wide_chunks):
+        def pump(first, last, made=wide_subs):
             def step(i, carry):
                 pump_step(i, carry)
 
@@ -885,21 +940,23 @@
             emit(grads, j - early_chunks, j, value, ahead)
 
         def wide_step(j, carry):
-            emit_late(j, wide_value(j), AHEAD)
+            emit_late(2 * j, wide_value(j), AHEAD)
             return carry
 
-        lax.fori_loop(early_chunks, wide_chunks, wide_step, 0)
-        pump(0, 2)
+        lax.fori_loop(early_chunks // 2, wide_chunks, wide_step, 0)
+        pump(0, 3)
 
         for j in range(2):
-            part_swaps[1][j].wait_recv()
+            part_swaps[0][j].wait_recv()
 
             def norm_back_strip(at):
-                grad = own_part[at, :] + part_in[1, at, :].astype(full)
-                xhat, inverse = norm_stats(hidden[at, :])
+                grad = own_part[at, :] + part_in[0, at, :].astype(full)
+                kept = hidden[at, :]
+                xhat, inverse = norm_stats(kept)
+                own_down[at, :] += kept
                 out_rows = wide_left[1, at, :].astype(full)
                 value = out_rows + norm_grad(xhat, inverse, gain_two, grad)
-                grad_hidden[at, :] = value
+                hidden[at, :] = value
                 rounded = value.astype(low)
                 thin_left[1, at, :] = rounded
                 totals[2:3] += column_sums(rounded.astype(full))[None]
@@ -909,10 +966,10 @@
 
             strips(half_block, j * half_block, norm_back_strip)
             hidden_swaps[j].start()
-        for copy in part_swaps[2]:
+        for copy in part_swaps[1]:
             copy.start()
 
-        pump(2, 3)
+        pump(3, 5)
 
         def back_step(b, carry):
             here = pl.ds(pl.multiple_of(b * block, block), block)
@@ -972,16 +1029,16 @@
 
                 @pl.when(b == 1)
                 def _():
-                    part_send[3, :, at] = value.astype(low)
+                    part_send[2, :, at] = value.astype(low)
 
                 return inner
 
             lax.fori_loop(0, width // 384, normed_tile, 0)
-            pump(3 + 2 * b, 5 + 2 * b)
+            pump(5 + 4 * b, 9 + 4 * b)
             return carry
 
         lax.fori_loop(0, 2, back_step, 0)
-        for copy in part_swaps[3]:
+        for copy in part_swaps[2]:
             copy.start()
 
         for b in range(2):
@@ -1000,17 +1057,15 @@
 
         def thin_step(j, carry):
             columns = pl.ds(pl.multiple_of(j * CW, CW), CW)
-            emit_late(wide_chunks + 2 * j, first_part(columns), 7 + AHEAD)
-            emit_late(wide_chunks + 2 * j + 1, second_part(columns), 7 + AHEAD)
+            emit_late(2 * (wide_chunks + 2 * j), first_part(columns), 13 + AHEAD)
+            emit_late(2 * (wide_chunks + 2 * j + 1), second_part(columns), 13 + AHEAD)
             return carry
 
         lax.fori_loop(0, 2, thin_step, 0)
         thin_rest = pl.ds(2 * CW, thin - 2 * CW)
         wide_rest = pl.ds(wide_chunks * CW, CW // 2)
-        rest = wide - wide_chunks * CW
-        rest_columns = pl.ds(wide_chunks * CW, rest)
         emit_late(
-            chunks - 1,
+            chunks - 2,
             jnp.concatenate(
                 [
                     product_tn(wide_left[core], wide_right[core, :, wide_rest])
@@ -1020,18 +1075,18 @@
                 ],
                 axis=1,
             ),
-            7 + AHEAD,
-        )
-        pump(7, 10, chunks)
-
-        for copy in part_swaps[3]:
+            13 + AHEAD,
+        )
+        pump(13, 17, chunks)
+
+        for copy in part_swaps[2]:
             copy.wait_recv()
 
         def final_strip(at):
-            grad = own_part[at, :] + part_in[3, at, :].astype(full)
+            grad = own_part[at, :] + part_in[2, at, :].astype(full)
             xhat, inverse = norm_stats(all_tokens[at, :].astype(full))
             rows_out[1, at, :] = (
-                grad_hidden[at, :] + norm_grad(xhat, inverse, gain_one, grad)
+                hidden[at, :] + norm_grad(xhat, inverse, gain_one, grad)
             ).astype(low)
             totals[0:1] += column_sums(grad * xhat)[None]
             totals[1:2] += column_sums(grad)[None]
@@ -1043,9 +1098,9 @@
         halves[0] = jnp.where(shard == 0, lower, upper)
         halves[1] = jnp.where(shard == 0, upper, lower)
         halves_swap.start()
-        pump(10, 12, chunks)
         grad_query_bias = column_sums(thin_first[0].astype(full))[None]
         grad_value_bias = column_sums(thin_first[1].astype(full))[None]
+        pump(17, 19, chunks)
         halves_swap.wait_recv()
         vector_sum[0] = halves[0] + halves_in[...]
         vector_sum[0, 6:7] = grad_query_bias
@@ -1054,10 +1109,10 @@
         def vector_copies(i):
             return (
                 remote(
-                    vector_sum.at[i], vector_in.at[i], vec_send.at[2 * i], vec_recv.at[2 * i], peers[i]
+                    vector_sum.at[i], vector_in.at[i], vec_send.at[2 * i], vec_recv.at[2 * i], vector_peers[i]
                 ),
                 remote(
-                    up_sum.at[i], up_in.at[i], vec_send.at[2 * i + 1], vec_recv.at[2 * i + 1], peers[i]
+                    up_sum.at[i], up_in.at[i], vec_send.at[2 * i + 1], vec_recv.at[2 * i + 1], vector_peers[i]
                 ),
             )
 
@@ -1072,35 +1127,44 @@
             up_sum[i + 1] = up_sum[i] + up_in[i]
 
         vector_start(0)
-        for copy in part_swaps[2]:
+        for copy in part_swaps[1]:
             copy.wait_recv()
 
         def out_strip(at):
-            value = hidden[at, :] + own_down[at, :] + part_in[2, at, :].astype(full) + bias_down
+            value = own_down[at, :] + part_in[1, at, :].astype(full) + bias_down
             rows_out[0, at, :] = value.astype(low)
 
         strips(block, 0, out_strip)
         alive = jnp.transpose(all_slots[0])[:, 1:2].astype(low)
         rows_out[0] = rows_out[0] * alive
 
+        row_copy = pltpu.make_async_copy(rows_out, rows_hbm, out_sem.at[0])
+        row_copy.start()
         vector_finish(0)
         vector_start(1)
-        pump(12, chunks + 1, chunks)
+        pump(19, 22, chunks)
         vector_finish(1)
         vector_start(2)
-        pump(chunks + 1, chunks + 4, chunks)
+        pump(22, chunks - 1, chunks)
+        wide_copy = pltpu.make_async_copy(wide_out, wide_hbm, out_sem.at[1])
+        wide_copy.start()
         vector_finish(2)
         vector_start(3)
-        pump(chunks + 4, chunks + 6, chunks)
-        for slot in range(2):
-            source = jnp.where(core == slot, summed[chunks - 1, core], rest_in[...])
-            wide_out[slot, :, rest_columns] = source[:, :rest]
-            for place in range(2):
-                start = CW // 2 + place * (thin - 2 * CW)
-                thin_out[slot, place, :, thin_rest] = source[:, start : start + thin - 2 * CW]
+        pump(chunks - 1, chunks + second_lag, chunks)
         vector_finish(3)
-        vectors_out[...] = vector_sum[4]
-        up_bias_out[...] = up_sum[4]
+        last_copies = [
+            pltpu.make_async_copy(vector_sum.at[4], vectors_hbm, out_sem.at[2]),
+            pltpu.make_async_copy(up_sum.at[4], up_sum_hbm, out_sem.at[3]),
+            pltpu.make_async_copy(thin_out, thin_hbm, out_sem.at[4]),
+            pltpu.make_async_copy(rest_out, rest_hbm, out_sem.at[5]),
+        ]
+        for copy in last_copies[:2]:
+            copy.start()
+        pump(chunks + second_lag, chunks + core_lag, chunks)
+        for copy in last_copies[2:]:
+            copy.start()
+        for copy in [row_copy, wide_copy] + last_copies:
+            copy.wait()
 
         def drain(j, carry):
             held(j, lambda ref, k, i: first_copy(ref, k, i, False).wait_send())
@@ -1116,14 +1180,16 @@
 
     pl.run_scoped(
         grad_scope,
-        pltpu.VMEM((chunks - early_chunks, 2, 2, 2, rows, CW), low),
-        pltpu.VMEM((chunks, 2, rows // 2, CW), full),
-    )
-    for copy in [vectors_swap, slots_swap, *tokens_swaps, out_swap, halves_swap]:
+        pltpu.VMEM((chunks - early_chunks, 2, 2, 2, rows, SUB), low),
+        pltpu.VMEM((chunks, 2, rows // 2, SUB), full),
+    )
+    for copy in [vectors_swap, slots_swap, *tokens_swaps, *out_swaps, *mixed_swaps, proj_swap, halves_swap]:
         copy.wait_send()
-    for copies in part_swaps + [normed_swaps, hidden_swaps]:
+    for copies in part_swaps + [hidden_swaps]:
         for copy in copies:
             copy.wait_send()
+    for copy in (proj_y, proj_low, proj_core):
+        copy.wait_send()
     for q in range(4):
         right_pair(q).wait_send()
     for b in range(2):
@@ -1131,18 +1197,23 @@
             pair(b).wait_send()
 
 
-def publish_kernel(rows_in, wide_in, thin_in, vectors_in, up_in, *refs):
-    outs, (rows_at, wide_at, thin_at, vectors_at, up_at) = refs[:17], refs[17:22]
-    flats, in_sem, out_sem = refs[22:31], refs[31], refs[32]
+def publish_kernel(rows_in, wide_in, thin_in, rest_in, vectors_in, up_in, *refs):
+    outs, refs = refs[:17], refs[17:]
+    rows_at, wide_at, thin_at, rest_at, vectors_at, up_at = refs[:6]
+    flats, in_sem, out_sem = refs[6:15], refs[15], refs[16]
+    wide_main = wide_in.shape[2]
+    thin_main = thin_in.shape[3]
+    wide, thin = wide_at.shape[2], thin_at.shape[3]
     loads = [
         pltpu.make_async_copy(source, target, in_sem.at[i])
         for i, (source, target) in enumerate(
             (
                 (vectors_in, vectors_at),
                 (up_in, up_at),
-                (thin_in, thin_at),
-                (wide_in, wide_at),
+                (rest_in, rest_at),
                 (rows_in, rows_at),
+                (thin_in, thin_at.at[:, :, :, pl.ds(0, thin_main)]),
+                (wide_in, wide_at.at[:, :, pl.ds(0, wide_main)]),
             )
         )
     ]
@@ -1159,50 +1230,62 @@
     loads[1].wait()
     for i in range(8):
         flats[i][...] = vectors_at[i : i + 1, :].reshape(flats[i].shape)
-    wide = flats[8].shape[0]
     flats[8][...] = up_at[:, :wide].reshape(flats[8].shape)
     loads[2].wait()
-    for source, place in ((thin_at.at[0, 0], 4), (thin_at.at[0, 1], 6), (thin_at.at[1, 0], 7), (thin_at.at[1, 1], 9)):
-        store(source, place)
     loads[3].wait()
+    store(rows_at.at[0], 0)
+    store(rows_at.at[1], 1)
+    for slot in range(2):
+        wide_at[slot, :, wide_main:] = rest_at[slot, 0, :, : wide - wide_main]
+        for place in range(2):
+            start = place * (thin - thin_main)
+            thin_at[slot, place, :, thin_main:] = rest_at[
+                slot, 1, :, start : start + thin - thin_main
+            ]
+    loads[4].wait()
+    for i, place in enumerate((4, 6, 7, 9)):
+        store(thin_at.at[i // 2, i % 2], place)
+    loads[5].wait()
     store(wide_at.at[0], 13)
     store(wide_at.at[1], 15)
-    loads[4].wait()
-    store(rows_at.at[0], 0)
-    store(rows_at.at[1], 1)
     for flat, place in zip(flats, (2, 3, 10, 11, 12, 16, 5, 8, 14)):
         store(flat, place)
     for copy in stores:
         copy.wait()
 
 
-def publish_call(rows_out, wide_out, thin_out, vectors, up_bias_grad):
+def publish_call(packed, wide):
     full = jnp.float32
+    rows_out, wide_out, thin_out, rest_out, vectors, up_bias_grad = packed
     thin = vectors.shape[1]
-    _, half, wide = wide_out.shape
+    half = wide_out.shape[1]
     anywhere = pl.BlockSpec(memory_space=pl.ANY)
     vector = jax.ShapeDtypeStruct((thin,), full)
     matrix = jax.ShapeDtypeStruct((half, thin), full)
     tall = jax.ShapeDtypeStruct((half, wide), full)
     rows = jax.ShapeDtypeStruct(rows_out.shape[1:], rows_out.dtype)
-    inputs = (rows_out, wide_out, thin_out, vectors, up_bias_grad)
     return pl.pallas_call(
         publish_kernel,
         out_shape=(
             rows, rows, vector, vector, matrix, vector, matrix, matrix, vector, matrix, vector,
             vector, vector, tall, jax.ShapeDtypeStruct((wide,), full), tall, vector,
         ),
-        in_specs=[anywhere] * 5,
+        in_specs=[anywhere] * 6,
         out_specs=(anywhere,) * 17,
         scratch_shapes=[
-            *[pltpu.VMEM(value.shape, value.dtype) for value in inputs],
+            pltpu.VMEM(rows_out.shape, rows_out.dtype),
+            pltpu.VMEM((2, half, wide), full),
+            pltpu.VMEM((2, 2, half, thin), full),
+            pltpu.VMEM(rest_out.shape, full),
+            pltpu.VMEM(vectors.shape, full),
+            pltpu.VMEM(up_bias_grad.shape, full),
             *[pltpu.VMEM((thin,), full)] * 8,
             pltpu.VMEM((wide,), full),
-            pltpu.SemaphoreType.DMA((5,)),
+            pltpu.SemaphoreType.DMA((6,)),
             pltpu.SemaphoreType.DMA((17,)),
         ],
         name="publish",
-    )(*inputs)
+    )(*packed)
 
 
 def layer_call(tokens, out_grad, slots, vectors, up_bias, matrices):
@@ -1216,24 +1299,29 @@
     heads = thin // HDIM
     replicas = lax.axis_size("replica")
     rows = width // replicas * 2
-    chunks = wide // CW + 5
+    wide_main = wide // CW * CW
+    chunks = 2 * (wide // CW + 5)
     half = rows // 2
     both = 2 * block
-    vmem = pl.BlockSpec(memory_space=pltpu.VMEM)
     anywhere = pl.BlockSpec(memory_space=pl.ANY)
     dma = pltpu.SemaphoreType.DMA
     return pl.pallas_call(
         layer_kernel,
         out_shape=(
             jax.ShapeDtypeStruct((2,) + tokens.shape, low),
-            jax.ShapeDtypeStruct((2, half, wide), full),
-            jax.ShapeDtypeStruct((2, 2, half, thin), full),
+            jax.ShapeDtypeStruct((2, half, wide_main), full),
+            jax.ShapeDtypeStruct((2, 2, half, 2 * CW), full),
+            jax.ShapeDtypeStruct((2, 2, half, SUB), full),
             jax.ShapeDtypeStruct((8, thin), full),
             jax.ShapeDtypeStruct((1, wide_pad), full),
         ),
         in_specs=[anywhere] * 19,
-        out_specs=(vmem,) * 5,
+        out_specs=(anywhere,) * 6,
         scratch_shapes=[
+            pltpu.VMEM((2,) + tokens.shape, low),
+            pltpu.VMEM((2, half, wide_main), full),
+            pltpu.VMEM((2, 2, half, 2 * CW), full),
+            pltpu.VMEM((2, 2, half, SUB), full),
             pltpu.VMEM((8, block), full),
             pltpu.VMEM((8, thin), full),
             pltpu.VMEM((8, wide), full),
@@ -1241,6 +1329,8 @@
             pltpu.VMEM((thin, width), low),
             pltpu.VMEM((thin, width), low),
             pltpu.VMEM((thin, width), low),
+            pltpu.VMEM((thin, width), low),
+            pltpu.VMEM((both, thin), low),
             pltpu.VMEM((both, width), low),
             pltpu.VMEM((2, 8, block), full),
             pltpu.VMEM((8, thin), full),
@@ -1251,9 +1341,8 @@
             pltpu.VMEM((block, width), full),
             pltpu.VMEM((block, width), full),
             pltpu.VMEM((block, width), full),
-            pltpu.VMEM((block, width), full),
-            pltpu.VMEM((4, block, width), low),
-            pltpu.VMEM((4, block, width), low),
+            pltpu.VMEM((3, block, width), low),
+            pltpu.VMEM((3, block, width), low),
             pltpu.VMEM((2, both, width), low),
             pltpu.VMEM((2, both, wide_pad), low),
             pltpu.VMEM((2, both, width), low),
@@ -1265,11 +1354,10 @@
             pltpu.VMEM((both, width), low),
             pltpu.VMEM((both, thin), low),
             pltpu.VMEM((both, thin), low),
-            pltpu.VMEM((EARLY, 2, 2, 2, rows, CW), low),
-            pltpu.VMEM((chunks, 2, 2, rows, CW), low),
-            pltpu.VMEM((chunks, 2, rows, CW), low),
-            pltpu.VMEM((chunks, rows, CW), low),
-            pltpu.VMEM((half, CW), full),
+            pltpu.VMEM((EARLY, 2, 2, 2, rows, SUB), low),
+            pltpu.VMEM((chunks, 2, 2, rows, SUB), low),
+            pltpu.VMEM((chunks, 2, rows, SUB), low),
+            pltpu.VMEM((chunks, rows, SUB), low),
             pltpu.VMEM((8, width), full),
             pltpu.VMEM((2, 8, thin), full),
             pltpu.VMEM((8, thin), full),
@@ -1284,6 +1372,8 @@
             dma((6,)),
             dma((18,)),
             dma((18,)),
+            dma((3,)),
+            dma((3,)),
             dma((14,)),
             dma((14,)),
             dma((chunks,)),
@@ -1296,6 +1386,7 @@
             dma((chunks,)),
             dma((8,)),
             dma((8,)),
+            dma((6,)),
         ],
         compiler_params=pltpu.CompilerParams(
             collective_id=0, has_side_effects=True, vmem_limit_bytes=67043328
@@ -1324,7 +1415,7 @@
         up_bias,
         (query_weight.T, key_weight.T, value_weight.T, proj_weight, up_weight.T, down_weight),
     )
-    outs = list(publish_call(*packed))
+    outs = list(publish_call(packed, up_weight.shape[1]))
     outs[9] = outs[9].T
     outs[15] = outs[15].T
     return tuple(outs)

time: 161 us -> 153 us (0.950)
  Pallas kernels: 160 us -> 152 us
    pallas_call x1, Pallas kernels: 157 us -> 148 us  [layer_call(): pl.pallas_call(layer_kernel, out_shape=(jax.ShapeDtypeStruct((2,) + token...]
where the time goes in v5:
time: 153 us
  Pallas kernels  152 us (99%)
    pallas_call x1, Pallas kernels, layer_call(): pl.pallas_call(layer_kernel, out_shape=(jax.ShapeDtypeStruct((2,) + token...  148 us
    pallas_call x1, Pallas kernels, publish_call(): pl.pallas_call(publish_kernel, out_shape=(rows, rows, vector, vector, mat...  3.28 us

profile of v5, /device:TPU:0, one launch (start us, length us, event | category | flops | bytes accessed | tf_op | source)
XLA Modules:
  0.0 152.5 jit_solution(2696947530336800672)
XLA Ops:
  0.7 148.4 %layer.1 = (bf16[2,256,1152]{2,1,0:T(8,128)(2,1)}, f32[2,72,2048]{2,1,0:T(8,128)}, f32[2,2,72,512]{3,2,1,0:T(8,128)}, f32[2,2,72,128]{3,2,1,0:T(8,128)}, f32[8,576]{1,0:T(8,128)}, /*index=5*/f32[1,2176]{1,0:T(1,128)}) custom-call(bf16[256,1152]{1,0:T(8,128)(2,1)} %tokens_hbm.1, bf16[256,1152]{1,0:T(8,128)(2,1)} %out_hbm.1, s32[256]{0:T(256)} %picture_ids.1, ...), custom_call_target="tpu_custom_call" | custom-call | tf_op jit(solution)/shard_map/layer/pallas_call | solution.py:1308
  149.0 3.3 %publish.1 = (bf16[256,1152]{1,0:T(8,128)(2,1)}, bf16[256,1152]{1,0:T(8,128)(2,1)}, f32[576]{0:T(1024)}, f32[576]{0:T(1024)}, f32[72,576]{1,0:T(8,128)}, /*index...) custom-call(bf16[2,256,1152]{2,1,0:T(8,128)(2,1)} %get-tuple-element, ...), custom_call_target="tpu_custom_call" | custom-call | tf_op jit(solution)/shard_map/publish/pallas_call | solution.py:1267

commit v6 on v5

--- a/solution.py
+++ b/solution.py
@@ -12,8 +12,9 @@
 MESH = pl.DeviceIdType.MESH
 CW = 256
 SUB = 128
-EARLY = 4
+EARLY = 6
 AHEAD = 6
+FIRST = 2
 LAGS = (3, 6, 8)
 UNROLL = 2
 GELU_SCALE = 0.7978845608028654
@@ -292,7 +293,6 @@
     value_weight,
     proj_weight,
     proj_other,
-    mixed_other,
     all_tokens,
     all_slots,
     vectors_in,
@@ -312,6 +312,7 @@
     thin_second,
     wide_left_in,
     wide_right_in,
+    rest_right_in,
     thin_left_in,
     thin_other_in,
     thin_first_in,
@@ -473,8 +474,8 @@
         [
             swapped(
                 4 + 2 * i + j,
-                part_send.at[i, pl.ds(j * half_block, half_block)],
-                part_in.at[i, pl.ds(j * half_block, half_block)],
+                part_send.at[i % 2, pl.ds(j * half_block, half_block)],
+                part_in.at[i % 2, pl.ds(j * half_block, half_block)],
             )
             for j in range(2)
         ]
@@ -484,7 +485,7 @@
         swapped(
             10 + b,
             thin_second.at[1, pl.ds(b * block, block)],
-            mixed_other.at[pl.ds((1 - b) * block, block)],
+            thin_first_in.at[pl.ds((1 - b) * block, block)],
         )
         for b in range(2)
     ]
@@ -514,24 +515,43 @@
         here = pl.ds(b * block, block)
         return paired_copy(index + b, source.at[here], target.at[here])
 
+    half_wide = wide_right_in.shape[2]
+    pieces = ((0, block), (block, half_block), (block + half_block, half_block))
+
+    def out_pair(p):
+        here = pl.ds(*pieces[p])
+        return paired_copy(p, wide_left.at[1, here], wide_left_in.at[1, here])
+
     def left_pair(b):
-        return pair_rows(0, wide_left.at[other], wide_left_in, b)
-
-    def right_pair(q):
-        here = pl.ds(q * half_block, half_block)
-        return paired_copy(2 + q, wide_right.at[other, here], wide_right_in.at[here])
+        return pair_rows(3, wide_left.at[0], wide_left_in.at[0], b)
+
+    def theirs(kind, here):
+        columns = pl.ds(pl.multiple_of(other * half_wide, CW), half_wide)
+        return wide_right.at[kind, here, columns]
+
+    def act_pair(b):
+        here = pl.ds(b * block, block)
+        return paired_copy(5 + b, theirs(1, here), wide_right_in.at[1, here])
+
+    def grad_pair(p):
+        here = pl.ds(*pieces[p])
+        return paired_copy(7 + p, theirs(0, here), wide_right_in.at[0, here])
+
+    def rest_pair():
+        source = wide_right.at[other, :, pl.ds(2 * half_wide, SUB)]
+        return paired_copy(10, source, rest_right_in)
 
     def normed_pair(b):
-        return pair_rows(6, thin_left.at[0], thin_left_in, b)
+        return pair_rows(11, thin_left.at[0], thin_left_in, b)
 
     def other_pair(b):
-        return pair_rows(8, thin_left.at[other], thin_other_in, b)
+        return pair_rows(13, thin_left.at[other], thin_other_in, b)
 
     def first_pair(b):
-        return pair_rows(10, thin_first.at[other], thin_first_in, b)
+        return pair_rows(15, thin_first.at[other], thin_first_in, b)
 
     def second_pair(b):
-        return pair_rows(12, thin_second.at[other], thin_second_in, b)
+        return pair_rows(17, thin_second.at[other], thin_second_in, b)
 
     vectors_swap.start()
     slots_swap.start()
@@ -642,7 +662,10 @@
         high_copy(grads, k, j).start()
 
     def wide_place(slot, j):
-        return wide_out.at[slot, :, pl.ds(pl.multiple_of(j * SUB, SUB), SUB)]
+        tile = j // 2
+        start = slot * half_wide + lax.rem(tile, wide_chunks // 2) * CW + lax.rem(j, 2) * SUB
+        kind = jnp.where(tile < wide_chunks // 2, 1, 0)
+        return wide_out.at[kind, :, pl.ds(pl.multiple_of(start, SUB), SUB)]
 
     def thin_place(slot, j):
         tile = j // 2 - wide_chunks
@@ -677,13 +700,17 @@
                 core_copy(summed, j, place).start()
                 place(core, j)[...] = summed[j, core]
 
-    def wide_value(j):
-        columns = pl.ds(pl.multiple_of(j * CW, CW), CW)
-        return product_tn(wide_left[core], wide_right[core, :, columns]) + product_tn(
-            wide_left_in[...], wide_right_in[:, columns]
-        )
-
-    def mlp_scope(up_weight, down_weight, grad_act, wide_sem):
+    def wide_value(tile, before=None):
+        kind = jnp.where(tile < wide_chunks // 2, 1, 0)
+        start = lax.rem(tile, wide_chunks // 2) * CW
+        mine = pl.ds(pl.multiple_of(core * half_wide + start, CW), CW)
+        value = product_tn(wide_left[kind], wide_right[kind, :, mine])
+        if before is not None:
+            before()
+        columns = pl.ds(pl.multiple_of(start, CW), CW)
+        return value + product_tn(wide_left_in[kind], wide_right_in[kind, :, columns])
+
+    def mlp_scope(up_weight, down_weight, wide_sem):
         wide_loads = [
             pltpu.make_async_copy(up_hbm, up_weight, wide_sem.at[0]),
             pltpu.make_async_copy(down_hbm, down_weight, wide_sem.at[1]),
@@ -754,27 +781,29 @@
         proj_core.start()
         for load in wide_loads:
             load.wait()
-        out_rows = wide_left[1, pl.ds(0, block), :]
+        out_pair(0).start()
+        near = pl.ds(0, block)
+        out_rows = wide_left[1, near, :]
 
         def act_tile(t, carry):
             at = pl.ds(pl.multiple_of(t * 512, 512), 512)
-            grad_act[:, at] = product_nt(out_rows, down_weight[at, :]).astype(low)
+            wide_right[0, near, at] = product_nt(out_rows, down_weight[at, :]).astype(low)
             return carry
 
         lax.fori_loop(0, wide_chunks // 2, act_tile, 0)
         rest_from = wide_chunks * CW
         rest = wide - rest_from
         rest_at = pl.ds(rest_from, rest)
-        grad_act[:, rest_at] = product_nt(out_rows, down_weight[rest_at, :]).astype(low)
         pad_at = pl.ds(rest_from, CW // 2)
         wide_right[0, :, pad_at] = jnp.zeros((2 * block, CW // 2), low)
         wide_right[1, :, pad_at] = jnp.zeros((2 * block, CW // 2), low)
+        wide_right[0, near, rest_at] = product_nt(out_rows, down_weight[rest_at, :]).astype(low)
 
         def make_hidden(b):
             here = pl.ds(b * block, block)
             mixed_swaps[1 - b].wait_recv()
             mixed = thin_second[1, here, :]
-            mixed_far = mixed_other[here, :]
+            mixed_far = thin_first_in[here, :]
 
             def proj_tile(n, inner):
                 at = pl.ds(pl.multiple_of(n * 384, 384), 384)
@@ -818,14 +847,13 @@
             lax.fori_loop(0, wide_chunks, step, 0, unroll=UNROLL)
             tile(rest_at)
 
-        near = pl.ds(0, block)
         far = pl.ds(block, block)
 
         def far_tile(at):
             wide_right[0, far, at] = gelu_parts(far, at).astype(low)
 
         def near_tile(at):
-            keep_grad(near, at, gelu_parts(near, at) * grad_act[:, at].astype(full))
+            keep_grad(near, at, gelu_parts(near, at) * wide_right[0, near, at].astype(full))
 
         def back_tiles(b):
             grad_rows = wide_right[0, pl.ds(b * block, block), pl.ds(0, wide)]
@@ -844,38 +872,54 @@
         proj_core.wait_recv()
         make_hidden(1)
         over_tiles(far_tile)
+        left_pair(1).start()
+        act_pair(1).start()
         make_hidden(0)
         left_pair(0).start()
         over_tiles(near_tile)
-        for q in range(2):
-            right_pair(q).start()
-        back_tiles(0)
-        for j in range(2):
-            out_swaps[j].wait_recv()
-            mask_rows(1, j * half_block, half_block)
+        act_pair(0).start()
+        grad_pair(0).start()
+
+        def slope_rows(j):
             here = pl.ds(block + j * half_block, half_block)
 
             def slope_tile(at):
                 grad = product_nt(wide_left[1, here, :], down_weight[at, :])
                 keep_grad(here, at, wide_right[0, here, at].astype(full) * grad)
 
-            if j == 1:
-                left_pair(1).start()
             over_tiles(slope_tile)
-            right_pair(2 + j).start()
-        for i in range(2):
-            left_pair(i).wait_recv()
-        for q in range(4):
-            right_pair(q).wait_recv()
+            grad_pair(1 + j).start()
+
+        def out_arrived(j):
+            out_swaps[j].wait_recv()
+            mask_rows(1, j * half_block, half_block)
+            out_pair(1 + j).start()
+
+        out_arrived(0)
+        slope_rows(0)
+        back_tiles(0)
+        out_arrived(1)
+
+        def pair_arrived():
+            for p in range(3):
+                out_pair(p).wait_recv()
+            for i in range(2):
+                act_pair(i).wait_recv()
+
+        emit(early, 0, 0, wide_value(0, pair_arrived), AHEAD)
 
         def early_step(j, inner):
             emit(early, 2 * j, 2 * j, wide_value(j), AHEAD)
             return inner
 
-        lax.fori_loop(0, early_chunks // 2, early_step, 0)
+        lax.fori_loop(1, early_chunks // 2, early_step, 0)
+        slope_rows(1)
+        rest_pair().start()
         back_tiles(1)
         for copy in part_swaps[0]:
             copy.start()
+        for i in range(FIRST):
+            take_first(early, i, i)
         act_rows = wide_right[1, :, pl.ds(0, wide)]
 
         def down_tile(n, inner):
@@ -891,7 +935,6 @@
         mlp_scope,
         pltpu.VMEM(up_hbm.shape, low),
         pltpu.VMEM(down_hbm.shape, low),
-        pltpu.VMEM((block, wide_right.shape[2]), low),
         pltpu.SemaphoreType.DMA((2,)),
     )
 
@@ -939,12 +982,17 @@
         def emit_late(j, value, ahead):
             emit(grads, j - early_chunks, j, value, ahead)
 
+        for i in range(2):
+            left_pair(i).wait_recv()
+        for p in range(3):
+            grad_pair(p).wait_recv()
+
         def wide_step(j, carry):
-            emit_late(2 * j, wide_value(j), AHEAD)
+            emit_late(2 * j, wide_value(j), FIRST + AHEAD)
             return carry
 
         lax.fori_loop(early_chunks // 2, wide_chunks, wide_step, 0)
-        pump(0, 3)
+        pump(FIRST, 4)
 
         for j in range(2):
             part_swaps[0][j].wait_recv()
@@ -966,16 +1014,20 @@
 
             strips(half_block, j * half_block, norm_back_strip)
             hidden_swaps[j].start()
+            if j == 0:
+                pump(4, 5)
         for copy in part_swaps[1]:
             copy.start()
 
-        pump(3, 5)
+        pump(5, 7)
 
         def back_step(b, carry):
             here = pl.ds(pl.multiple_of(b * block, block), block)
 
             @pl.when(b == 1)
             def _():
+                for copy in part_swaps[0]:
+                    copy.wait_send()
                 for copy in hidden_swaps:
                     copy.wait_recv()
                 for i in range(2):
@@ -1029,12 +1081,12 @@
 
                 @pl.when(b == 1)
                 def _():
-                    part_send[2, :, at] = value.astype(low)
+                    part_send[0, :, at] = value.astype(low)
 
                 return inner
 
             lax.fori_loop(0, width // 384, normed_tile, 0)
-            pump(5 + 4 * b, 9 + 4 * b)
+            pump(7 + 4 * b, 11 + 3 * b)
             return carry
 
         lax.fori_loop(0, 2, back_step, 0)
@@ -1044,6 +1096,7 @@
         for b in range(2):
             for pair in (normed_pair, other_pair, first_pair, second_pair):
                 pair(b).wait_recv()
+        rest_pair().wait_recv()
 
         def first_part(columns):
             return product_tn(thin_left[0], thin_first[core, :, columns]) + product_tn(
@@ -1057,8 +1110,10 @@
 
         def thin_step(j, carry):
             columns = pl.ds(pl.multiple_of(j * CW, CW), CW)
-            emit_late(2 * (wide_chunks + 2 * j), first_part(columns), 13 + AHEAD)
-            emit_late(2 * (wide_chunks + 2 * j + 1), second_part(columns), 13 + AHEAD)
+            ahead = 14 + j + AHEAD
+            emit_late(2 * (wide_chunks + 2 * j), first_part(columns), ahead)
+            emit_late(2 * (wide_chunks + 2 * j + 1), second_part(columns), ahead)
+            pump(14 + j, 15 + 2 * j, 2 * (wide_chunks + 2 * j + 2))
             return carry
 
         lax.fori_loop(0, 2, thin_step, 0)
@@ -1069,21 +1124,21 @@
             jnp.concatenate(
                 [
                     product_tn(wide_left[core], wide_right[core, :, wide_rest])
-                    + product_tn(wide_left_in[...], wide_right_in[:, wide_rest]),
+                    + product_tn(wide_left_in[core], rest_right_in[...]),
                     first_part(thin_rest),
                     second_part(thin_rest),
                 ],
                 axis=1,
             ),
-            13 + AHEAD,
+            17 + AHEAD,
         )
-        pump(13, 17, chunks)
+        pump(17, 19, chunks)
 
         for copy in part_swaps[2]:
             copy.wait_recv()
 
         def final_strip(at):
-            grad = own_part[at, :] + part_in[2, at, :].astype(full)
+            grad = own_part[at, :] + part_in[0, at, :].astype(full)
             xhat, inverse = norm_stats(all_tokens[at, :].astype(full))
             rows_out[1, at, :] = (
                 hidden[at, :] + norm_grad(xhat, inverse, gain_one, grad)
@@ -1100,7 +1155,7 @@
         halves_swap.start()
         grad_query_bias = column_sums(thin_first[0].astype(full))[None]
         grad_value_bias = column_sums(thin_first[1].astype(full))[None]
-        pump(17, 19, chunks)
+        pump(19, 21, chunks)
         halves_swap.wait_recv()
         vector_sum[0] = halves[0] + halves_in[...]
         vector_sum[0, 6:7] = grad_query_bias
@@ -1138,34 +1193,6 @@
         alive = jnp.transpose(all_slots[0])[:, 1:2].astype(low)
         rows_out[0] = rows_out[0] * alive
 
-        row_copy = pltpu.make_async_copy(rows_out, rows_hbm, out_sem.at[0])
-        row_copy.start()
-        vector_finish(0)
-        vector_start(1)
-        pump(19, 22, chunks)
-        vector_finish(1)
-        vector_start(2)
-        pump(22, chunks - 1, chunks)
-        wide_copy = pltpu.make_async_copy(wide_out, wide_hbm, out_sem.at[1])
-        wide_copy.start()
-        vector_finish(2)
-        vector_start(3)
-        pump(chunks - 1, chunks + second_lag, chunks)
-        vector_finish(3)
-        last_copies = [
-            pltpu.make_async_copy(vector_sum.at[4], vectors_hbm, out_sem.at[2]),
-            pltpu.make_async_copy(up_sum.at[4], up_sum_hbm, out_sem.at[3]),
-            pltpu.make_async_copy(thin_out, thin_hbm, out_sem.at[4]),
-            pltpu.make_async_copy(rest_out, rest_hbm, out_sem.at[5]),
-        ]
-        for copy in last_copies[:2]:
-            copy.start()
-        pump(chunks + second_lag, chunks + core_lag, chunks)
-        for copy in last_copies[2:]:
-            copy.start()
-        for copy in [row_copy, wide_copy] + last_copies:
-            copy.wait()
-
         def drain(j, carry):
             held(j, lambda ref, k, i: first_copy(ref, k, i, False).wait_send())
             held(j, lambda ref, k, i: second_copy(ref, k, i, False).wait_send())
@@ -1173,7 +1200,42 @@
             rest_copy(summed, j).wait_send()
             return carry
 
-        lax.fori_loop(0, chunks, drain, 0)
+        out_copies = [
+            pltpu.make_async_copy(source, target, out_sem.at[i])
+            for i, (source, target) in enumerate(
+                (
+                    (rows_out, rows_hbm),
+                    (wide_out, wide_hbm),
+                    (vector_sum.at[4], vectors_hbm),
+                    (up_sum.at[4], up_sum_hbm),
+                    (thin_out, thin_hbm),
+                    (rest_out, rest_hbm),
+                )
+            )
+        ]
+        out_copies[0].start()
+        pump(21, 22, chunks)
+        vector_finish(0)
+        vector_start(1)
+        pump(22, 24, chunks)
+        out_copies[1].start()
+        vector_finish(1)
+        vector_start(2)
+        pump(24, 25, chunks)
+        vector_finish(2)
+        vector_start(3)
+        pump(25, 29, chunks)
+        vector_finish(3)
+        out_copies[2].start()
+        out_copies[3].start()
+        lax.fori_loop(0, chunks - core_lag, drain, 0)
+        pump(29, 32, chunks)
+        out_copies[4].start()
+        pump(32, chunks + core_lag, chunks)
+        out_copies[5].start()
+        lax.fori_loop(chunks - core_lag, chunks, drain, 0)
+        for copy in out_copies:
+            copy.wait()
         for i in range(4):
             for copy in vector_copies(i):
                 copy.wait_send()
@@ -1185,15 +1247,17 @@
     )
     for copy in [vectors_swap, slots_swap, *tokens_swaps, *out_swaps, *mixed_swaps, proj_swap, halves_swap]:
         copy.wait_send()
-    for copies in part_swaps + [hidden_swaps]:
+    for copies in part_swaps[1:] + [hidden_swaps]:
         for copy in copies:
             copy.wait_send()
     for copy in (proj_y, proj_low, proj_core):
         copy.wait_send()
-    for q in range(4):
-        right_pair(q).wait_send()
+    for p in range(3):
+        out_pair(p).wait_send()
+        grad_pair(p).wait_send()
+    rest_pair().wait_send()
     for b in range(2):
-        for pair in (left_pair, normed_pair, other_pair, first_pair, second_pair):
+        for pair in (left_pair, act_pair, normed_pair, other_pair, first_pair, second_pair):
             pair(b).wait_send()
 
 
@@ -1330,7 +1394,6 @@
             pltpu.VMEM((thin, width), low),
             pltpu.VMEM((thin, width), low),
             pltpu.VMEM((thin, width), low),
-            pltpu.VMEM((both, thin), low),
             pltpu.VMEM((both, width), low),
             pltpu.VMEM((2, 8, block), full),
             pltpu.VMEM((8, thin), full),
@@ -1341,15 +1404,16 @@
             pltpu.VMEM((block, width), full),
             pltpu.VMEM((block, width), full),
             pltpu.VMEM((block, width), full),
-            pltpu.VMEM((3, block, width), low),
-            pltpu.VMEM((3, block, width), low),
+            pltpu.VMEM((2, block, width), low),
+            pltpu.VMEM((2, block, width), low),
             pltpu.VMEM((2, both, width), low),
             pltpu.VMEM((2, both, wide_pad), low),
             pltpu.VMEM((2, both, width), low),
             pltpu.VMEM((2, both, thin), low),
             pltpu.VMEM((2, both, thin), low),
-            pltpu.VMEM((both, width), low),
-            pltpu.VMEM((both, wide_pad), low),
+            pltpu.VMEM((2, both, width), low),
+            pltpu.VMEM((2, both, wide_main // 2), low),
+            pltpu.VMEM((both, SUB), low),
             pltpu.VMEM((both, width), low),
             pltpu.VMEM((both, width), low),
             pltpu.VMEM((both, thin), low),
@@ -1374,8 +1438,8 @@
             dma((18,)),
             dma((3,)),
             dma((3,)),
-            dma((14,)),
-            dma((14,)),
+            dma((19,)),
+            dma((19,)),
             dma((chunks,)),
             dma((chunks,)),
             dma((chunks,)),

time: 153 us -> 150 us (0.980)
  Pallas kernels: 152 us -> 149 us
    pallas_call x1, Pallas kernels: 148 us -> 145 us  [layer_call(): pl.pallas_call(layer_kernel, out_shape=(jax.ShapeDtypeStruct((2,) + token...]
where the time goes in v6:
time: 150 us; the launch traced here: 149 us
  Pallas kernels  149 us (99%)
    pallas_call x1, Pallas kernels, layer_call(): pl.pallas_call(layer_kernel, out_shape=(jax.ShapeDtypeStruct((2,) + token...  145 us
    pallas_call x1, Pallas kernels, publish_call(): pl.pallas_call(publish_kernel, out_shape=(rows, rows, vector, vector, mat...  3.28 us

profile of v6, /device:TPU:0, one launch (start us, length us, event | category | flops | bytes accessed | tf_op | source)
XLA Modules:
  0.0 149.4 jit_solution(10911997247594864414)
XLA Ops:
  0.7 145.3 %layer.1 = (bf16[2,256,1152]{2,1,0:T(8,128)(2,1)}, f32[2,72,2048]{2,1,0:T(8,128)}, f32[2,2,72,512]{3,2,1,0:T(8,128)}, f32[2,2,72,128]{3,2,1,0:T(8,128)}, f32[8,576]{1,0:T(8,128)}, /*index=5*/f32[1,2176]{1,0:T(1,128)}) custom-call(bf16[256,1152]{1,0:T(8,128)(2,1)} %tokens_hbm.1, bf16[256,1152]{1,0:T(8,128)(2,1)} %out_hbm.1, s32[256]{0:T(256)} %picture_ids.1, ...), custom_call_target="tpu_custom_call" | custom-call | tf_op jit(solution)/shard_map/layer/pallas_call | solution.py:1372
  145.9 3.3 %publish.1 = (bf16[256,1152]{1,0:T(8,128)(2,1)}, bf16[256,1152]{1,0:T(8,128)(2,1)}, f32[576]{0:T(1024)}, f32[576]{0:T(1024)}, f32[72,576]{1,0:T(8,128)}, /*index...) custom-call(bf16[2,256,1152]{2,1,0:T(8,128)(2,1)} %get-tuple-element, ...), custom_call_target="tpu_custom_call" | custom-call | tf_op jit(solution)/shard_map/publish/pallas_call | solution.py:1331

commit v7 on v6

--- a/solution.py
+++ b/solution.py
@@ -281,7 +281,6 @@
     rest_hbm,
     vectors_hbm,
     up_sum_hbm,
-    rows_out,
     wide_out,
     thin_out,
     rest_out,
@@ -492,15 +491,35 @@
     quarter = thin // 4
     most = width // 9 * 5
     rest_width = width - most
-    own_rows = pl.ds((2 * low_bit + y_bit) * quarter, quarter)
+    some = quarter // 9 * 5
+    own_quarter = (2 * low_bit + y_bit) * quarter
     own_columns = pl.ds(pl.multiple_of(core * rest_width, 128), most)
-    proj_piece = proj_other.at[own_rows, own_columns]
-    proj_swap = swapped(12, proj_hbm.at[own_rows, own_columns], proj_piece)
-    proj_y = remote(proj_piece, proj_piece, proj_send.at[0], proj_recv.at[0], y_peer)
-    proj_low_piece = proj_other.at[pl.ds(low_bit * 2 * quarter, 2 * quarter), own_columns]
-    proj_low = remote(proj_low_piece, proj_low_piece, proj_send.at[1], proj_recv.at[1], low_peer)
-    proj_core_piece = proj_other.at[:, pl.ds(pl.multiple_of(core * most, 128), rest_width)]
-    proj_core = remote(proj_core_piece, proj_core_piece, proj_send.at[2], proj_recv.at[2], partner)
+
+    def proj_rows(start, count):
+        return pl.ds(pl.multiple_of(start, 16), count)
+
+    own_rows = proj_rows(own_quarter + high_bit * (quarter - some), some)
+    proj_swap = swapped(
+        12, proj_hbm.at[own_rows, own_columns], proj_other.at[own_rows, own_columns]
+    )
+
+    def proj_copy(index, rows_at, columns, peer):
+        piece = proj_other.at[rows_at, columns]
+        return remote(piece, piece, proj_send.at[index], proj_recv.at[index], peer)
+
+    proj_high = proj_copy(
+        3, proj_rows(own_quarter + high_bit * some, quarter - some), own_columns, high_peer
+    )
+    proj_y = proj_copy(0, proj_rows(own_quarter, quarter), own_columns, y_peer)
+    proj_low = [
+        proj_copy(1, proj_rows(own_quarter, quarter), own_columns, low_peer),
+        proj_copy(
+            4, proj_rows((2 * low_bit + 1 - y_bit) * quarter, quarter), own_columns, low_peer
+        ),
+    ]
+    proj_core = proj_copy(
+        2, pl.ds(0, thin), pl.ds(pl.multiple_of(core * most, 128), rest_width), partner
+    )
     hidden_swaps = [
         swapped(
             14 + j,
@@ -700,13 +719,22 @@
                 core_copy(summed, j, place).start()
                 place(core, j)[...] = summed[j, core]
 
-    def wide_value(tile, before=None):
+    def first_value(arrived, last_arrived):
+        mine = pl.ds(pl.multiple_of(core * half_wide, CW), CW)
+        known = pl.ds(0, block + half_block)
+        final = pl.ds(block + half_block, half_block)
+        columns = pl.ds(0, CW)
+        value = product_tn(wide_left[1], wide_right[1, :, mine])
+        arrived()
+        value += product_tn(wide_left_in[1, known, :], wide_right_in[1, known, columns])
+        last_arrived()
+        return value + product_tn(wide_left_in[1, final, :], wide_right_in[1, final, columns])
+
+    def wide_value(tile):
         kind = jnp.where(tile < wide_chunks // 2, 1, 0)
         start = lax.rem(tile, wide_chunks // 2) * CW
         mine = pl.ds(pl.multiple_of(core * half_wide + start, CW), CW)
         value = product_tn(wide_left[kind], wide_right[kind, :, mine])
-        if before is not None:
-            before()
         columns = pl.ds(pl.multiple_of(start, CW), CW)
         return value + product_tn(wide_left_in[kind], wide_right_in[kind, :, columns])
 
@@ -724,12 +752,15 @@
             @pl.when(b == 0)
             def _():
                 proj_swap.wait_recv()
-                proj_y.start()
+                proj_high.start()
 
             @pl.when(b == 1)
             def _():
+                proj_high.wait_recv()
+                proj_y.start()
+                proj_low[0].start()
                 proj_y.wait_recv()
-                proj_low.start()
+                proj_low[1].start()
                 for copy in tokens_swaps:
                     copy.wait_recv()
 
@@ -777,7 +808,8 @@
             copy.start()
         for b in range(2):
             normed_pair(b).start()
-        proj_low.wait_recv()
+        for copy in proj_low:
+            copy.wait_recv()
         proj_core.start()
         for load in wide_loads:
             load.wait()
@@ -901,12 +933,12 @@
         out_arrived(1)
 
         def pair_arrived():
-            for p in range(3):
+            for p in range(2):
                 out_pair(p).wait_recv()
             for i in range(2):
                 act_pair(i).wait_recv()
 
-        emit(early, 0, 0, wide_value(0, pair_arrived), AHEAD)
+        emit(early, 0, 0, first_value(pair_arrived, lambda: out_pair(2).wait_recv()), AHEAD)
 
         def early_step(j, inner):
             emit(early, 2 * j, 2 * j, wide_value(j), AHEAD)
@@ -1136,11 +1168,13 @@
 
         for copy in part_swaps[2]:
             copy.wait_recv()
+        for copy in part_swaps[1]:
+            copy.wait_send()
 
         def final_strip(at):
             grad = own_part[at, :] + part_in[0, at, :].astype(full)
             xhat, inverse = norm_stats(all_tokens[at, :].astype(full))
-            rows_out[1, at, :] = (
+            part_send[1, at, :] = (
                 hidden[at, :] + norm_grad(xhat, inverse, gain_one, grad)
             ).astype(low)
             totals[0:1] += column_sums(grad * xhat)[None]
@@ -1184,14 +1218,16 @@
         vector_start(0)
         for copy in part_swaps[1]:
             copy.wait_recv()
+        for copy in part_swaps[2]:
+            copy.wait_send()
 
         def out_strip(at):
             value = own_down[at, :] + part_in[1, at, :].astype(full) + bias_down
-            rows_out[0, at, :] = value.astype(low)
+            part_send[0, at, :] = value.astype(low)
 
         strips(block, 0, out_strip)
         alive = jnp.transpose(all_slots[0])[:, 1:2].astype(low)
-        rows_out[0] = rows_out[0] * alive
+        part_send[0] = part_send[0] * alive
 
         def drain(j, carry):
             held(j, lambda ref, k, i: first_copy(ref, k, i, False).wait_send())
@@ -1204,7 +1240,7 @@
             pltpu.make_async_copy(source, target, out_sem.at[i])
             for i, (source, target) in enumerate(
                 (
-                    (rows_out, rows_hbm),
+                    (part_send, rows_hbm),
                     (wide_out, wide_hbm),
                     (vector_sum.at[4], vectors_hbm),
                     (up_sum.at[4], up_sum_hbm),
@@ -1247,10 +1283,9 @@
     )
     for copy in [vectors_swap, slots_swap, *tokens_swaps, *out_swaps, *mixed_swaps, proj_swap, halves_swap]:
         copy.wait_send()
-    for copies in part_swaps[1:] + [hidden_swaps]:
-        for copy in copies:
-            copy.wait_send()
-    for copy in (proj_y, proj_low, proj_core):
+    for copy in hidden_swaps:
+        copy.wait_send()
+    for copy in (proj_high, proj_y, *proj_low, proj_core):
         copy.wait_send()
     for p in range(3):
         out_pair(p).wait_send()
@@ -1382,7 +1417,6 @@
         in_specs=[anywhere] * 19,
         out_specs=(anywhere,) * 6,
         scratch_shapes=[
-            pltpu.VMEM((2,) + tokens.shape, low),
             pltpu.VMEM((2, half, wide_main), full),
             pltpu.VMEM((2, 2, half, 2 * CW), full),
             pltpu.VMEM((2, 2, half, SUB), full),
@@ -1436,8 +1470,8 @@
             dma((6,)),
             dma((18,)),
             dma((18,)),
-            dma((3,)),
-            dma((3,)),
+            dma((5,)),
+            dma((5,)),
             dma((19,)),
             dma((19,)),
             dma((chunks,)),

time: 150 us -> 148 us (0.987)
  Pallas kernels: 149 us -> 146 us
    pallas_call x1, Pallas kernels: 145 us -> 143 us  [layer_call(): pl.pallas_call(layer_kernel, out_shape=(jax.ShapeDtypeStruct((2,) + token...]
where the time goes in v7:
time: 148 us; the launch traced here: 147 us
  Pallas kernels  146 us (99%)
    pallas_call x1, Pallas kernels, layer_call(): pl.pallas_call(layer_kernel, out_shape=(jax.ShapeDtypeStruct((2,) + token...  143 us
    pallas_call x1, Pallas kernels, publish_call(): pl.pallas_call(publish_kernel, out_shape=(rows, rows, vector, vector, mat...  3.28 us

profile of v7, /device:TPU:0, one launch (start us, length us, event | category | flops | bytes accessed | tf_op | source)
XLA Modules:
  0.0 147.3 jit_solution(1302219090071841552)
XLA Ops:
  0.7 143.1 %layer.1 = (bf16[2,256,1152]{2,1,0:T(8,128)(2,1)}, f32[2,72,2048]{2,1,0:T(8,128)}, f32[2,2,72,512]{3,2,1,0:T(8,128)}, f32[2,2,72,128]{3,2,1,0:T(8,128)}, f32[8,576]{1,0:T(8,128)}, /*index=5*/f32[1,2176]{1,0:T(1,128)}) custom-call(bf16[256,1152]{1,0:T(8,128)(2,1)} %tokens_hbm.1, bf16[256,1152]{1,0:T(8,128)(2,1)} %out_hbm.1, s32[256]{0:T(256)} %picture_ids.1, ...), custom_call_target="tpu_custom_call" | custom-call | tf_op jit(solution)/shard_map/layer/pallas_call | solution.py:1407
  143.8 3.3 %publish.1 = (bf16[256,1152]{1,0:T(8,128)(2,1)}, bf16[256,1152]{1,0:T(8,128)(2,1)}, f32[576]{0:T(1024)}, f32[576]{0:T(1024)}, f32[72,576]{1,0:T(8,128)}, /*index...) custom-call(bf16[2,256,1152]{2,1,0:T(8,128)(2,1)} %get-tuple-element, ...), custom_call_target="tpu_custom_call" | custom-call | tf_op jit(solution)/shard_map/publish/pallas_call | solution.py:1366
